TPU v7x, 32 devices: a whole 2x2x4 slice. The times are simulated.
32 devices in a mesh: parts: 2 (over x), snp: 16 (over z, y, core).
Axes of the slice: x: 2, y: 2, z: 4, core: 2. Of those that a mesh axis runs over, the one named last changes fastest.
Arguments:
- local_block: float32 [32768, 1024], P(('parts', 'snp')), parts along dimension 0, may hold values from -1 to 1, as said below
- next_block: float32 [32768, 1024], P(('parts', 'snp')), parts along dimension 0, may hold values from -1 to 1, as said below
- shrinkage: float32 [64, 1], replicated, may hold values from 0.3 to 1
- marginal: float32 [64, 32768], P(None, ('parts', 'snp')), parts along dimension 1, may hold values from -12 to 12
- warm_start: float32 [64, 32768], P(None, ('parts', 'snp')), parts along dimension 1, may hold values from -3 to 3
Outputs:
- solution: float32 [64, 32768], P(None, ('parts', 'snp')), parts along dimension 1
- residual: float32 [64, 32768], P(None, ('parts', 'snp')), parts along dimension 1
There are 2 independent parts, one for each index of `parts`. A program takes and returns all parts, laid end to end along the dimension named above; an argument that names none is the same for every part. Nothing has to cross between parts.
Inputs may be any that keep to these rules, and one draw needn't show every extreme that they name: `local_block`: each 1024 x 1024 block of rows is symmetric with ones on its diagonal. `next_block`: inside each 1024 x 1024 block of rows, entries whose column index exceeds the row index are zero; the last block of rows is zero.
All inputs are finite; a program needn't handle non-finite values.
Results may differ from a plain program's by a relative error of at most 0.0003.
Values sent between devices are 32-bit elements; how exact they have to be, the bound alone decides.
No kernel may reach another device: no remote copies, remote signals or barrier semaphores. Data moves between devices by JAX's collectives and lax.ppermute only.
A program may use at most 64 MiB of HBM per device.

v0:
```python
import jax
import jax.numpy as jnp
from jax import lax
from jax.sharding import PartitionSpec as P

ITERS = 3


HIGH = lax.Precision.HIGHEST


def shifted(block, axis, distance):
    devices = range(lax.axis_size(axis))
    route = [(i - distance, i) for i in devices if i - distance in devices]
    return lax.ppermute(block, axis, route)


def product(left, right):
    return jnp.dot(left, right, precision=HIGH, preferred_element_type=jnp.float32)


def product_across(left, right):
    return lax.dot_general(
        left, right, (((1,), (1,)), ((), ())), precision=HIGH, preferred_element_type=jnp.float32
    )


def paired(residual, image):
    return lax.psum(
        (
            jnp.sum(residual * residual, axis=1, keepdims=True),
            jnp.sum(residual * image, axis=1, keepdims=True),
        ),
        "snp",
    )


def on_device(local_block, next_block, shrinkage, marginal, warm_start):

    def operate(field):
        upper = shifted(field, "snp", -1)
        lower = shifted(product(field, next_block), "snp", 1)
        total = product(field, local_block) + product_across(upper, next_block) + lower
        return total + shrinkage * field

    solution = warm_start
    residual = marginal - operate(warm_start)
    image = operate(residual)
    norm_now, curve = paired(residual, image)
    alpha = norm_now / curve
    direction, along = (residual, image)
    for step in range(ITERS):
        solution = solution + alpha * direction
        residual = residual - alpha * along
        if step + 1 < ITERS:
            image = operate(residual)
            norm_next, curve = paired(residual, image)
            ratio = norm_next / norm_now
            alpha = norm_next / (curve - ratio * norm_next / alpha)
            direction = residual + ratio * direction
            along = image + ratio * along
            norm_now = norm_next
    return (solution, residual)


def solution(mesh):
    return jax.shard_map(
        on_device,
        mesh=mesh,
        in_specs=(
            P(("parts", "snp"), None),
            P(("parts", "snp"), None),
            P(),
            P(None, ("parts", "snp")),
            P(None, ("parts", "snp")),
        ),
        out_specs=(P(None, ("parts", "snp")), P(None, ("parts", "snp"))),
        check_vma=False,
    )
```

profile of v0, /device:TPU:0, one launch (start us, length us, event | category | flops | bytes accessed | tf_op | source)
XLA Modules:
  0.0 163.6 jit_solution(8602006641580616598)
XLA Ops:
  0.6 0.0 copy-start
  0.7 1.6 collective-permute-start
  2.2 4.9 %fusion.11 = f32[64,1024]{1,0:T(8,128)S(1)} fusion(f32[64,1024]{1,0:T(8,128)} %param.9, f32[1024,1024]{1,0:T(8,128)} %param.6), kind=kOutput, calls=%fused_computation.30 | convolution fusion | flops 805306368 | bytes 4718592 | tf_op jit(solution)/shard_map/dot_general | solution.py:19
  7.2 3.0 %collective-permute-start.1 = (f32[64,1024]{1,0:T(8,128)S(1)}, f32[64,1024]{1,0:T(8,128)S(1)}, u32[]{:S(2)}, u32[]{:S(2)}) collective-permute-start(f32[64,1024]{1,0:T(8,128)S(1)} %fusion.11), channel_id=1, source_target_pairs={{0,1},{1,2},{2,3},{3,4},{4,5},{5,6},{6,7},{7,8},{8,9},{9,10},{10,1... | collective-permute-start | bytes 786440 | tf_op jit(solution)/shard_map/ppermute | solution.py:15
  10.2 4.8 %fusion.10 = f32[64,1024]{1,0:T(8,128)S(1)} fusion(f32[64,1024]{1,0:T(8,128)S(1)} %copy-done.6, f32[1024,1024]{1,0:T(8,128)} %param.5), kind=kOutput, calls=%fused_computation.29 | convolution fusion | flops 805306368 | bytes 4718592 | tf_op jit(solution)/shard_map/dot_general | solution.py:19
  15.1 0.0 collective-permute-done
  15.1 4.2 %fusion.8 = f32[64,1024]{1,0:T(8,128)S(1)} fusion(f32[64,1024]{1,0:T(8,128)S(1)} %copy-done.7, f32[64,1024]{1,0:T(8,128)S(1)} %collective-permute-done.1, f32[64,1024]{1,0:T(8,128)S(1)} %fusion.10, f32[64,1024]{1,0:T(8,128)S(1)} %collective-permute-done, f32[1024,1024]{1,0:T(8,128)S(1)} %copy-done, f32[64,1024]{1,0:T(8,128)S(1)} %copy-done.6, ...), kind=kOutput, calls=%fused_computation.12 | convolution fusion | flops 805634048 | bytes 5767424 | tf_op jit(solution)/shard_map/dot_general | solution.py:23
  19.3 0.0 copy-start.3
  19.3 1.6 collective-permute-start.2
  20.9 2.7 %fusion.13 = f32[64,1024]{1,0:T(8,128)S(1)} fusion(f32[64,1024]{1,0:T(8,128)S(1)} %fusion.8, f32[1024,1024]{1,0:T(8,128)S(1)} %copy-done), kind=kOutput, calls=%fused_computation.32 | convolution fusion | flops 805306368 | bytes 4718592 | tf_op jit(solution)/shard_map/dot_general | solution.py:19
  23.5 5.3 %collective-permute-start.3 = (f32[64,1024]{1,0:T(8,128)S(1)}, f32[64,1024]{1,0:T(8,128)S(1)}, u32[]{:S(2)}, u32[]{:S(2)}) collective-permute-start(f32[64,1024]{1,0:T(8,128)S(1)} %fusion.13), channel_id=1, source_target_pairs={{0,1},{1,2},{2,3},{3,4},{4,5},{5,6},{6,7},{7,8},{8,9},{9,10},{10,1... | collective-permute-start | bytes 786440 | tf_op jit(solution)/shard_map/ppermute | solution.py:15
  28.9 0.0 collective-permute-done.2
  28.9 4.2 %fusion.12 = f32[64,1024]{1,0:T(8,128)S(1)} fusion(f32[64,1024]{1,0:T(8,128)S(1)} %collective-permute-done.2, f32[1024,1024]{1,0:T(8,128)S(1)} %copy-done), kind=kOutput, calls=%fused_computation.31 | convolution fusion | flops 805306368 | bytes 4718592 | tf_op jit(solution)/shard_map/dot_general | solution.py:23
  33.0 2.8 %multiply_reduce_fusion.4 = (f32[64]{0:T(128)S(1)}, f32[64]{0:T(128)S(1)}, f32[64,1024]{1,0:T(8,128)S(1)}) fusion(f32[64,1024]{1,0:T(8,128)S(1)} %fusion.8, f32[64]{0:T(128)S(1)} %bitcast.40, f32[64,1024]{1,0:T(8,128)S(1)} %collective-permute-done.3, f32[64,1024]{1,0:T(8,128)S(1)} %fusion.12, f32[1024,1024]{1,0:T(8,128)S(1)} %copy-done.3), kind=kOutput, calls=%fused_computation.22 | convolution fusion | flops 805830528 | bytes 5243648 | tf_op jit(solution)/shard_map/dot_general | solution.py:19
  35.8 32.8 %all-reduce.2 = (f32[64,1]{0,1:T(1,128)S(1)}, f32[64,1]{0,1:T(1,128)S(1)}) all-reduce(f32[64,1]{0,1:T(1,128)S(1)} %bitcast.49, f32[64,1]{0,1:T(1,128)S(1)} %bitcast.48), channel_id=1, replica_groups=mesh['parts'=2,'snp'=16] {'snp'}, use_global_device_ids=true, to_apply=%region_1.0 | all-reduce | flops 128 | bytes 1024 | tf_op jit(solution)/shard_map/psum | solution.py:29
  68.6 0.1 multiply_subtract_fusion.2
  68.7 0.0 copy-start.4
  68.7 1.6 collective-permute-start.4
  70.3 5.6 %fusion.15 = f32[64,1024]{1,0:T(8,128)S(1)} fusion(f32[64,1024]{1,0:T(8,128)S(1)} %multiply_subtract_fusion.2, f32[1024,1024]{1,0:T(8,128)} %param.6), kind=kOutput, calls=%fused_computation.34 | convolution fusion | flops 805306368 | bytes 4718592 | tf_op jit(solution)/shard_map/dot_general | solution.py:19
  75.9 2.5 %collective-permute-start.5 = (f32[64,1024]{1,0:T(8,128)S(1)}, f32[64,1024]{1,0:T(8,128)S(1)}, u32[]{:S(2)}, u32[]{:S(2)}) collective-permute-start(f32[64,1024]{1,0:T(8,128)S(1)} %fusion.15), channel_id=1, source_target_pairs={{0,1},{1,2},{2,3},{3,4},{4,5},{5,6},{6,7},{7,8},{8,9},{9,10},{10,1... | collective-permute-start | bytes 786440 | tf_op jit(solution)/shard_map/ppermute | solution.py:15
  78.4 4.2 %fusion.14 = f32[64,1024]{1,0:T(8,128)S(1)} fusion(f32[64,1024]{1,0:T(8,128)S(1)} %collective-permute-done.4, f32[1024,1024]{1,0:T(8,128)S(1)} %copy-done.1), kind=kOutput, calls=%fused_computation.33 | convolution fusion | flops 805306368 | bytes 4718592 | tf_op jit(solution)/shard_map/dot_general | solution.py:23
  82.6 2.8 %multiply_reduce_fusion.2 = (f32[64]{0:T(128)S(1)}, f32[64]{0:T(128)S(1)}, f32[64,1024]{1,0:T(8,128)S(1)}) fusion(f32[64,1024]{1,0:T(8,128)S(1)} %multiply_subtract_fusion.2, f32[64]{0:T(128)S(1)} %bitcast.41, f32[64,1024]{1,0:T(8,128)S(1)} %collective-permute-done.5, f32[64,1024]{1,0:T(8,128)S(1)} %fusion.14, f32[1024,1024]{1,0:T(8,128)S(1)} %copy-done.4), kind=kOutput, calls=%fused_computation.19 | convolution fusion | flops 805830528 | bytes 5243648 | tf_op jit(solution)/shard_map/dot_general | solution.py:19
  85.4 29.5 %all-reduce.1 = (f32[64,1]{0,1:T(1,128)S(1)}, f32[64,1]{0,1:T(1,128)S(1)}) all-reduce(f32[64,1]{0,1:T(1,128)S(1)} %bitcast.51, f32[64,1]{0,1:T(1,128)S(1)} %bitcast.50), channel_id=1, replica_groups=mesh['parts'=2,'snp'=16] {'snp'}, use_global_device_ids=true, to_apply=%region_5.0 | all-reduce | flops 128 | bytes 1024 | tf_op jit(solution)/shard_map/psum | solution.py:29
  114.9 0.1 multiply_subtract_fusion.1
  115.0 0.0 copy-start.2
  115.0 5.0 %fusion.17 = f32[64,1024]{1,0:T(8,128)S(1)} fusion(f32[64,1024]{1,0:T(8,128)S(1)} %multiply_subtract_fusion.1, f32[1024,1024]{1,0:T(8,128)} %param.6), kind=kOutput, calls=%fused_computation.36 | convolution fusion | flops 805306368 | bytes 4718592 | tf_op jit(solution)/shard_map/dot_general | solution.py:19
  120.0 1.3 collective-permute-start.6
  121.3 3.3 %collective-permute-start.7 = (f32[64,1024]{1,0:T(8,128)S(1)}, f32[64,1024]{1,0:T(8,128)S(1)}, u32[]{:S(2)}, u32[]{:S(2)}) collective-permute-start(f32[64,1024]{1,0:T(8,128)S(1)} %fusion.17), channel_id=1, source_target_pairs={{0,1},{1,2},{2,3},{3,4},{4,5},{5,6},{6,7},{7,8},{8,9},{9,10},{10,1... | collective-permute-start | bytes 786440 | tf_op jit(solution)/shard_map/ppermute | solution.py:15
  124.6 2.6 %fusion.16 = f32[64,1024]{1,0:T(8,128)S(1)} fusion(f32[64,1024]{1,0:T(8,128)S(1)} %multiply_subtract_fusion.1, f32[1024,1024]{1,0:T(8,128)S(1)} %copy-done.5), kind=kOutput, calls=%fused_computation.35 | convolution fusion | flops 805306368 | bytes 4718592 | tf_op jit(solution)/shard_map/dot_general | solution.py:19
  127.3 4.3 %multiply_reduce_fusion = (f32[64]{0:T(128)S(1)}, f32[64]{0:T(128)S(1)}, f32[64,1024]{1,0:T(8,128)S(1)}) fusion(f32[64,1024]{1,0:T(8,128)S(1)} %multiply_subtract_fusion.1, f32[64]{0:T(128)S(1)} %bitcast.42, f32[64,1024]{1,0:T(8,128)S(1)} %collective-permute-done.7, f32[64,1024]{1,0:T(8,128)S(1)} %fusion.16, f32[64,1024]{1,0:T(8,128)S(1)} %collective-permute-done.6, ...), kind=kOutput, calls=%fused_computation.15 | convolution fusion | flops 805830528 | bytes 5505792 | tf_op jit(solution)/shard_map/dot_general | solution.py:23
  131.6 30.9 %all-reduce = (f32[64,1]{0,1:T(1,128)S(1)}, f32[64,1]{0,1:T(1,128)S(1)}) all-reduce(f32[64,1]{0,1:T(1,128)S(1)} %bitcast.47, f32[64,1]{0,1:T(1,128)S(1)} %bitcast.46), channel_id=1, replica_groups=mesh['parts'=2,'snp'=16] {'snp'}, use_global_device_ids=true, to_apply=%region_9.0 | all-reduce | flops 128 | bytes 1024 | tf_op jit(solution)/shard_map/psum | solution.py:29
  162.5 1.0 multiply_subtract_fusion
  (23 shorter events, 0.1 us)
Async XLA Ops:
  0.6 9.6 %copy-start.6 = (f32[64,1024]{1,0:T(8,128)S(1)}, f32[64,1024]{1,0:T(8,128)}, u32[]{:S(2)}) copy-start(f32[64,1024]{1,0:T(8,128)} %param.9) | copy-start | bytes 786436
  0.6 14.4 %copy-start = (f32[1024,1024]{1,0:T(8,128)S(1)}, f32[1024,1024]{1,0:T(8,128)}, u32[]{:S(2)}) copy-start(f32[1024,1024]{1,0:T(8,128)} %param.6) | copy-start | bytes 12582916
  0.7 14.4 %copy-start.8 = (f32[64,1]{0,1:T(1,128)S(1)}, f32[64,1]{0,1:T(1,128)}, u32[]{:S(2)}) copy-start(f32[64,1]{0,1:T(1,128)} %param.7) | copy-start | bytes 772
  0.7 14.4 %copy-start.7 = (f32[64,1024]{1,0:T(8,128)S(1)}, f32[64,1024]{1,0:T(8,128)}, u32[]{:S(2)}) copy-start(f32[64,1024]{1,0:T(8,128)} %param.8) | copy-start | bytes 786436
  0.7 14.4 %collective-permute-start = (f32[64,1024]{1,0:T(8,128)}, f32[64,1024]{1,0:T(8,128)S(1)}, u32[]{:S(2)}, u32[]{:S(2)}) collective-permute-start(f32[64,1024]{1,0:T(8,128)} %param.9), channel_id=1, source_target_pairs={{1,0},{2,1},{3,2},{4,3},{5,4},{6,5},{7,6},{8,7},{9,8},{10,9},{11,1... | collective-permute-start | bytes 786440 | tf_op jit(solution)/shard_map/ppermute | solution.py:15
  7.2 7.9 %collective-permute-start.1 = (f32[64,1024]{1,0:T(8,128)S(1)}, f32[64,1024]{1,0:T(8,128)S(1)}, u32[]{:S(2)}, u32[]{:S(2)}) collective-permute-start(f32[64,1024]{1,0:T(8,128)S(1)} %fusion.11), channel_id=1, source_target_pairs={{0,1},{1,2},{2,3},{3,4},{4,5},{5,6},{6,7},{7,8},{8,9},{9,10},{10,1... | collective-permute-start | bytes 786440 | tf_op jit(solution)/shard_map/ppermute | solution.py:15
  19.3 13.7 %copy-start.3 = (f32[1024,1024]{1,0:T(8,128)S(1)}, f32[1024,1024]{1,0:T(8,128)}, u32[]{:S(2)}) copy-start(f32[1024,1024]{1,0:T(8,128)} %param.5) | copy-start | bytes 12582916
  19.3 9.6 %collective-permute-start.2 = (f32[64,1024]{1,0:T(8,128)S(1)}, f32[64,1024]{1,0:T(8,128)S(1)}, u32[]{:S(2)}, u32[]{:S(2)}) collective-permute-start(f32[64,1024]{1,0:T(8,128)S(1)} %fusion.8), channel_id=1, source_target_pairs={{1,0},{2,1},{3,2},{4,3},{5,4},{6,5},{7,6},{8,7},{9,8},{10,9},{11,1... | collective-permute-start | bytes 786440 | tf_op jit(solution)/shard_map/ppermute | solution.py:15
  23.5 9.5 %collective-permute-start.3 = (f32[64,1024]{1,0:T(8,128)S(1)}, f32[64,1024]{1,0:T(8,128)S(1)}, u32[]{:S(2)}, u32[]{:S(2)}) collective-permute-start(f32[64,1024]{1,0:T(8,128)S(1)} %fusion.13), channel_id=1, source_target_pairs={{0,1},{1,2},{2,3},{3,4},{4,5},{5,6},{6,7},{7,8},{8,9},{9,10},{10,1... | collective-permute-start | bytes 786440 | tf_op jit(solution)/shard_map/ppermute | solution.py:15
  68.6 9.8 %copy-start.1 = (f32[1024,1024]{1,0:T(8,128)S(1)}, f32[1024,1024]{1,0:T(8,128)}, u32[]{:S(2)}) copy-start(f32[1024,1024]{1,0:T(8,128)} %param.6) | copy-start | bytes 12582916
  68.7 13.9 %copy-start.4 = (f32[1024,1024]{1,0:T(8,128)S(1)}, f32[1024,1024]{1,0:T(8,128)}, u32[]{:S(2)}) copy-start(f32[1024,1024]{1,0:T(8,128)} %param.5) | copy-start | bytes 12582916
  68.7 9.7 %collective-permute-start.4 = (f32[64,1024]{1,0:T(8,128)S(1)}, f32[64,1024]{1,0:T(8,128)S(1)}, u32[]{:S(2)}, u32[]{:S(2)}) collective-permute-start(f32[64,1024]{1,0:T(8,128)S(1)} %multiply_subtract_fusion.2), channel_id=1, source_target_pairs={{1,0},{2,1},{3,2},{4,3},{5,4},{6,5},{7,6},{8,7},{9,8},{10,9},{11,1... | collective-permute-start | bytes 786440 | tf_op jit(solution)/shard_map/ppermute | solution.py:15
  75.9 6.7 %collective-permute-start.5 = (f32[64,1024]{1,0:T(8,128)S(1)}, f32[64,1024]{1,0:T(8,128)S(1)}, u32[]{:S(2)}, u32[]{:S(2)}) collective-permute-start(f32[64,1024]{1,0:T(8,128)S(1)} %fusion.15), channel_id=1, source_target_pairs={{0,1},{1,2},{2,3},{3,4},{4,5},{5,6},{6,7},{7,8},{8,9},{9,10},{10,1... | collective-permute-start | bytes 786440 | tf_op jit(solution)/shard_map/ppermute | solution.py:15
  114.9 9.7 %copy-start.5 = (f32[1024,1024]{1,0:T(8,128)S(1)}, f32[1024,1024]{1,0:T(8,128)}, u32[]{:S(2)}) copy-start(f32[1024,1024]{1,0:T(8,128)} %param.5) | copy-start | bytes 12582916
  115.0 12.3 %copy-start.2 = (f32[1024,1024]{1,0:T(8,128)S(1)}, f32[1024,1024]{1,0:T(8,128)}, u32[]{:S(2)}) copy-start(f32[1024,1024]{1,0:T(8,128)} %param.6) | copy-start | bytes 12582916
  120.0 7.3 %collective-permute-start.6 = (f32[64,1024]{1,0:T(8,128)S(1)}, f32[64,1024]{1,0:T(8,128)S(1)}, u32[]{:S(2)}, u32[]{:S(2)}) collective-permute-start(f32[64,1024]{1,0:T(8,128)S(1)} %multiply_subtract_fusion.1), channel_id=1, source_target_pairs={{1,0},{2,1},{3,2},{4,3},{5,4},{6,5},{7,6},{8,7},{9,8},{10,9},{11,1... | collective-permute-start | bytes 786440 | tf_op jit(solution)/shard_map/ppermute | solution.py:15
  121.3 6.0 %collective-permute-start.7 = (f32[64,1024]{1,0:T(8,128)S(1)}, f32[64,1024]{1,0:T(8,128)S(1)}, u32[]{:S(2)}, u32[]{:S(2)}) collective-permute-start(f32[64,1024]{1,0:T(8,128)S(1)} %fusion.17), channel_id=1, source_target_pairs={{0,1},{1,2},{2,3},{3,4},{4,5},{5,6},{6,7},{7,8},{8,9},{9,10},{10,1... | collective-permute-start | bytes 786440 | tf_op jit(solution)/shard_map/ppermute | solution.py:15
where the time goes:
time: 164 us
  blocking collectives  93.2 us (57%)
  matrix products  47.9 us (29%)
  starting transfers between devices  20.2 us (12%)
    psum x3, blocking collectives, paired(): lax.psum((jnp.sum(residual * residual, axis=1, keepdims=True), jnp.sum(re...  93.2 us
    dot_general x8, matrix products, product(): jnp.dot(left, right, precision=HIGH, preferred_element_type=jnp.float32)  31.2 us
    ppermute x8, starting transfers between devices, shifted(): return lax.ppermute(block, axis, route)  20.2 us
    dot_general x4, matrix products, product_across(): lax.dot_general(left, right, (((1,), (1,)), ((), ())), precision=HIGH, pr...  16.8 us
  transfers between devices with their start and end apart: 8, of which 0 were waited for; matrix products, arithmetic and copies ran while one was open for 18% of the time, Pallas kernels for 0%

commit v1 on v0

v1 whole, which is shorter than its diff:
```python
import functools

import jax
import jax.numpy as jnp
from jax import lax
from jax.experimental import pallas as pl
from jax.experimental.pallas import tpu as pltpu
from jax.sharding import PartitionSpec as P

ITERS = 3
F32 = jnp.float32
BF16 = jnp.bfloat16
VMEM = pltpu.VMEM
MOMENT_ROWS = 8


def tile_of(size):
    return 256 if size % 256 == 0 else size


def halves(x):
    high = x.astype(BF16)
    return high, (x - high.astype(F32)).astype(BF16)


def dot(left, right, across):
    dims = (((1,), (1 if across else 0,)), ((), ()))
    return lax.dot_general(left, right, dims, preferred_element_type=F32)


def product(both, right_high, right_low, across=False):
    rows = both.shape[0] // 2
    main = dot(both, right_high, across)
    return main[:rows] + main[rows:] + dot(both[:rows], right_low, across)


def stacked(field):
    return jnp.concatenate(halves(field), axis=0)


def coupling(both, high, low, store):
    size = high.shape[0]
    tile = tile_of(size)
    for start in range(0, size, tile):
        rows, cols = pl.ds(start, size - start), pl.ds(start, tile)
        store(start, product(both[:, start:], high[rows, cols], low[rows, cols]))


def forward(both, high, low, store):
    size = high.shape[0]
    tile = tile_of(size)
    for start in range(0, size, tile):
        rows, cols = pl.ds(start, tile), pl.ds(0, start + tile)
        store(start, product(both[:, : start + tile], high[rows, cols], low[rows, cols], True))


def sends(odd, field, high, low, pair_ref, cross_ref):
    tile = tile_of(field.shape[1])

    def store(start, part):
        cols = pl.ds(start, tile)
        own = field[:, start : start + tile]
        pair_ref[:, cols] = jnp.where(odd, own, part)
        cross_ref[:, cols] = jnp.where(odd, part, own)

    coupling(stacked(field), high, low, store)


def begin_kernel(odd_ref, next_ref, field_ref, high_ref, low_ref, pair_ref, cross_ref, raw, sems):
    size = raw.shape[0]
    tile = tile_of(size)
    copies = []
    for index, start in enumerate(range(0, size, tile)):
        part = (pl.ds(start, tile), pl.ds(0, start + tile))
        copies.append(pltpu.make_async_copy(next_ref.at[part], raw.at[part], sems.at[index]))
        copies[-1].start()
    for index, start in enumerate(range(0, size, tile)):
        part = (pl.ds(start, tile), pl.ds(0, start + tile))
        copies[index].wait()
        high, low = halves(raw[part])
        high_ref[part] = high
        low_ref[part] = low
    sends(odd_ref[0] == 1, field_ref[...], high_ref, low_ref, pair_ref, cross_ref)


def local_kernel(local_ref, field_ref, high_ref, low_ref, own_ref):
    size = local_ref.shape[0]
    tile = tile_of(size)
    both = stacked(field_ref[...])
    total = None
    for start in range(0, size, tile):
        rows = pl.ds(start, tile)
        row = lax.broadcasted_iota(jnp.int32, (tile, size), 0) + start
        col = lax.broadcasted_iota(jnp.int32, (tile, size), 1)
        high, low = halves(local_ref[rows, :] - jnp.where(row == col, 1.0, 0.0))
        high_ref[rows, :] = high
        low_ref[rows, :] = low
        part = product(both[:, start : start + tile], high, low)
        total = part if total is None else total + part
    own_ref[...] = total


def moment(left, right):
    return jnp.sum(left * right, axis=1, keepdims=True)


def own_kernel(before_ref, field_ref, high_ref, low_ref, own_ref, moments_ref):
    field = field_ref[...]
    own_ref[...] = product(stacked(field), high_ref[...], low_ref[...])
    lane = lax.broadcasted_iota(jnp.int32, moments_ref.shape, 1)
    cross = 0.0 if before_ref is None else moment(before_ref[...], field)
    moments_ref[...] = jnp.where(lane == 0, moment(field, field), jnp.where(lane == 1, cross, 0.0))


def received(odd, pair_ref, cross_ref):
    upper = jnp.where(odd, cross_ref[...], pair_ref[...])
    lower = jnp.where(odd, pair_ref[...], cross_ref[...])
    return upper, lower


def first_kernel(
    odd_ref, own_ref, got_pair_ref, got_cross_ref, high_in, low_in, shrinkage_ref, marginal_ref, start_ref,
    field_ref, pair_ref, cross_ref,
):
    odd = odd_ref[0] == 1
    tile = tile_of(own_ref.shape[1])
    upper, lower = received(odd, got_pair_ref, got_cross_ref)
    base = marginal_ref[...] - (1.0 + shrinkage_ref[...]) * start_ref[...] - own_ref[...] - lower

    def store(start, part):
        field_ref[:, pl.ds(start, tile)] = base[:, start : start + tile] - part

    forward(stacked(upper), high_in, low_in, store)
    sends(odd, field_ref[...], high_in, low_in, pair_ref, cross_ref)


def step_kernel(
    odd_ref, own_ref, got_pair_ref, got_cross_ref, high_in, low_in, field_ref, pair_ref, cross_ref,
):
    odd = odd_ref[0] == 1
    tile = tile_of(own_ref.shape[1])
    upper, lower = received(odd, got_pair_ref, got_cross_ref)
    base = own_ref[...] + lower

    def store(start, part):
        field_ref[:, pl.ds(start, tile)] = base[:, start : start + tile] + part

    forward(stacked(upper), high_in, low_in, store)
    sends(odd, field_ref[...], high_in, low_in, pair_ref, cross_ref)


def reduce_kernel(odd_ref, field_ref, own_ref, got_pair_ref, got_cross_ref, one_ref, two_ref, three_ref, out_ref):
    odd = odd_ref[0] == 1
    _, lower = received(odd, got_pair_ref, got_cross_ref)
    traits = field_ref.shape[0]
    last = moment(field_ref[...], own_ref[...] + 2.0 * lower)
    lane = lax.broadcasted_iota(jnp.int32, (traits, 128), 1)
    parts = (
        one_ref[:, 0:1],
        two_ref[:, 1:2],
        two_ref[:, 0:1],
        three_ref[:, 1:2],
        three_ref[:, 0:1],
        last,
    )
    table = jnp.zeros((traits, 128), F32)
    for index, part in enumerate(parts):
        table = jnp.where(lane == index, part, table)
    rows = jnp.transpose(table)[:MOMENT_ROWS]
    for index in range(out_ref.shape[0]):
        out_ref[index] = rows


def coefficients(moments, shift):
    def inner(left, right):
        total = None
        for i, a in enumerate(left):
            for j, b in enumerate(right):
                term = (a * b) * moments[i + j]
                total = term if total is None else total + term
        return total

    one = jnp.ones_like(shift)
    zero = jnp.zeros_like(shift)
    residual, direction, gain = [one], [one], []
    norm_now = moments[0]
    for step in range(ITERS):
        image = [shift * a + b for a, b in zip(direction + [zero], [zero] + direction)]
        alpha = norm_now / inner(direction, image)
        gain = [a + alpha * b for a, b in zip(gain + [zero], direction)]
        residual = [a - alpha * b for a, b in zip(residual + [zero], image)]
        if step + 1 < ITERS:
            norm_next = inner(residual, residual)
            ratio = norm_next / norm_now
            direction = [a + ratio * b for a, b in zip(residual, direction + [zero])]
            norm_now = norm_next
    return gain, residual


def final_kernel(
    odd_ref, table_ref, shrinkage_ref, start_ref, zero_ref, one_ref, two_ref, own_ref, got_pair_ref, got_cross_ref,
    high_in, low_in, solution_ref, residual_ref,
):
    odd = odd_ref[0] == 1
    traits, size = own_ref.shape
    tile = tile_of(size)
    upper, lower = received(odd, got_pair_ref, got_cross_ref)
    sums = jnp.sum(table_ref[...], axis=0)
    columns = jnp.transpose(jnp.concatenate([sums, jnp.zeros((128 - MOMENT_ROWS, traits), F32)], axis=0))
    moments = [columns[:, i : i + 1] for i in range(2 * ITERS)]
    gain, residual = coefficients(moments, 1.0 + shrinkage_ref[...])
    zero, one, two = zero_ref[...], one_ref[...], two_ref[...]
    solution_ref[...] = start_ref[...] + gain[0] * zero + gain[1] * one + gain[2] * two
    base = residual[0] * zero + residual[1] * one + residual[2] * two + residual[3] * (own_ref[...] + lower)

    def store(start, part):
        residual_ref[:, pl.ds(start, tile)] = base[:, start : start + tile] + residual[3] * part

    forward(stacked(upper), high_in, low_in, store)


def call(kernel, out, *args, spaces=None, scratch=(), limit=32):
    shapes = [jax.ShapeDtypeStruct(shape, dtype) for shape, dtype in out]
    spaces = spaces or {}
    specs = [
        pl.BlockSpec(memory_space=spaces.get(i, VMEM)) for i in range(len(args))
    ]
    return pl.pallas_call(
        kernel,
        out_shape=shapes,
        in_specs=specs,
        out_specs=[pl.BlockSpec(memory_space=VMEM) for _ in shapes],
        scratch_shapes=scratch,
        compiler_params=pltpu.CompilerParams(vmem_limit_bytes=limit * 1024 * 1024),
    )(*args)


def on_device(local_block, next_block, shrinkage, marginal, warm_start):
    count = lax.axis_size("snp")
    odd = lax.rem(lax.axis_index("snp"), 2).astype(jnp.int32).reshape(1)
    traits, size = warm_start.shape
    field = ((traits, size), F32)
    matrix = ((size, size), BF16)
    steps = size // tile_of(size)
    on_chip = [(i, i ^ 1) for i in range(count) if i ^ 1 < count]
    off_chip = [(i, ((i - 1) ^ 1) + 1) for i in range(1, count) if ((i - 1) ^ 1) + 1 < count]
    smem = {0: pltpu.SMEM}

    def swap(pair, cross):
        got_cross = lax.ppermute(cross, "snp", off_chip)
        got_pair = lax.ppermute(pair, "snp", on_chip)
        return got_pair, got_cross

    high_n, low_n, pair, cross = call(
        begin_kernel,
        [matrix, matrix, field, field],
        odd, next_block, warm_start,
        spaces={0: pltpu.SMEM, 1: pl.ANY},
        scratch=(pltpu.VMEM((size, size), F32), pltpu.SemaphoreType.DMA((steps,))),
    )
    got = swap(pair, cross)
    high_l, low_l, own = call(local_kernel, [matrix, matrix, field], local_block, warm_start)
    zero, pair, cross = call(
        first_kernel,
        [field, field, field],
        odd, own, *got, high_n, low_n, shrinkage, marginal, warm_start,
        spaces=smem,
    )
    got = swap(pair, cross)
    table = ((traits, 128), F32)
    fields, tables = [zero], []
    for step in range(ITERS):
        if step == 0:
            own, part = call(
                lambda *refs: own_kernel(None, *refs), [field, table], fields[0], high_l, low_l
            )
        else:
            own, part = call(own_kernel, [field, table], fields[-2], fields[-1], high_l, low_l)
        tables.append(part)
        if step + 1 < ITERS:
            after, pair, cross = call(
                step_kernel, [field, field, field], odd, own, *got, high_n, low_n, spaces=smem
            )
            got = swap(pair, cross)
            fields.append(after)
    (moments,) = call(
        reduce_kernel,
        [((count, MOMENT_ROWS, traits), F32)],
        odd, fields[-1], own, *got, *tables,
        spaces=smem,
    )
    moments = lax.all_to_all(moments, "snp", 0, 0)
    return tuple(
        call(
            final_kernel,
            [field, field],
            odd, moments, shrinkage, warm_start, *fields, own, *got, high_n, low_n,
            spaces=smem,
        )
    )


def solution(mesh):
    return jax.shard_map(
        on_device,
        mesh=mesh,
        in_specs=(
            P(("parts", "snp"), None),
            P(("parts", "snp"), None),
            P(),
            P(None, ("parts", "snp")),
            P(None, ("parts", "snp")),
        ),
        out_specs=(P(None, ("parts", "snp")), P(None, ("parts", "snp"))),
        check_vma=False,
    )
```

time: 164 us -> 78.8 us (0.48)
  blocking collectives: 93.2 us -> 21.4 us
  matrix products: 47.9 us -> 0 us
  local copies, waits for them, and re-layouts: 0.05 us -> 16.9 us
  Pallas kernels: 0 us -> 12.2 us
  starting transfers between devices: 20.2 us -> 26.3 us
    psum x3 -> x0, blocking collectives: 93.2 us -> none  [paired(): lax.psum((jnp.sum(residual * residual, axis=1, keepdims=True), jnp.sum(re...]
    dot_general x12 -> x0, matrix products: 47.9 us -> none  [the longest x8 31.2 us: product(): jnp.dot(left, right, precision=HIGH, preferred_element_type=jnp.float32)]
    all_to_all x0 -> x1, blocking collectives: none -> 21.4 us  [on_device(): moments = lax.all_to_all(moments, 'snp', 0, 0)]
    unnamed x18 -> x43, local copies, waits for them, and re-layouts: 0.05 us -> 16.4 us
    pallas_call x0 -> x10, Pallas kernels: none -> 12.2 us  [call(): pl.pallas_call(kernel, out_shape=shapes, in_specs=specs, out_specs=[pl.Bl...]
    ppermute x8, starting transfers between devices: 20.2 us -> 26.3 us  [the longest x4 23.5 us: swap(): got_pair = lax.ppermute(pair, 'snp', on_chip)]
  transfers between devices with their start and end apart: 8 -> 8, of which waited for: 0 -> 0; matrix products, arithmetic and copies ran while one was open for 18% -> 0% of each run, Pallas kernels for 0% -> 4%
where the time goes in v1:
time: 78.8 us; the launch traced here: 78.3 us
  starting transfers between devices  26.3 us (33%)
  blocking collectives  21.4 us (27%)
  local copies, waits for them, and re-layouts  16.9 us (21%)
  Pallas kernels  12.2 us (15%)
  between operations  0.89 us (1%)
    ppermute x4, starting transfers between devices, swap(): got_pair = lax.ppermute(pair, 'snp', on_chip)  23.5 us
    all_to_all x1, blocking collectives, on_device(): moments = lax.all_to_all(moments, 'snp', 0, 0)  21.4 us
    unnamed x43, local copies, waits for them, and re-layouts  16.4 us
    pallas_call x10, Pallas kernels, call(): pl.pallas_call(kernel, out_shape=shapes, in_specs=specs, out_specs=[pl.Bl...  12.2 us
    ppermute x4, starting transfers between devices, swap(): got_cross = lax.ppermute(cross, 'snp', off_chip)  2.79 us
  transfers between devices with their start and end apart: 8, of which 0 were waited for; matrix products, arithmetic and copies ran while one was open for 0% of the time, Pallas kernels for 4%

profile of v1, /device:TPU:0, one launch (start us, length us, event | category | flops | bytes accessed | tf_op | source)
XLA Modules:
  0.0 78.3 jit_solution(2770948931172992923)
XLA Ops:
  0.6 0.9 %copy-done.8 = f32[64,1024]{1,0:T(8,128)S(1)} copy-done((f32[64,1024]{1,0:T(8,128)S(1)}, f32[64,1024]{1,0:T(8,128)}, u32[]{:S(2)}) %copy-start.8) | copy-done | bytes 262168
  1.6 2.2 %copy-done.10 = f32[1024,1024]{1,0:T(8,128)S(1)} copy-done((f32[1024,1024]{1,0:T(8,128)S(1)}, f32[1024,1024]{1,0:T(8,128)}, u32[]{:S(2)}) %copy-start.10) | copy-done | bytes 4194328
  3.8 2.0 %shard_map.69 = (bf16[1024,1024]{1,0:T(8,128)(2,1)S(1)}, bf16[1024,1024]{1,0:T(8,128)(2,1)S(1)}, f32[64,1024]{1,0:T(8,128)}, f32[64,1024]{1,0:T(8,128)}) custom-call(s32[1]{0:T(128)} %bitcast.odd_ref, f32[1024,1024]{1,0:T(8,128)S(1)} %copy-done.10, f32[64,1024]{1,0:T(8,128)S(1)} %copy-done.8), custom_call_target="tpu_custom_call" | custom-call | tf_op jit(solution)/shard_map/pallas_call | solution.py:228
  5.8 1.3 %copy-done = bf16[1024,1024]{1,0:T(8,128)(2,1)} copy-done((bf16[1024,1024]{1,0:T(8,128)(2,1)}, bf16[1024,1024]{1,0:T(8,128)(2,1)S(1)}, u32[]{:S(2)}) %copy-start) | copy-done | bytes 2097176
  7.7 0.8 %collective-permute-start.1 = (f32[64,1024]{1,0:T(8,128)}, f32[64,1024]{1,0:T(8,128)S(1)}, u32[]{:S(2)}, u32[]{:S(2)}) collective-permute-start(f32[64,1024]{1,0:T(8,128)} %get-tuple-element.26), channel_id=1, source_target_pairs={{1,2},{2,1},{3,4},{4,3},{5,6},{6,5},{7,8},{8,7},{9,10},{10,9},{11,... | collective-permute-start | bytes 786440 | tf_op jit(solution)/shard_map/ppermute | solution.py:250
  8.5 1.0 %shard_map.68 = (bf16[1024,1024]{1,0:T(8,128)(2,1)S(1)}, bf16[1024,1024]{1,0:T(8,128)(2,1)S(1)}, f32[64,1024]{1,0:T(8,128)S(1)}) custom-call(f32[1024,1024]{1,0:T(8,128)S(1)} %copy-done.11, f32[64,1024]{1,0:T(8,128)S(1)} %copy-done.9), custom_call_target="tpu_custom_call" | custom-call | tf_op jit(solution)/shard_map/pallas_call | solution.py:228
  9.6 1.3 %copy-done.4 = bf16[1024,1024]{1,0:T(8,128)(2,1)} copy-done((bf16[1024,1024]{1,0:T(8,128)(2,1)}, bf16[1024,1024]{1,0:T(8,128)(2,1)S(1)}, u32[]{:S(2)}) %copy-start.4) | copy-done | bytes 2097176
  10.9 1.4 %copy-done.6 = bf16[1024,1024]{1,0:T(8,128)(2,1)} copy-done((bf16[1024,1024]{1,0:T(8,128)(2,1)}, bf16[1024,1024]{1,0:T(8,128)(2,1)S(1)}, u32[]{:S(2)}) %copy-start.6) | copy-done | bytes 2097176
  12.3 0.7 copy-done.17
  13.1 1.6 %copy-done.1 = bf16[1024,1024]{1,0:T(8,128)(2,1)S(1)} copy-done((bf16[1024,1024]{1,0:T(8,128)(2,1)S(1)}, bf16[1024,1024]{1,0:T(8,128)(2,1)}, u32[]{:S(2)}) %copy-start.1) | copy-done | bytes 2097176
  14.7 0.9 %copy-done.18 = f32[64,1024]{1,0:T(8,128)S(1)} copy-done((f32[64,1024]{1,0:T(8,128)S(1)}, f32[64,1024]{1,0:T(8,128)}, u32[]{:S(2)}) %copy-start.18) | copy-done | bytes 262168
  15.6 1.6 %shard_map.70 = (f32[64,1024]{1,0:T(8,128)S(1)}, f32[64,1024]{1,0:T(8,128)S(1)}, f32[64,1024]{1,0:T(8,128)S(1)}) custom-call(s32[1]{0:T(128)} %bitcast.odd_ref, f32[64,1024]{1,0:T(8,128)S(1)} %copy-done.18, f32[64,1024]{1,0:T(8,128)S(1)} %collective-permute-done.got_pair_ref, f32[64,1024]{1,0:T(8,128)S(1)} %collective-permute-done.1.got_cross_ref, ...), custom_call_target="tpu_custom_call" | custom-call | tf_op jit(solution)/shard_map/pallas_call | solution.py:228
  17.2 5.7 %collective-permute-start.2 = (f32[64,1024]{1,0:T(8,128)S(1)}, f32[64,1024]{1,0:T(8,128)S(1)}, u32[]{:S(2)}, u32[]{:S(2)}) collective-permute-start(f32[64,1024]{1,0:T(8,128)S(1)} %get-tuple-element.33), channel_id=1, source_target_pairs={{0,1},{1,0},{2,3},{3,2},{4,5},{5,4},{6,7},{7,6},{8,9},{9,8},{10,11... | collective-permute-start | bytes 786440 | tf_op jit(solution)/shard_map/ppermute | solution.py:251
  23.0 0.7 collective-permute-start.3
  23.7 0.8 %shard_map.71 = (f32[64,1024]{1,0:T(8,128)S(1)}, f32[64,128]{1,0:T(8,128)S(1)}) custom-call(f32[64,1024]{1,0:T(8,128)S(1)} %get-tuple-element.29.refs_0_.before_ref.zero_ref, bf16[1024,1024]{1,0:T(8,128)(2,1)S(1)} %copy-done.5, bf16[1024,1024]{1,0:T(8,128)(2,1)S(1)} %copy-done.7), custom_call_target="tpu_custom_call" | custom-call | tf_op jit(solution)/shard_map/pallas_call | solution.py:228
  24.5 0.8 copy-done.2
  25.3 1.6 %shard_map.72 = (f32[64,1024]{1,0:T(8,128)S(1)}, f32[64,1024]{1,0:T(8,128)S(1)}, f32[64,1024]{1,0:T(8,128)S(1)}) custom-call(s32[1]{0:T(128)} %bitcast.odd_ref, f32[64,1024]{1,0:T(8,128)S(1)} %get-tuple-element.32.own_ref, f32[64,1024]{1,0:T(8,128)S(1)} %collective-permute-done.2.got_pair_ref, f32[64,1024]{1,0:T(8,128)S(1)} %collective-permute-done.3.got_cross_ref, ...), custom_call_target="tpu_custom_call" | custom-call | tf_op jit(solution)/shard_map/pallas_call | solution.py:228
  26.9 8.2 %collective-permute-start.4 = (f32[64,1024]{1,0:T(8,128)S(1)}, f32[64,1024]{1,0:T(8,128)S(1)}, u32[]{:S(2)}, u32[]{:S(2)}) collective-permute-start(f32[64,1024]{1,0:T(8,128)S(1)} %get-tuple-element.37), channel_id=1, source_target_pairs={{0,1},{1,0},{2,3},{3,2},{4,5},{5,4},{6,7},{7,6},{8,9},{9,8},{10,11... | collective-permute-start | bytes 786440 | tf_op jit(solution)/shard_map/ppermute | solution.py:251
  35.0 0.7 collective-permute-start.5
  35.7 0.8 %shard_map.73 = (f32[64,1024]{1,0:T(8,128)S(1)}, f32[64,128]{1,0:T(8,128)S(1)}) custom-call(f32[64,1024]{1,0:T(8,128)S(1)} %get-tuple-element.29.refs_0_.before_ref.zero_ref, f32[64,1024]{1,0:T(8,128)S(1)} %get-tuple-element.35.field_ref.before_ref.one_ref, bf16[1024,1024]{1,0:T(8,128)(2,1)S(1)} %copy-done.5, bf16[1024,1024]{1,0:T(8,128)(2,1)S(1)} %copy-done.7), custom_call_target="tpu_custom_call" | custom-call | tf_op jit(solution)/shard_map/pallas_call | solution.py:228
  36.5 1.6 %shard_map.74 = (f32[64,1024]{1,0:T(8,128)S(1)}, f32[64,1024]{1,0:T(8,128)S(1)}, f32[64,1024]{1,0:T(8,128)S(1)}) custom-call(s32[1]{0:T(128)} %bitcast.odd_ref, f32[64,1024]{1,0:T(8,128)S(1)} %get-tuple-element.36.own_ref, f32[64,1024]{1,0:T(8,128)S(1)} %collective-permute-done.4.got_pair_ref, f32[64,1024]{1,0:T(8,128)S(1)} %collective-permute-done.5.got_cross_ref, ...), custom_call_target="tpu_custom_call" | custom-call | tf_op jit(solution)/shard_map/pallas_call | solution.py:228
  38.1 9.1 %collective-permute-start.6 = (f32[64,1024]{1,0:T(8,128)S(1)}, f32[64,1024]{1,0:T(8,128)S(1)}, u32[]{:S(2)}, u32[]{:S(2)}) collective-permute-start(f32[64,1024]{1,0:T(8,128)S(1)} %get-tuple-element.41), channel_id=1, source_target_pairs={{0,1},{1,0},{2,3},{3,2},{4,5},{5,4},{6,7},{7,6},{8,9},{9,8},{10,11... | collective-permute-start | bytes 786440 | tf_op jit(solution)/shard_map/ppermute | solution.py:251
  47.2 0.7 collective-permute-start.7
  47.9 0.8 %shard_map.75 = (f32[64,1024]{1,0:T(8,128)S(1)}, f32[64,128]{1,0:T(8,128)S(1)}) custom-call(f32[64,1024]{1,0:T(8,128)S(1)} %get-tuple-element.35.field_ref.before_ref.one_ref, f32[64,1024]{1,0:T(8,128)S(1)} %get-tuple-element.39.field_ref.two_ref, bf16[1024,1024]{1,0:T(8,128)(2,1)S(1)} %copy-done.5, bf16[1024,1024]{1,0:T(8,128)(2,1)S(1)} %copy-done.7), custom_call_target="tpu_custom_call" | custom-call | tf_op jit(solution)/shard_map/pallas_call | solution.py:228
  49.0 0.7 copy-done.12
  49.7 0.7 copy-done.14
  50.5 21.4 %all_to_all.5 = f32[16,1,512]{2,1,0:T(1,128)S(1)} all-to-all(f32[16,1,512]{2,1,0:T(1,128)S(1)} %reshape.8), channel_id=1, replica_groups=mesh['parts'=2,'snp'=16] {'snp'}, dimensions={0} | all-to-all | bytes 65536 | tf_op jit(solution)/shard_map/all_to_all | solution.py:292
  72.4 0.6 reduce
  73.1 1.6 %copy-done.3 = bf16[1024,1024]{1,0:T(8,128)(2,1)S(1)} copy-done((bf16[1024,1024]{1,0:T(8,128)(2,1)S(1)}, bf16[1024,1024]{1,0:T(8,128)(2,1)}, u32[]{:S(2)}) %copy-start.3) | copy-done | bytes 2097176
  74.7 0.9 %copy-done.13 = f32[64,1024]{1,0:T(8,128)S(1)} copy-done((f32[64,1024]{1,0:T(8,128)S(1)}, f32[64,1024]{1,0:T(8,128)}, u32[]{:S(2)}) %copy-start.13) | copy-done | bytes 262168
  75.6 0.9 %copy-done.15 = f32[64,1024]{1,0:T(8,128)S(1)} copy-done((f32[64,1024]{1,0:T(8,128)S(1)}, f32[64,1024]{1,0:T(8,128)}, u32[]{:S(2)}) %copy-start.15) | copy-done | bytes 262168
  76.6 1.8 %shard_map.77 = (f32[64,1024]{1,0:T(8,128)}, f32[64,1024]{1,0:T(8,128)}) custom-call(s32[1]{0:T(128)} %bitcast.odd_ref, f32[16,8,64]{2,1,0:T(8,128)S(1)} %reshape.9.table_ref, f32[64,1]{1,0:T(8,128)S(1)} %copy.7.shrinkage_ref, f32[64,1024]{1,0:T(8,128)S(1)} %copy-done.9, f32[64,1024]{1,0:T(8,128)S(1)} %get-tuple-element.29.refs_0_.before_ref.zero_ref, ...), custom_call_target="tpu_custom_call" | custom-call | tf_op jit(solution)/shard_map/pallas_call | solution.py:228
  (40 shorter events, 1.6 us)
Async XLA Ops:
  0.6 1.0 %copy-start.8 = (f32[64,1024]{1,0:T(8,128)S(1)}, f32[64,1024]{1,0:T(8,128)}, u32[]{:S(2)}) copy-start(f32[64,1024]{1,0:T(8,128)} %start_ref.3) | copy-start | bytes 786436
  1.6 2.2 %copy-start.10 = (f32[1024,1024]{1,0:T(8,128)S(1)}, f32[1024,1024]{1,0:T(8,128)}, u32[]{:S(2)}) copy-start(f32[1024,1024]{1,0:T(8,128)} %next_ref.1) | copy-start | bytes 12582916
  3.8 4.7 %copy-start.9 = (f32[64,1024]{1,0:T(8,128)S(1)}, f32[64,1024]{1,0:T(8,128)}, u32[]{:S(2)}) copy-start(f32[64,1024]{1,0:T(8,128)} %start_ref.3) | copy-start | bytes 786436
  3.8 4.7 %copy-start.11 = (f32[1024,1024]{1,0:T(8,128)S(1)}, f32[1024,1024]{1,0:T(8,128)}, u32[]{:S(2)}) copy-start(f32[1024,1024]{1,0:T(8,128)} %local_ref.1) | copy-start | bytes 12582916
  5.8 1.4 %copy-start = (bf16[1024,1024]{1,0:T(8,128)(2,1)}, bf16[1024,1024]{1,0:T(8,128)(2,1)S(1)}, u32[]{:S(2)}) copy-start(bf16[1024,1024]{1,0:T(8,128)(2,1)S(1)} %get-tuple-element.28.low_in) | copy-start | bytes 6291460
  7.2 5.9 %collective-permute-start = (f32[64,1024]{1,0:T(8,128)}, f32[64,1024]{1,0:T(8,128)S(1)}, u32[]{:S(2)}, u32[]{:S(2)}) collective-permute-start(f32[64,1024]{1,0:T(8,128)} %get-tuple-element.25), channel_id=1, source_target_pairs={{0,1},{1,0},{2,3},{3,2},{4,5},{5,4},{6,7},{7,6},{8,9},{9,8},{10,11... | collective-permute-start | bytes 786440 | tf_op jit(solution)/shard_map/ppermute | solution.py:251
  7.7 5.3 %copy-start.19 = (f32[64,1]{0,1:T(1,128)S(1)}, f32[64,1]{0,1:T(1,128)}, u32[]{:S(2)}) copy-start(f32[64,1]{0,1:T(1,128)} %param.7) | copy-start | bytes 772
  7.7 5.4 %copy-start.16 = (f32[64,1024]{1,0:T(8,128)S(1)}, f32[64,1024]{1,0:T(8,128)}, u32[]{:S(2)}) copy-start(f32[64,1024]{1,0:T(8,128)} %marginal_ref.1) | copy-start | bytes 786436
  7.7 5.4 %collective-permute-start.1 = (f32[64,1024]{1,0:T(8,128)}, f32[64,1024]{1,0:T(8,128)S(1)}, u32[]{:S(2)}, u32[]{:S(2)}) collective-permute-start(f32[64,1024]{1,0:T(8,128)} %get-tuple-element.26), channel_id=1, source_target_pairs={{1,2},{2,1},{3,4},{4,3},{5,6},{6,5},{7,8},{8,7},{9,10},{10,9},{11,... | collective-permute-start | bytes 786440 | tf_op jit(solution)/shard_map/ppermute | solution.py:250
  9.6 1.3 %copy-start.4 = (bf16[1024,1024]{1,0:T(8,128)(2,1)}, bf16[1024,1024]{1,0:T(8,128)(2,1)S(1)}, u32[]{:S(2)}) copy-start(bf16[1024,1024]{1,0:T(8,128)(2,1)S(1)} %get-tuple-element.30.refs_1_.high_ref) | copy-start | bytes 6291460
  10.9 1.4 %copy-start.6 = (bf16[1024,1024]{1,0:T(8,128)(2,1)}, bf16[1024,1024]{1,0:T(8,128)(2,1)S(1)}, u32[]{:S(2)}) copy-start(bf16[1024,1024]{1,0:T(8,128)(2,1)S(1)} %get-tuple-element.31.refs_2_.low_ref) | copy-start | bytes 6291460
  12.3 0.7 copy-start.17
  13.1 1.6 %copy-start.1 = (bf16[1024,1024]{1,0:T(8,128)(2,1)S(1)}, bf16[1024,1024]{1,0:T(8,128)(2,1)}, u32[]{:S(2)}) copy-start(bf16[1024,1024]{1,0:T(8,128)(2,1)} %copy-done) | copy-start | bytes 6291460
  14.7 0.9 %copy-start.18 = (f32[64,1024]{1,0:T(8,128)S(1)}, f32[64,1024]{1,0:T(8,128)}, u32[]{:S(2)}) copy-start(f32[64,1024]{1,0:T(8,128)} %copy-done.17) | copy-start | bytes 786436
  15.6 8.0 %copy-start.5 = (bf16[1024,1024]{1,0:T(8,128)(2,1)S(1)}, bf16[1024,1024]{1,0:T(8,128)(2,1)}, u32[]{:S(2)}) copy-start(bf16[1024,1024]{1,0:T(8,128)(2,1)} %copy-done.4) | copy-start | bytes 6291460
  15.6 8.0 %copy-start.7 = (bf16[1024,1024]{1,0:T(8,128)(2,1)S(1)}, bf16[1024,1024]{1,0:T(8,128)(2,1)}, u32[]{:S(2)}) copy-start(bf16[1024,1024]{1,0:T(8,128)(2,1)} %copy-done.6) | copy-start | bytes 6291460
  17.2 7.2 %collective-permute-start.2 = (f32[64,1024]{1,0:T(8,128)S(1)}, f32[64,1024]{1,0:T(8,128)S(1)}, u32[]{:S(2)}, u32[]{:S(2)}) collective-permute-start(f32[64,1024]{1,0:T(8,128)S(1)} %get-tuple-element.33), channel_id=1, source_target_pairs={{0,1},{1,0},{2,3},{3,2},{4,5},{5,4},{6,7},{7,6},{8,9},{9,8},{10,11... | collective-permute-start | bytes 786440 | tf_op jit(solution)/shard_map/ppermute | solution.py:251
  23.0 1.5 %collective-permute-start.3 = (f32[64,1024]{1,0:T(8,128)S(1)}, f32[64,1024]{1,0:T(8,128)S(1)}, u32[]{:S(2)}, u32[]{:S(2)}) collective-permute-start(f32[64,1024]{1,0:T(8,128)S(1)} %get-tuple-element.34), channel_id=1, source_target_pairs={{1,2},{2,1},{3,4},{4,3},{5,6},{6,5},{7,8},{8,7},{9,10},{10,9},{11,... | collective-permute-start | bytes 786440 | tf_op jit(solution)/shard_map/ppermute | solution.py:250
  23.7 1.6 %copy-start.2 = (bf16[1024,1024]{1,0:T(8,128)(2,1)S(1)}, bf16[1024,1024]{1,0:T(8,128)(2,1)}, u32[]{:S(2)}) copy-start(bf16[1024,1024]{1,0:T(8,128)(2,1)} %copy-done) | copy-start | bytes 6291460
  26.9 9.7 %collective-permute-start.4 = (f32[64,1024]{1,0:T(8,128)S(1)}, f32[64,1024]{1,0:T(8,128)S(1)}, u32[]{:S(2)}, u32[]{:S(2)}) collective-permute-start(f32[64,1024]{1,0:T(8,128)S(1)} %get-tuple-element.37), channel_id=1, source_target_pairs={{0,1},{1,0},{2,3},{3,2},{4,5},{5,4},{6,7},{7,6},{8,9},{9,8},{10,11... | collective-permute-start | bytes 786440 | tf_op jit(solution)/shard_map/ppermute | solution.py:251
  35.0 1.5 %collective-permute-start.5 = (f32[64,1024]{1,0:T(8,128)S(1)}, f32[64,1024]{1,0:T(8,128)S(1)}, u32[]{:S(2)}, u32[]{:S(2)}) collective-permute-start(f32[64,1024]{1,0:T(8,128)S(1)} %get-tuple-element.38), channel_id=1, source_target_pairs={{1,2},{2,1},{3,4},{4,3},{5,6},{6,5},{7,8},{8,7},{9,10},{10,9},{11,... | collective-permute-start | bytes 786440 | tf_op jit(solution)/shard_map/ppermute | solution.py:250
  38.1 10.6 %collective-permute-start.6 = (f32[64,1024]{1,0:T(8,128)S(1)}, f32[64,1024]{1,0:T(8,128)S(1)}, u32[]{:S(2)}, u32[]{:S(2)}) collective-permute-start(f32[64,1024]{1,0:T(8,128)S(1)} %get-tuple-element.41), channel_id=1, source_target_pairs={{0,1},{1,0},{2,3},{3,2},{4,5},{5,4},{6,7},{7,6},{8,9},{9,8},{10,11... | collective-permute-start | bytes 786440 | tf_op jit(solution)/shard_map/ppermute | solution.py:251
  47.2 1.5 %collective-permute-start.7 = (f32[64,1024]{1,0:T(8,128)S(1)}, f32[64,1024]{1,0:T(8,128)S(1)}, u32[]{:S(2)}, u32[]{:S(2)}) collective-permute-start(f32[64,1024]{1,0:T(8,128)S(1)} %get-tuple-element.42), channel_id=1, source_target_pairs={{1,2},{2,1},{3,4},{4,3},{5,6},{6,5},{7,8},{8,7},{9,10},{10,9},{11,... | collective-permute-start | bytes 786440 | tf_op jit(solution)/shard_map/ppermute | solution.py:250
  49.0 0.7 copy-start.12
  49.7 0.7 copy-start.14
  73.1 1.6 %copy-start.3 = (bf16[1024,1024]{1,0:T(8,128)(2,1)S(1)}, bf16[1024,1024]{1,0:T(8,128)(2,1)}, u32[]{:S(2)}) copy-start(bf16[1024,1024]{1,0:T(8,128)(2,1)} %copy-done) | copy-start | bytes 6291460
  74.7 0.9 %copy-start.13 = (f32[64,1024]{1,0:T(8,128)S(1)}, f32[64,1024]{1,0:T(8,128)}, u32[]{:S(2)}) copy-start(f32[64,1024]{1,0:T(8,128)} %copy-done.12) | copy-start | bytes 786436
  75.6 0.9 %copy-start.15 = (f32[64,1024]{1,0:T(8,128)S(1)}, f32[64,1024]{1,0:T(8,128)}, u32[]{:S(2)}) copy-start(f32[64,1024]{1,0:T(8,128)} %copy-done.14) | copy-start | bytes 786436

commit v2 on v1

v2 whole, which is shorter than its diff:
```python
import jax
import jax.numpy as jnp
from jax import lax
from jax.experimental import pallas as pl
from jax.experimental.pallas import tpu as pltpu
from jax.sharding import PartitionSpec as P


ITERS = 3
F32 = jnp.float32
BF16 = jnp.bfloat16
VMEM = pltpu.VMEM
MOMENT_ROWS = 8


def tile_of(size):
    return 256 if size % 256 == 0 else size


def is_odd():
    return lax.rem(lax.axis_index("snp"), 2) == 1


def halves(x):
    high = x.astype(BF16)
    return high, (x - high.astype(F32)).astype(BF16)


def dot(left, right):
    return jnp.dot(left, right, preferred_element_type=F32)


def product(both, right_high, right_low):
    rows = both.shape[0] // 2
    main = dot(both, right_high)
    return main[:rows] + main[rows:] + dot(both[:rows], right_low)


def stacked(field):
    return jnp.concatenate(halves(field), axis=0)


def coupling(both, high, low, store):
    size = high.shape[0]
    tile = tile_of(size)
    for start in range(0, size, tile):
        rows, cols = pl.ds(start, size - start), pl.ds(start, tile)
        store(start, product(both[:, start:], high[rows, cols], low[rows, cols]))


def forward(both, high, low, store):
    size = high.shape[0]
    tile = tile_of(size)
    for start in range(0, size, tile):
        rows, cols = pl.ds(0, start + tile), pl.ds(start, tile)
        store(start, product(both[:, : start + tile], high[rows, cols], low[rows, cols]))


def sends(odd, field, high, low, pair_ref, cross_ref):
    tile = tile_of(field.shape[1])

    def store(start, part):
        cols = pl.ds(start, tile)
        own = field[:, start : start + tile]
        pair_ref[:, cols] = jnp.where(odd, own, part)
        cross_ref[:, cols] = jnp.where(odd, part, own)

    coupling(stacked(field), high, low, store)


def begin_kernel(next_ref, start_ref, high_ref, low_ref, pair_ref, cross_ref, raw, field, total, sems, field_sem):
    size = raw.shape[0]
    tile = tile_of(size)
    odd = is_odd()
    starts = list(range(0, size, tile))
    field_copy = pltpu.make_async_copy(start_ref, field, field_sem)
    field_copy.start()
    copies = []
    for index, start in enumerate(starts):
        part = (pl.ds(start, tile), pl.ds(0, start + tile))
        copies.append(pltpu.make_async_copy(next_ref.at[part], raw.at[part], sems.at[index]))
        copies[-1].start()
    field_copy.wait()
    for index, start in enumerate(starts):
        part = (pl.ds(start, tile), pl.ds(0, start + tile))
        copies[index].wait()
        high, low = halves(raw[part])
        high_ref[part] = high
        low_ref[part] = low
        done = product(stacked(field[:, pl.ds(start, tile)]), high, low)
        if start:
            done_before = total[:, pl.ds(0, start)] + done[:, :start]
            total[:, pl.ds(0, start)] = done_before
        total[:, pl.ds(start, tile)] = done[:, start:]
    own = field[...]
    pair_ref[...] = jnp.where(odd, own, total[...])
    cross_ref[...] = jnp.where(odd, total[...], own)


def flip_kernel(high_in, low_in, high_ref, low_ref):
    size = high_in.shape[0]
    tile = tile_of(size)
    for row in range(0, size, tile):
        for col in range(0, row + tile, tile):
            source, target = (pl.ds(row, tile), pl.ds(col, tile)), (pl.ds(col, tile), pl.ds(row, tile))
            high_ref[target] = jnp.transpose(high_in[source])
            low_ref[target] = jnp.transpose(low_in[source])


def local_kernel(
    local_ref, field_ref, marginal_ref, shrinkage_ref, pair_in, high_ref, low_ref, rest_ref, shift_ref, pair_ref
):
    del pair_in, pair_ref
    size = local_ref.shape[0]
    tile = tile_of(size)
    both = stacked(field_ref[...])
    total = None
    for start in range(0, size, tile):
        rows = pl.ds(start, tile)
        row = lax.broadcasted_iota(jnp.int32, (tile, size), 0) + start
        col = lax.broadcasted_iota(jnp.int32, (tile, size), 1)
        high, low = halves(local_ref[rows, :] - jnp.where(row == col, 1.0, 0.0))
        high_ref[rows, :] = high
        low_ref[rows, :] = low
        part = product(both[:, start : start + tile], high, low)
        total = part if total is None else total + part
    traits = field_ref.shape[0]
    here = lax.broadcasted_iota(jnp.int32, (traits, traits), 0) == lax.broadcasted_iota(jnp.int32, (traits, traits), 1)
    ridge = jnp.sum(jnp.where(here, shrinkage_ref[...], 0.0), axis=1, keepdims=True)
    shift = 1.0 + ridge
    shift_ref[...] = jnp.broadcast_to(shift, shift_ref.shape)
    rest_ref[...] = marginal_ref[...] - shift * field_ref[...] - total


def moment(left, right):
    return jnp.sum(left * right, axis=1, keepdims=True)


def own_kernel(before_ref, field_ref, high_ref, low_ref, pair_in, own_ref, moments_ref, pair_ref):
    del pair_in, pair_ref
    field = field_ref[...]
    own_ref[...] = product(stacked(field), high_ref[...], low_ref[...])
    lane = lax.broadcasted_iota(jnp.int32, moments_ref.shape, 1)
    cross = 0.0 if before_ref is None else moment(before_ref[...], field)
    moments_ref[...] = jnp.where(lane == 0, moment(field, field), jnp.where(lane == 1, cross, 0.0))


def received(odd, pair_ref, cross_ref):
    upper = jnp.where(odd, cross_ref[...], pair_ref[...])
    lower = jnp.where(odd, pair_ref[...], cross_ref[...])
    return upper, lower


def first_kernel(
    rest_ref, got_pair_ref, got_cross_ref, high_in, low_in, high_up, low_up, field_ref, pair_ref, cross_ref,
):
    odd = is_odd()
    tile = tile_of(rest_ref.shape[1])
    upper, lower = received(odd, got_pair_ref, got_cross_ref)
    base = rest_ref[...] - lower

    def store(start, part):
        field_ref[:, pl.ds(start, tile)] = base[:, start : start + tile] - part

    forward(stacked(upper), high_up, low_up, store)
    sends(odd, field_ref[...], high_in, low_in, pair_ref, cross_ref)


def step_kernel(
    own_ref, got_pair_ref, got_cross_ref, high_in, low_in, high_up, low_up, field_ref, pair_ref,
    cross_ref,
):
    odd = is_odd()
    tile = tile_of(own_ref.shape[1])
    upper, lower = received(odd, got_pair_ref, got_cross_ref)
    base = own_ref[...] + lower

    def store(start, part):
        field_ref[:, pl.ds(start, tile)] = base[:, start : start + tile] + part

    forward(stacked(upper), high_up, low_up, store)
    sends(odd, field_ref[...], high_in, low_in, pair_ref, cross_ref)


def reduce_kernel(field_ref, own_ref, got_pair_ref, got_cross_ref, one_ref, two_ref, three_ref, out_ref):
    odd = is_odd()
    _, lower = received(odd, got_pair_ref, got_cross_ref)
    traits = field_ref.shape[0]
    last = moment(field_ref[...], own_ref[...] + 2.0 * lower)
    lane = lax.broadcasted_iota(jnp.int32, (traits, 128), 1)
    parts = (
        one_ref[:, 0:1],
        two_ref[:, 1:2],
        two_ref[:, 0:1],
        three_ref[:, 1:2],
        three_ref[:, 0:1],
        last,
    )
    table = jnp.zeros((traits, 128), F32)
    for index, part in enumerate(parts):
        table = jnp.where(lane == index, part, table)
    lanes = out_ref.shape[2]
    if lanes > traits:
        table = jnp.concatenate([table, jnp.zeros((lanes - traits, 128), F32)], axis=0)
    rows = jnp.transpose(table)[:MOMENT_ROWS]
    for index in range(out_ref.shape[0]):
        out_ref[index] = rows


def coefficients(moments, shift):
    def inner(left, right):
        total = None
        for i, a in enumerate(left):
            for j, b in enumerate(right):
                term = (a * b) * moments[i + j]
                total = term if total is None else total + term
        return total

    one = jnp.ones_like(shift)
    zero = jnp.zeros_like(shift)
    residual, direction, gain = [one], [one], []
    norm_now = moments[0]
    for step in range(ITERS):
        image = [shift * a + b for a, b in zip(direction + [zero], [zero] + direction)]
        alpha = norm_now / inner(direction, image)
        gain = [a + alpha * b for a, b in zip(gain + [zero], direction)]
        residual = [a - alpha * b for a, b in zip(residual + [zero], image)]
        if step + 1 < ITERS:
            norm_next = inner(residual, residual)
            ratio = norm_next / norm_now
            direction = [a + ratio * b for a, b in zip(residual, direction + [zero])]
            norm_now = norm_next
    return gain, residual


def final_kernel(
    table_ref, shift_ref, start_ref, zero_ref, one_ref, two_ref, own_ref, got_pair_ref, got_cross_ref,
    high_up, low_up, solution_ref, residual_ref,
):
    odd = is_odd()
    traits, size = own_ref.shape
    tile = tile_of(size)
    upper, lower = received(odd, got_pair_ref, got_cross_ref)
    sums = jnp.sum(table_ref[...], axis=0)
    square = jnp.concatenate([sums, jnp.zeros((sums.shape[1] - MOMENT_ROWS, sums.shape[1]), F32)], axis=0)
    columns = jnp.transpose(square)[:traits]
    moments = [columns[:, i : i + 1] for i in range(2 * ITERS)]
    gain, residual = coefficients(moments, shift_ref[:, 0:1])
    zero, one, two = zero_ref[...], one_ref[...], two_ref[...]
    solution_ref[...] = start_ref[...] + gain[0] * zero + gain[1] * one + gain[2] * two
    base = residual[0] * zero + residual[1] * one + residual[2] * two + residual[3] * (own_ref[...] + lower)

    def store(start, part):
        residual_ref[:, pl.ds(start, tile)] = base[:, start : start + tile] + residual[3] * part

    forward(stacked(upper), high_up, low_up, store)


def call(kernel, out, *args, spaces=None, scratch=(), limit=12, aliases=None, keep=True, flops=0):
    spaces = spaces or {}
    places = [spaces.get(i, VMEM) for i in range(len(args))]
    args = [
        arg if place is pltpu.SMEM else pltpu.with_memory_space_constraint(arg, place)
        for arg, place in zip(args, places)
    ]
    make = VMEM if keep else jax.ShapeDtypeStruct
    return pl.pallas_call(
        kernel,
        out_shape=[make(shape, dtype) for shape, dtype in out],
        in_specs=[pl.BlockSpec(memory_space=place) for place in places],
        out_specs=[pl.BlockSpec(memory_space=VMEM) for _ in out],
        scratch_shapes=scratch,
        input_output_aliases=aliases or {},
        cost_estimate=pl.CostEstimate(flops=flops, bytes_accessed=0, transcendentals=0) if flops else None,
        compiler_params=pltpu.CompilerParams(vmem_limit_bytes=limit * 1024 * 1024),
    )(*args)


def on_device(local_block, next_block, shrinkage, marginal, warm_start):
    count = lax.axis_size("snp")
    traits, size = warm_start.shape
    field = ((traits, size), F32)
    matrix = ((size, size), BF16)
    steps = size // tile_of(size)
    work = 6 * traits * size * size
    on_chip = [(i, i ^ 1) for i in range(count) if i ^ 1 < count]
    off_chip = [(i, ((i - 1) ^ 1) + 1) for i in range(1, count) if ((i - 1) ^ 1) + 1 < count]

    def swap_off(cross):
        return lax.ppermute(cross, "snp", off_chip)

    def swap_on(pair):
        return lax.ppermute(pair, "snp", on_chip)

    high_n, low_n, pair, cross = call(
        begin_kernel,
        [matrix, matrix, field, field],
        next_block, warm_start,
        spaces={0: pltpu.HBM, 1: pltpu.HBM},
        scratch=(
            pltpu.VMEM((size, size), F32),
            pltpu.VMEM((traits, size), F32),
            pltpu.VMEM((traits, size), F32),
            pltpu.SemaphoreType.DMA((steps,)),
            pltpu.SemaphoreType.DMA,
        ),
    )
    got_cross = swap_off(cross)
    table = ((traits, 128), F32)
    high_l, low_l, rest, shift, pair = call(
        local_kernel,
        [matrix, matrix, field, table, field],
        local_block, warm_start, marginal, shrinkage.reshape(1, traits), pair,
        aliases={4: 4},
        flops=work,
    )
    got_pair = swap_on(pair)
    up = call(flip_kernel, [matrix, matrix], high_n, low_n, flops=work)
    zero, pair, cross = call(
        first_kernel,
        [field, field, field],
        rest, got_pair, got_cross, high_n, low_n, *up,
    )
    fields, tables = [zero], []
    for step in range(ITERS):
        before = fields[-2:-1]
        kernel = own_kernel if before else lambda *refs: own_kernel(None, *refs)
        got_cross = swap_off(cross)
        own, part, pair = call(
            kernel,
            [field, table, field],
            *before, fields[-1], high_l, low_l, pair,
            aliases={3 + len(before): 2},
            flops=work,
        )
        got_pair = swap_on(pair)
        tables.append(part)
        if step + 1 < ITERS:
            after, pair, cross = call(
                step_kernel,
                [field, field, field],
                own, got_pair, got_cross, high_n, low_n, *up,
            )
            fields.append(after)
    lanes = -(-traits // 128) * 128
    (moments,) = call(
        reduce_kernel,
        [((count, MOMENT_ROWS, lanes), F32)],
        fields[-1], own, got_pair, got_cross, *tables,
    )
    moments = lax.all_to_all(moments, "snp", 0, 0)
    return tuple(
        call(
            final_kernel,
            [field, field],
            moments, shift, warm_start, *fields, own, got_pair, got_cross, *up,
            keep=False,
        )
    )


def solution(mesh):
    return jax.shard_map(
        on_device,
        mesh=mesh,
        in_specs=(
            P(("parts", "snp"), None),
            P(("parts", "snp"), None),
            P(),
            P(None, ("parts", "snp")),
            P(None, ("parts", "snp")),
        ),
        out_specs=(P(None, ("parts", "snp")), P(None, ("parts", "snp"))),
        check_vma=False,
    )
```

time: 78.8 us -> 61.5 us (0.78)
  local copies, waits for them, and re-layouts: 16.9 us -> 0.96 us
  starting transfers between devices: 26.3 us -> 23 us
  waiting for transfers between devices: 0.02 us -> 3.19 us
  Pallas kernels: 12.2 us -> 11.4 us
    unnamed x43 -> x8, local copies, waits for them, and re-layouts: 16.4 us -> 0.96 us
    ppermute x8, starting transfers between devices: 26.3 us -> 23 us  [the longest x4 20.3 us: swap_on(): return lax.ppermute(pair, 'snp', on_chip)]
    ppermute x8, waiting for transfers between devices: 0.02 us -> 3.19 us  [the longest x4 3.18 us: swap_on(): return lax.ppermute(pair, 'snp', on_chip)]
    pallas_call x10 -> x11, Pallas kernels: 12.2 us -> 11.4 us  [call(): pl.pallas_call(kernel, out_shape=[make(shape, dtype) for shape, dtype in...]
  transfers between devices with their start and end apart: 8 -> 8, of which waited for: 0 -> 4; matrix products, arithmetic and copies ran while one was open for 0% -> 0% of each run, Pallas kernels for 4% -> 6%
where the time goes in v2:
time: 61.5 us; the launch traced here: 61.2 us
  starting transfers between devices  23 us (37%)
  blocking collectives  21.8 us (35%)
  Pallas kernels  11.4 us (19%)
  waiting for transfers between devices  3.19 us (5%)
  local copies, waits for them, and re-layouts  0.96 us (2%)
  between operations  0.79 us (1%)
    all_to_all x1, blocking collectives, on_device(): moments = lax.all_to_all(moments, 'snp', 0, 0)  21.8 us
    ppermute x4, starting transfers between devices, swap_on(): return lax.ppermute(pair, 'snp', on_chip)  20.3 us
    pallas_call x11, Pallas kernels, call(): pl.pallas_call(kernel, out_shape=[make(shape, dtype) for shape, dtype in...  11.4 us
    ppermute x4, waiting for transfers between devices, swap_on(): return lax.ppermute(pair, 'snp', on_chip)  3.18 us
    ppermute x4, starting transfers between devices, swap_off(): return lax.ppermute(cross, 'snp', off_chip)  2.7 us
  transfers between devices with their start and end apart: 8, of which 4 were waited for; matrix products, arithmetic and copies ran while one was open for 0% of the time, Pallas kernels for 6%

profile of v2, /device:TPU:0, one launch (start us, length us, event | category | flops | bytes accessed | tf_op | source)
XLA Modules:
  0.0 61.2 jit_solution(2310626206752341528)
XLA Ops:
  0.6 0.0 copy-start.1
  0.6 0.0 copy-start.3
  0.7 2.5 %shard_map.68 = (bf16[1024,1024]{1,0:T(8,128)(2,1)S(1)}, bf16[1024,1024]{1,0:T(8,128)(2,1)S(1)}, f32[64,1024]{1,0:T(8,128)S(1)}, f32[64,1024]{1,0:T(8,128)S(1)}) custom-call(f32[1024,1024]{1,0:T(8,128)} %next_ref.1, f32[64,1024]{1,0:T(8,128)} %start_ref.3), custom_call_target="tpu_custom_call" | custom-call | tf_op jit(solution)/shard_map/pallas_call | solution.py:267
  3.1 0.7 %collective-permute-start.1 = (f32[64,1024]{1,0:T(8,128)S(1)}, f32[64,1024]{1,0:T(8,128)S(1)}, u32[]{:S(2)}, u32[]{:S(2)}) collective-permute-start(f32[64,1024]{1,0:T(8,128)S(1)} %get-tuple-element.34), channel_id=1, source_target_pairs={{1,2},{2,1},{3,4},{4,3},{5,6},{6,5},{7,8},{8,7},{9,10},{10,9},{11,... | collective-permute-start | bytes 786440 | tf_op jit(solution)/shard_map/ppermute | solution.py:290
  3.8 0.0 copy-start.2
  3.9 0.9 %copy-done.2 = f32[64,1024]{1,0:T(8,128)S(1)} copy-done((f32[64,1024]{1,0:T(8,128)S(1)}, f32[64,1024]{1,0:T(8,128)}, u32[]{:S(2)}) %copy-start.2) | copy-done | bytes 262168
  4.8 1.1 %shard_map.69 = (bf16[1024,1024]{1,0:T(8,128)(2,1)S(1)}, bf16[1024,1024]{1,0:T(8,128)(2,1)S(1)}, f32[64,1024]{1,0:T(8,128)S(1)}, f32[64,128]{1,0:T(8,128)S(1)}, f32[64,1024]{1,0:T(8,128)S(1)}) custom-call(f32[1024,1024]{1,0:T(8,128)S(1)} %copy-done, f32[64,1024]{1,0:T(8,128)S(1)} %copy-done.1, ...), custom_call_target="tpu_custom_call", output_to_operand_aliasing={{4}: (4, {})} | custom-call | flops 402653184 | tf_op jit(solution)/shard_map/pallas_call | solution.py:267
  5.9 4.4 %collective-permute-start = (f32[64,1024]{1,0:T(8,128)S(1)}, f32[64,1024]{1,0:T(8,128)S(1)}, u32[]{:S(2)}, u32[]{:S(2)}) collective-permute-start(f32[64,1024]{1,0:T(8,128)S(1)} %get-tuple-element.33), channel_id=1, source_target_pairs={{0,1},{1,0},{2,3},{3,2},{4,5},{5,4},{6,7},{7,6},{8,9},{9,8},{10,11... | collective-permute-start | bytes 786440 | tf_op jit(solution)/shard_map/ppermute | solution.py:293
  10.3 0.8 %shard_map.70 = (bf16[1024,1024]{1,0:T(8,128)(2,1)S(1)}, bf16[1024,1024]{1,0:T(8,128)(2,1)S(1)}) custom-call(bf16[1024,1024]{1,0:T(8,128)(2,1)S(1)} %get-tuple-element.35.high_in, bf16[1024,1024]{1,0:T(8,128)(2,1)S(1)} %get-tuple-element.36.low_in), custom_call_target="tpu_custom_call" | custom-call | flops 402653184 | tf_op jit(solution)/shard_map/pallas_call | solution.py:267
  11.0 0.0 collective-permute-done.1.got_cross_ref
  11.0 0.4 collective-permute-done.got_pair_ref
  11.4 1.1 %shard_map.71 = (f32[64,1024]{1,0:T(8,128)S(1)}, f32[64,1024]{1,0:T(8,128)S(1)}, f32[64,1024]{1,0:T(8,128)S(1)}) custom-call(f32[64,1024]{1,0:T(8,128)S(1)} %get-tuple-element.32.rest_ref, f32[64,1024]{1,0:T(8,128)S(1)} %collective-permute-done.got_pair_ref, f32[64,1024]{1,0:T(8,128)S(1)} %collective-permute-done.1.got_cross_ref, ...), custom_call_target="tpu_custom_call" | custom-call | tf_op jit(solution)/shard_map/pallas_call | solution.py:267
  12.5 0.7 %collective-permute-start.3 = (f32[64,1024]{1,0:T(8,128)S(1)}, f32[64,1024]{1,0:T(8,128)S(1)}, u32[]{:S(2)}, u32[]{:S(2)}) collective-permute-start(f32[64,1024]{1,0:T(8,128)S(1)} %get-tuple-element.45), channel_id=1, source_target_pairs={{1,2},{2,1},{3,4},{4,3},{5,6},{6,5},{7,8},{8,7},{9,10},{10,9},{11,... | collective-permute-start | bytes 786440 | tf_op jit(solution)/shard_map/ppermute | solution.py:290
  13.2 0.8 %shard_map.72 = (f32[64,1024]{1,0:T(8,128)S(1)}, f32[64,128]{1,0:T(8,128)S(1)}, f32[64,1024]{1,0:T(8,128)S(1)}) custom-call(f32[64,1024]{1,0:T(8,128)S(1)} %get-tuple-element.39.refs_0_.before_ref.zero_ref, bf16[1024,1024]{1,0:T(8,128)(2,1)S(1)} %get-tuple-element.40.refs_1_.high_ref, ...), custom_call_target="tpu_custom_call", output_to_operand_aliasing={{2}: (3, {})} | custom-call | flops 402653184 | tf_op jit(solution)/shard_map/pallas_call | solution.py:267
  13.9 6.6 %collective-permute-start.2 = (f32[64,1024]{1,0:T(8,128)S(1)}, f32[64,1024]{1,0:T(8,128)S(1)}, u32[]{:S(2)}, u32[]{:S(2)}) collective-permute-start(f32[64,1024]{1,0:T(8,128)S(1)} %get-tuple-element.44), channel_id=1, source_target_pairs={{0,1},{1,0},{2,3},{3,2},{4,5},{5,4},{6,7},{7,6},{8,9},{9,8},{10,11... | collective-permute-start | bytes 786440 | tf_op jit(solution)/shard_map/ppermute | solution.py:293
  20.6 0.0 collective-permute-done.3.got_cross_ref
  20.6 1.2 %collective-permute-done.2.got_pair_ref = f32[64,1024]{1,0:T(8,128)S(1)} collective-permute-done((f32[64,1024]{1,0:T(8,128)S(1)}, f32[64,1024]{1,0:T(8,128)S(1)}, u32[]{:S(2)}, u32[]{:S(2)}) %collective-permute-start.2) | collective-permute-done | bytes 262176 | tf_op jit(solution)/shard_map/ppermute | solution.py:293
  21.7 1.0 %shard_map.73 = (f32[64,1024]{1,0:T(8,128)S(1)}, f32[64,1024]{1,0:T(8,128)S(1)}, f32[64,1024]{1,0:T(8,128)S(1)}) custom-call(f32[64,1024]{1,0:T(8,128)S(1)} %get-tuple-element.43.own_ref, f32[64,1024]{1,0:T(8,128)S(1)} %collective-permute-done.2.got_pair_ref, f32[64,1024]{1,0:T(8,128)S(1)} %collective-permute-done.3.got_cross_ref, ...), custom_call_target="tpu_custom_call" | custom-call | tf_op jit(solution)/shard_map/pallas_call | solution.py:267
  22.8 0.7 %collective-permute-start.5 = (f32[64,1024]{1,0:T(8,128)S(1)}, f32[64,1024]{1,0:T(8,128)S(1)}, u32[]{:S(2)}, u32[]{:S(2)}) collective-permute-start(f32[64,1024]{1,0:T(8,128)S(1)} %get-tuple-element.50), channel_id=1, source_target_pairs={{1,2},{2,1},{3,4},{4,3},{5,6},{6,5},{7,8},{8,7},{9,10},{10,9},{11,... | collective-permute-start | bytes 786440 | tf_op jit(solution)/shard_map/ppermute | solution.py:290
  23.5 0.8 %shard_map.74 = (f32[64,1024]{1,0:T(8,128)S(1)}, f32[64,128]{1,0:T(8,128)S(1)}, f32[64,1024]{1,0:T(8,128)S(1)}) custom-call(f32[64,1024]{1,0:T(8,128)S(1)} %get-tuple-element.39.refs_0_.before_ref.zero_ref, f32[64,1024]{1,0:T(8,128)S(1)} %get-tuple-element.46.field_ref.before_ref.one_ref, ...), custom_call_target="tpu_custom_call", output_to_operand_aliasing={{2}: (4, {})} | custom-call | flops 402653184 | tf_op jit(solution)/shard_map/pallas_call | solution.py:267
  24.3 7.0 %collective-permute-start.4 = (f32[64,1024]{1,0:T(8,128)S(1)}, f32[64,1024]{1,0:T(8,128)S(1)}, u32[]{:S(2)}, u32[]{:S(2)}) collective-permute-start(f32[64,1024]{1,0:T(8,128)S(1)} %get-tuple-element.49), channel_id=1, source_target_pairs={{0,1},{1,0},{2,3},{3,2},{4,5},{5,4},{6,7},{7,6},{8,9},{9,8},{10,11... | collective-permute-start | bytes 786440 | tf_op jit(solution)/shard_map/ppermute | solution.py:293
  31.2 0.0 collective-permute-done.5.got_cross_ref
  31.2 1.2 %collective-permute-done.4.got_pair_ref = f32[64,1024]{1,0:T(8,128)S(1)} collective-permute-done((f32[64,1024]{1,0:T(8,128)S(1)}, f32[64,1024]{1,0:T(8,128)S(1)}, u32[]{:S(2)}, u32[]{:S(2)}) %collective-permute-start.4) | collective-permute-done | bytes 262176 | tf_op jit(solution)/shard_map/ppermute | solution.py:293
  32.4 1.0 %shard_map.75 = (f32[64,1024]{1,0:T(8,128)S(1)}, f32[64,1024]{1,0:T(8,128)S(1)}, f32[64,1024]{1,0:T(8,128)S(1)}) custom-call(f32[64,1024]{1,0:T(8,128)S(1)} %get-tuple-element.48.own_ref, f32[64,1024]{1,0:T(8,128)S(1)} %collective-permute-done.4.got_pair_ref, f32[64,1024]{1,0:T(8,128)S(1)} %collective-permute-done.5.got_cross_ref, ...), custom_call_target="tpu_custom_call" | custom-call | tf_op jit(solution)/shard_map/pallas_call | solution.py:267
  33.4 0.8 %shard_map.76 = (f32[64,1024]{1,0:T(8,128)S(1)}, f32[64,128]{1,0:T(8,128)S(1)}, f32[64,1024]{1,0:T(8,128)S(1)}) custom-call(f32[64,1024]{1,0:T(8,128)S(1)} %get-tuple-element.46.field_ref.before_ref.one_ref, f32[64,1024]{1,0:T(8,128)S(1)} %get-tuple-element.51.field_ref.two_ref, ...), custom_call_target="tpu_custom_call", output_to_operand_aliasing={{2}: (4, {})} | custom-call | flops 402653184 | tf_op jit(solution)/shard_map/pallas_call | solution.py:267
  34.2 2.3 %collective-permute-start.6 = (f32[64,1024]{1,0:T(8,128)S(1)}, f32[64,1024]{1,0:T(8,128)S(1)}, u32[]{:S(2)}, u32[]{:S(2)}) collective-permute-start(f32[64,1024]{1,0:T(8,128)S(1)} %get-tuple-element.54), channel_id=1, source_target_pairs={{0,1},{1,0},{2,3},{3,2},{4,5},{5,4},{6,7},{7,6},{8,9},{9,8},{10,11... | collective-permute-start | bytes 786440 | tf_op jit(solution)/shard_map/ppermute | solution.py:293
  36.6 0.7 %collective-permute-start.7 = (f32[64,1024]{1,0:T(8,128)S(1)}, f32[64,1024]{1,0:T(8,128)S(1)}, u32[]{:S(2)}, u32[]{:S(2)}) collective-permute-start(f32[64,1024]{1,0:T(8,128)S(1)} %get-tuple-element.55), channel_id=1, source_target_pairs={{1,2},{2,1},{3,4},{4,3},{5,6},{6,5},{7,8},{8,7},{9,10},{10,9},{11,... | collective-permute-start | bytes 786440 | tf_op jit(solution)/shard_map/ppermute | solution.py:290
  37.3 0.5 collective-permute-done.6.got_pair_ref
  37.8 0.0 collective-permute-done.7.got_cross_ref
  37.8 0.2 shard_map.77
  38.0 21.8 %all_to_all.5.table_ref = f32[16,8,128]{2,1,0:T(8,128)S(1)} all-to-all(f32[16,8,128]{2,1,0:T(8,128)S(1)} %shard_map.77), channel_id=1, replica_groups=mesh['parts'=2,'snp'=16] {'snp'}, dimensions={0} | all-to-all | bytes 131072 | tf_op jit(solution)/shard_map/all_to_all | solution.py:351
  59.8 1.4 %shard_map.78 = (f32[64,1024]{1,0:T(8,128)}, f32[64,1024]{1,0:T(8,128)}) custom-call(f32[16,8,128]{2,1,0:T(8,128)S(1)} %all_to_all.5.table_ref, f32[64,128]{1,0:T(8,128)S(1)} %get-tuple-element.59.shift_ref, f32[64,1024]{1,0:T(8,128)S(1)} %copy-done.1, f32[64,1024]{1,0:T(8,128)S(1)} %get-tuple-element.39.refs_0_.before_ref.zero_ref, ...), custom_call_target="tpu_custom_call" | custom-call | tf_op jit(solution)/shard_map/pallas_call | solution.py:267
  (4 shorter events, 0.0 us)
Async XLA Ops:
  0.6 3.2 %copy-start.1 = (f32[64,1024]{1,0:T(8,128)S(1)}, f32[64,1024]{1,0:T(8,128)}, u32[]{:S(2)}) copy-start(f32[64,1024]{1,0:T(8,128)} %start_ref.3) | copy-start | bytes 786436
  0.6 3.2 %copy-start.3 = (f32[64,1]{0,1:T(1,128)S(1)}, f32[64,1]{0,1:T(1,128)}, u32[]{:S(2)}) copy-start(f32[64,1]{0,1:T(1,128)} %param.7) | copy-start | bytes 772
  0.7 3.2 %copy-start = (f32[1024,1024]{1,0:T(8,128)S(1)}, f32[1024,1024]{1,0:T(8,128)}, u32[]{:S(2)}) copy-start(f32[1024,1024]{1,0:T(8,128)} %local_ref.1) | copy-start | bytes 12582916
  3.1 7.9 %collective-permute-start.1 = (f32[64,1024]{1,0:T(8,128)S(1)}, f32[64,1024]{1,0:T(8,128)S(1)}, u32[]{:S(2)}, u32[]{:S(2)}) collective-permute-start(f32[64,1024]{1,0:T(8,128)S(1)} %get-tuple-element.34), channel_id=1, source_target_pairs={{1,2},{2,1},{3,4},{4,3},{5,6},{6,5},{7,8},{8,7},{9,10},{10,9},{11,... | collective-permute-start | bytes 786440 | tf_op jit(solution)/shard_map/ppermute | solution.py:290
  3.8 1.0 %copy-start.2 = (f32[64,1024]{1,0:T(8,128)S(1)}, f32[64,1024]{1,0:T(8,128)}, u32[]{:S(2)}) copy-start(f32[64,1024]{1,0:T(8,128)} %marginal_ref.1) | copy-start | bytes 786436
  5.9 5.6 %collective-permute-start = (f32[64,1024]{1,0:T(8,128)S(1)}, f32[64,1024]{1,0:T(8,128)S(1)}, u32[]{:S(2)}, u32[]{:S(2)}) collective-permute-start(f32[64,1024]{1,0:T(8,128)S(1)} %get-tuple-element.33), channel_id=1, source_target_pairs={{0,1},{1,0},{2,3},{3,2},{4,5},{5,4},{6,7},{7,6},{8,9},{9,8},{10,11... | collective-permute-start | bytes 786440 | tf_op jit(solution)/shard_map/ppermute | solution.py:293
  12.5 8.1 %collective-permute-start.3 = (f32[64,1024]{1,0:T(8,128)S(1)}, f32[64,1024]{1,0:T(8,128)S(1)}, u32[]{:S(2)}, u32[]{:S(2)}) collective-permute-start(f32[64,1024]{1,0:T(8,128)S(1)} %get-tuple-element.45), channel_id=1, source_target_pairs={{1,2},{2,1},{3,4},{4,3},{5,6},{6,5},{7,8},{8,7},{9,10},{10,9},{11,... | collective-permute-start | bytes 786440 | tf_op jit(solution)/shard_map/ppermute | solution.py:290
  13.9 7.8 %collective-permute-start.2 = (f32[64,1024]{1,0:T(8,128)S(1)}, f32[64,1024]{1,0:T(8,128)S(1)}, u32[]{:S(2)}, u32[]{:S(2)}) collective-permute-start(f32[64,1024]{1,0:T(8,128)S(1)} %get-tuple-element.44), channel_id=1, source_target_pairs={{0,1},{1,0},{2,3},{3,2},{4,5},{5,4},{6,7},{7,6},{8,9},{9,8},{10,11... | collective-permute-start | bytes 786440 | tf_op jit(solution)/shard_map/ppermute | solution.py:293
  22.8 8.4 %collective-permute-start.5 = (f32[64,1024]{1,0:T(8,128)S(1)}, f32[64,1024]{1,0:T(8,128)S(1)}, u32[]{:S(2)}, u32[]{:S(2)}) collective-permute-start(f32[64,1024]{1,0:T(8,128)S(1)} %get-tuple-element.50), channel_id=1, source_target_pairs={{1,2},{2,1},{3,4},{4,3},{5,6},{6,5},{7,8},{8,7},{9,10},{10,9},{11,... | collective-permute-start | bytes 786440 | tf_op jit(solution)/shard_map/ppermute | solution.py:290
  24.3 8.1 %collective-permute-start.4 = (f32[64,1024]{1,0:T(8,128)S(1)}, f32[64,1024]{1,0:T(8,128)S(1)}, u32[]{:S(2)}, u32[]{:S(2)}) collective-permute-start(f32[64,1024]{1,0:T(8,128)S(1)} %get-tuple-element.49), channel_id=1, source_target_pairs={{0,1},{1,0},{2,3},{3,2},{4,5},{5,4},{6,7},{7,6},{8,9},{9,8},{10,11... | collective-permute-start | bytes 786440 | tf_op jit(solution)/shard_map/ppermute | solution.py:293
  34.2 3.5 %collective-permute-start.6 = (f32[64,1024]{1,0:T(8,128)S(1)}, f32[64,1024]{1,0:T(8,128)S(1)}, u32[]{:S(2)}, u32[]{:S(2)}) collective-permute-start(f32[64,1024]{1,0:T(8,128)S(1)} %get-tuple-element.54), channel_id=1, source_target_pairs={{0,1},{1,0},{2,3},{3,2},{4,5},{5,4},{6,7},{7,6},{8,9},{9,8},{10,11... | collective-permute-start | bytes 786440 | tf_op jit(solution)/shard_map/ppermute | solution.py:293
  36.6 1.2 %collective-permute-start.7 = (f32[64,1024]{1,0:T(8,128)S(1)}, f32[64,1024]{1,0:T(8,128)S(1)}, u32[]{:S(2)}, u32[]{:S(2)}) collective-permute-start(f32[64,1024]{1,0:T(8,128)S(1)} %get-tuple-element.55), channel_id=1, source_target_pairs={{1,2},{2,1},{3,4},{4,3},{5,6},{6,5},{7,8},{8,7},{9,10},{10,9},{11,... | collective-permute-start | bytes 786440 | tf_op jit(solution)/shard_map/ppermute | solution.py:290

commit v3 on v2

v3 whole, which is shorter than its diff:
```python
import functools

import jax
import jax.numpy as jnp
from jax import lax
from jax.experimental import pallas as pl
from jax.experimental.pallas import tpu as pltpu
from jax.sharding import PartitionSpec as P


ITERS = 3
F32 = jnp.float32
BF16 = jnp.bfloat16
VMEM = pltpu.VMEM
MOMENT_ROWS = 8


def tile_of(size):
    return 256 if size % 256 == 0 else size


def is_odd():
    return lax.rem(lax.axis_index("snp"), 2) == 1


def halves(x):
    high = x.astype(BF16)
    return high, (x - high.astype(F32)).astype(BF16)


def dot(left, right):
    return jnp.dot(left, right, preferred_element_type=F32)


def product(both, right_high, right_low):
    rows = both.shape[0] // 2
    main = dot(both, right_high)
    return main[:rows] + main[rows:] + dot(both[:rows], right_low)


def stacked(field):
    return jnp.concatenate(halves(field), axis=0)


def coupling(both, high, low, store):
    size = high.shape[0]
    tile = tile_of(size)
    for start in range(0, size, tile):
        rows, cols = pl.ds(start, size - start), pl.ds(start, tile)
        store(start, product(both[:, start:], high[rows, cols], low[rows, cols]))


def forward(both, high, low, store):
    size = high.shape[0]
    tile = tile_of(size)
    for start in range(0, size, tile):
        rows, cols = pl.ds(0, start + tile), pl.ds(start, tile)
        store(start, product(both[:, : start + tile], high[rows, cols], low[rows, cols]))


def split_next(next_ref, high_ref, low_ref, field, store, raw, sems):
    size = raw.shape[0]
    tile = tile_of(size)
    starts = list(range(0, size, tile))
    parts = [(pl.ds(start, tile), pl.ds(0, start + tile)) for start in starts]
    copies = [
        pltpu.make_async_copy(next_ref.at[part], raw.at[part], sems.at[index]) for index, part in enumerate(parts)
    ]
    for copy in copies:
        copy.start()
    for start, part, copy in zip(starts, parts, copies):
        copy.wait()
        high, low = halves(raw[part])
        high_ref[part] = high
        low_ref[part] = low
        store(start, product(stacked(field[:, pl.ds(start, tile)]), high, low))


def adding(total_ref):
    def store(start, part):
        tile = part.shape[1] - start
        if start:
            total_ref[:, pl.ds(0, start)] = total_ref[:, pl.ds(0, start)] + part[:, :start]
        total_ref[:, pl.ds(start, tile)] = part[:, start:]

    return store


def begin_odd_kernel(next_ref, field_ref, high_ref, low_ref, cross_ref, raw, sems):
    @pl.when(is_odd())
    def _():
        split_next(next_ref, high_ref, low_ref, field_ref, adding(cross_ref), raw, sems)


def begin_even_kernel(next_ref, field_ref, high_in, low_in, high_ref, low_ref, pair_ref, raw, sems):
    del high_in, low_in

    @pl.when(jnp.logical_not(is_odd()))
    def _():
        split_next(next_ref, high_ref, low_ref, field_ref, adding(pair_ref), raw, sems)

    @pl.when(is_odd())
    def _():
        pair_ref[...] = field_ref[...]


def flip_kernel(high_in, low_in, high_ref, low_ref):
    size = high_in.shape[0]
    tile = tile_of(size)
    for row in range(0, size, tile):
        for col in range(0, row + tile, tile):
            source, target = (pl.ds(row, tile), pl.ds(col, tile)), (pl.ds(col, tile), pl.ds(row, tile))
            high_ref[target] = jnp.transpose(high_in[source])
            low_ref[target] = jnp.transpose(low_in[source])


def local_kernel(local_ref, field_ref, marginal_ref, shrinkage_ref, high_ref, low_ref, rest_ref, shift_ref):
    size = local_ref.shape[0]
    tile = tile_of(size)
    both = stacked(field_ref[...])
    total = None
    for start in range(0, size, tile):
        rows = pl.ds(start, tile)
        row = lax.broadcasted_iota(jnp.int32, (tile, size), 0) + start
        col = lax.broadcasted_iota(jnp.int32, (tile, size), 1)
        high, low = halves(local_ref[rows, :] - jnp.where(row == col, 1.0, 0.0))
        high_ref[rows, :] = high
        low_ref[rows, :] = low
        part = product(both[:, start : start + tile], high, low)
        total = part if total is None else total + part
    traits = field_ref.shape[0]
    here = lax.broadcasted_iota(jnp.int32, (traits, traits), 0) == lax.broadcasted_iota(jnp.int32, (traits, traits), 1)
    ridge = jnp.sum(jnp.where(here, shrinkage_ref[...], 0.0), axis=1, keepdims=True)
    shift = 1.0 + ridge
    shift_ref[...] = jnp.broadcast_to(shift, shift_ref.shape)
    rest_ref[...] = marginal_ref[...] - shift * field_ref[...] - total


def moment(left, right):
    return jnp.sum(left * right, axis=1, keepdims=True)


def own_kernel(before_ref, field_ref, high_ref, low_ref, own_ref, moments_ref):
    field = field_ref[...]
    own_ref[...] = product(stacked(field), high_ref[...], low_ref[...])
    lane = lax.broadcasted_iota(jnp.int32, moments_ref.shape, 1)
    cross = 0.0 if before_ref is None else moment(before_ref[...], field)
    moments_ref[...] = jnp.where(lane == 0, moment(field, field), jnp.where(lane == 1, cross, 0.0))


def pair_kernel(sign, own_ref, got_pair_ref, high_up, low_up, base_ref):
    @pl.when(is_odd())
    def _():
        base_ref[...] = own_ref[...] + sign * got_pair_ref[...]

    @pl.when(jnp.logical_not(is_odd()))
    def _():
        tile = tile_of(own_ref.shape[1])

        def store(start, part):
            cols = pl.ds(start, tile)
            base_ref[:, cols] = own_ref[:, cols] + sign * part

        forward(stacked(got_pair_ref[...]), high_up, low_up, store)


def even_kernel(sign, base_ref, got_ref, after_ref, field_ref):
    del after_ref

    @pl.when(jnp.logical_not(is_odd()))
    def _():
        field_ref[...] = base_ref[...] + sign * got_ref[...]


def odd_kernel(sign, base_ref, got_ref, high_in, low_in, high_up, low_up, after_ref, field_ref, cross_ref):
    del after_ref

    @pl.when(is_odd())
    def _():
        tile = tile_of(base_ref.shape[1])

        def keep(start, part):
            cols = pl.ds(start, tile)
            field_ref[:, cols] = base_ref[:, cols] + sign * part

        def send(start, part):
            cross_ref[:, pl.ds(start, tile)] = part

        forward(stacked(got_ref[...]), high_up, low_up, keep)
        coupling(stacked(field_ref[...]), high_in, low_in, send)


def merge_kernel(even_ref, odd_ref, high_in, low_in, field_ref, pair_ref):
    @pl.when(is_odd())
    def _():
        field_ref[...] = odd_ref[...]
        pair_ref[...] = odd_ref[...]

    @pl.when(jnp.logical_not(is_odd()))
    def _():
        tile = tile_of(even_ref.shape[1])

        def send(start, part):
            pair_ref[:, pl.ds(start, tile)] = part

        field_ref[...] = even_ref[...]
        coupling(stacked(even_ref[...]), high_in, low_in, send)


def reduce_kernel(field_ref, own_ref, got_pair_ref, got_up_ref, base_ref, one_ref, two_ref, three_ref, out_ref):
    del base_ref
    traits = field_ref.shape[0]
    lower = jnp.where(is_odd(), got_pair_ref[...], got_up_ref[...])
    last = moment(field_ref[...], own_ref[...] + 2.0 * lower)
    lane = lax.broadcasted_iota(jnp.int32, (traits, 128), 1)
    parts = (
        one_ref[:, 0:1],
        two_ref[:, 1:2],
        two_ref[:, 0:1],
        three_ref[:, 1:2],
        three_ref[:, 0:1],
        last,
    )
    table = jnp.zeros((traits, 128), F32)
    for index, part in enumerate(parts):
        table = jnp.where(lane == index, part, table)
    lanes = out_ref.shape[2]
    if lanes > traits:
        table = jnp.concatenate([table, jnp.zeros((lanes - traits, 128), F32)], axis=0)
    rows = jnp.transpose(table)[:MOMENT_ROWS]
    for index in range(out_ref.shape[0]):
        out_ref[index] = rows


def coefficients(moments, shift):
    def inner(left, right):
        total = None
        for i, a in enumerate(left):
            for j, b in enumerate(right):
                term = (a * b) * moments[i + j]
                total = term if total is None else total + term
        return total

    one = jnp.ones_like(shift)
    zero = jnp.zeros_like(shift)
    residual, direction, gain = [one], [one], []
    norm_now = moments[0]
    for step in range(ITERS):
        image = [shift * a + b for a, b in zip(direction + [zero], [zero] + direction)]
        alpha = norm_now / inner(direction, image)
        gain = [a + alpha * b for a, b in zip(gain + [zero], direction)]
        residual = [a - alpha * b for a, b in zip(residual + [zero], image)]
        if step + 1 < ITERS:
            norm_next = inner(residual, residual)
            ratio = norm_next / norm_now
            direction = [a + ratio * b for a, b in zip(residual, direction + [zero])]
            norm_now = norm_next
    return gain, residual


def weights_kernel(table_ref, shift_ref, weights_ref):
    traits = shift_ref.shape[0]
    sums = jnp.sum(table_ref[...], axis=0)
    square = jnp.concatenate([sums, jnp.zeros((sums.shape[1] - MOMENT_ROWS, sums.shape[1]), F32)], axis=0)
    columns = jnp.transpose(square)[:traits]
    moments = [columns[:, i : i + 1] for i in range(2 * ITERS)]
    gain, residual = coefficients(moments, shift_ref[:, 0:1])
    lane = lax.broadcasted_iota(jnp.int32, (traits, 128), 1)
    table = jnp.zeros((traits, 128), F32)
    for index, part in enumerate(gain + residual):
        table = jnp.where(lane == index, part, table)
    weights_ref[...] = table


def final_kernel(
    weights_ref, start_ref, zero_ref, one_ref, two_ref, base_ref, got_down_ref, got_up_ref, high_up, low_up,
    solution_ref, residual_ref,
):
    tile = tile_of(base_ref.shape[1])
    weights = [weights_ref[:, i : i + 1] for i in range(2 * ITERS + 1)]
    gain, residual = weights[:ITERS], weights[ITERS:]
    zero, one, two = zero_ref[...], one_ref[...], two_ref[...]
    solution_ref[...] = start_ref[...] + gain[0] * zero + gain[1] * one + gain[2] * two
    residual_ref[...] = residual[0] * zero + residual[1] * one + residual[2] * two + residual[3] * base_ref[...]

    @pl.when(is_odd())
    def _():
        def store(start, part):
            cols = pl.ds(start, tile)
            residual_ref[:, cols] = residual_ref[:, cols] + residual[3] * part

        forward(stacked(got_down_ref[...]), high_up, low_up, store)

    @pl.when(jnp.logical_not(is_odd()))
    def _():
        residual_ref[...] = residual_ref[...] + residual[3] * got_up_ref[...]


def call(kernel, out, *args, spaces=None, scratch=(), limit=12, aliases=None, keep=True, flops=0):
    spaces = spaces or {}
    places = [spaces.get(i, VMEM) for i in range(len(args))]
    args = [
        arg if place is pltpu.SMEM else pltpu.with_memory_space_constraint(arg, place)
        for arg, place in zip(args, places)
    ]
    make = VMEM if keep else jax.ShapeDtypeStruct
    return pl.pallas_call(
        kernel,
        out_shape=[make(shape, dtype) for shape, dtype in out],
        in_specs=[pl.BlockSpec(memory_space=place) for place in places],
        out_specs=[pl.BlockSpec(memory_space=VMEM) for _ in out],
        scratch_shapes=scratch,
        input_output_aliases=aliases or {},
        cost_estimate=pl.CostEstimate(flops=flops, bytes_accessed=0, transcendentals=0) if flops else None,
        compiler_params=pltpu.CompilerParams(vmem_limit_bytes=limit * 1024 * 1024),
    )(*args)


def on_device(local_block, next_block, shrinkage, marginal, warm_start):
    count = lax.axis_size("snp")
    traits, size = warm_start.shape
    field = ((traits, size), F32)
    table = ((traits, 128), F32)
    matrix = ((size, size), BF16)
    work = 6 * traits * size * size
    copies = (
        pltpu.VMEM((size, size), F32),
        pltpu.SemaphoreType.DMA((size // tile_of(size),)),
    )
    on_chip = [(i, i ^ 1) for i in range(count) if i ^ 1 < count]
    downward = [(i + 1, i) for i in range(count - 1)]
    upward = [(i, i + 1) for i in range(count - 1)]

    def shift(value, route):
        return lax.ppermute(value, "snp", route)

    def run(kernel, out, *args, **rest):
        return call(kernel, out, *args, **rest)

    down = shift(warm_start, downward)
    high_n, low_n, cross = run(
        begin_odd_kernel, [matrix, matrix, field], next_block, warm_start,
        spaces={0: pltpu.HBM}, scratch=copies, flops=work,
    )
    up = shift(cross, upward)
    high_n, low_n, pair = run(
        begin_even_kernel, [matrix, matrix, field], next_block, warm_start, high_n, low_n,
        spaces={0: pltpu.HBM}, scratch=copies, aliases={2: 0, 3: 1}, flops=work,
    )
    got_pair = shift(pair, on_chip)
    high_l, low_l, own, ridge = run(
        local_kernel, [matrix, matrix, field, table],
        local_block, warm_start, marginal, shrinkage.reshape(1, traits), flops=work,
    )
    flipped = run(flip_kernel, [matrix, matrix], high_n, low_n, flops=work)
    sign = -1.0
    fields, tables = [], []
    for step in range(1, ITERS + 1):
        (base,) = run(functools.partial(pair_kernel, sign), [field], own, got_pair, *flipped, flops=work)
        even = functools.partial(even_kernel, sign)
        odd = functools.partial(odd_kernel, sign)
        if step % 2:
            odd_field, cross = run(odd, [field, field], base, down, high_n, low_n, *flipped, ridge, flops=work)
            next_up = shift(cross, upward)
            (even_field,) = run(even, [field], base, up, odd_field, flops=work)
            down = shift(even_field, downward)
        else:
            (even_field,) = run(even, [field], base, up, ridge, flops=work)
            next_down = shift(even_field, downward)
            odd_field, cross = run(odd, [field, field], base, down, high_n, low_n, *flipped, even_field, flops=work)
            next_up = shift(cross, upward)
            down = next_down
        up = next_up
        merged, pair = run(merge_kernel, [field, field], even_field, odd_field, high_n, low_n, flops=work)
        got_pair = shift(pair, on_chip)
        before = fields[-1:]
        kernel = own_kernel if before else functools.partial(own_kernel, None)
        own, part = run(kernel, [field, table], *before, merged, high_l, low_l, flops=work)
        fields.append(merged)
        tables.append(part)
        sign = 1.0
    (base,) = run(functools.partial(pair_kernel, sign), [field], own, got_pair, *flipped, flops=work)
    lanes = -(-traits // 128) * 128
    (moments,) = run(reduce_kernel, [((count, MOMENT_ROWS, lanes), F32)], fields[-1], own, got_pair, up, base, *tables)
    moments = lax.all_to_all(moments, "snp", 0, 0)
    (weights,) = run(weights_kernel, [table], moments, ridge)
    return tuple(
        run(
            final_kernel, [field, field],
            weights, warm_start, *fields, base, down, up, *flipped,
            keep=False,
        )
    )


def solution(mesh):
    return jax.shard_map(
        on_device,
        mesh=mesh,
        in_specs=(
            P(("parts", "snp"), None),
            P(("parts", "snp"), None),
            P(),
            P(None, ("parts", "snp")),
            P(None, ("parts", "snp")),
        ),
        out_specs=(P(None, ("parts", "snp")), P(None, ("parts", "snp"))),
        check_vma=False,
    )
```

time: 61.5 us -> 68 us (1.11)
  starting transfers between devices: 23 us -> 29 us
  blocking collectives: 21.8 us -> 17.1 us
  Pallas kernels: 11.4 us -> 15.8 us
    ppermute x8 -> x12, starting transfers between devices: 23 us -> 29 us  [shift(): return lax.ppermute(value, 'snp', route)]
    all_to_all x1, blocking collectives: 21.8 us -> 17.1 us  [on_device(): moments = lax.all_to_all(moments, 'snp', 0, 0)]
    pallas_call x11 -> x23, Pallas kernels: 11.4 us -> 15.8 us  [call(): pl.pallas_call(kernel, out_shape=[make(shape, dtype) for shape, dtype in...]
    unnamed x8 -> x6, local copies, waits for them, and re-layouts: 0.96 us -> 1.39 us
    ppermute x8 -> x12, waiting for transfers between devices: 3.19 us -> 3.3 us  [shift(): return lax.ppermute(value, 'snp', route)]
  transfers between devices with their start and end apart: 8 -> 12, of which waited for: 4 -> 1; matrix products, arithmetic and copies ran while one was open for 0% -> 0% of each run, Pallas kernels for 6% -> 12%
where the time goes in v3:
time: 68 us; the launch traced here: 67.5 us
  starting transfers between devices  29 us (43%)
  blocking collectives  17.1 us (25%)
  Pallas kernels  15.8 us (23%)
  waiting for transfers between devices  3.3 us (5%)
  local copies, waits for them, and re-layouts  1.39 us (2%)
  between operations  0.92 us (1%)
    ppermute x12, starting transfers between devices, shift(): return lax.ppermute(value, 'snp', route)  29 us
    all_to_all x1, blocking collectives, on_device(): moments = lax.all_to_all(moments, 'snp', 0, 0)  17.1 us
    pallas_call x23, Pallas kernels, call(): pl.pallas_call(kernel, out_shape=[make(shape, dtype) for shape, dtype in...  15.8 us
    ppermute x12, waiting for transfers between devices, shift(): return lax.ppermute(value, 'snp', route)  3.3 us
    unnamed x6, local copies, waits for them, and re-layouts  1.39 us
  transfers between devices with their start and end apart: 12, of which 1 were waited for; matrix products, arithmetic and copies ran while one was open for 0% of the time, Pallas kernels for 12%

profile of v3, /device:TPU:0, one launch (start us, length us, event | category | flops | bytes accessed | tf_op | source)
XLA Modules:
  0.0 67.5 jit_solution(15669726835304107265)
XLA Ops:
  0.6 1.0 %shard_map.69 = (bf16[1024,1024]{1,0:T(8,128)(2,1)S(1)}, bf16[1024,1024]{1,0:T(8,128)(2,1)S(1)}, f32[64,1024]{1,0:T(8,128)S(1)}) custom-call(f32[1024,1024]{1,0:T(8,128)} %next_ref.3, f32[64,1024]{1,0:T(8,128)} %start_ref.1), custom_call_target="tpu_custom_call" | custom-call | flops 402653184 | tf_op jit(solution)/shard_map/pallas_call | solution.py:307
  1.6 3.1 %shard_map.70 = (bf16[1024,1024]{1,0:T(8,128)(2,1)S(1)}, bf16[1024,1024]{1,0:T(8,128)(2,1)S(1)}, f32[64,1024]{1,0:T(8,128)S(1)}) custom-call(f32[1024,1024]{1,0:T(8,128)} %next_ref.3, f32[64,1024]{1,0:T(8,128)} %start_ref.1, bf16[1024,1024]{1,0:T(8,128)(2,1)S(1)} %get-tuple-element.33.high_in, ...), custom_call_target="tpu_custom_call", output_to_operand_aliasing={{0}: (2, {}), {1}: (3, {})} | custom-call | flops 402653184 | tf_op jit(solution)/shard_map/pallas_call | solution.py:307
  4.7 0.6 collective-permute-start
  5.3 1.3 %collective-permute-start.2 = (f32[64,1024]{1,0:T(8,128)}, f32[64,1024]{1,0:T(8,128)S(1)}, u32[]{:S(2)}, u32[]{:S(2)}) collective-permute-start(f32[64,1024]{1,0:T(8,128)} %start_ref.1), channel_id=1, source_target_pairs={{1,0},{2,1},{3,2},{4,3},{5,4},{6,5},{7,6},{8,7},{9,8},{10,9},{11,1... | collective-permute-start | bytes 786440 | tf_op jit(solution)/shard_map/ppermute | solution.py:335
  6.6 3.0 %collective-permute-start.1 = (f32[64,1024]{1,0:T(8,128)S(1)}, f32[64,1024]{1,0:T(8,128)S(1)}, u32[]{:S(2)}, u32[]{:S(2)}) collective-permute-start(f32[64,1024]{1,0:T(8,128)S(1)} %get-tuple-element.40), channel_id=1, source_target_pairs={{0,1},{1,2},{2,3},{3,4},{4,5},{5,6},{6,7},{7,8},{8,9},{9,10},{10,1... | collective-permute-start | bytes 786440 | tf_op jit(solution)/shard_map/ppermute | solution.py:335
  9.7 0.8 %shard_map.71 = (bf16[1024,1024]{1,0:T(8,128)(2,1)S(1)}, bf16[1024,1024]{1,0:T(8,128)(2,1)S(1)}) custom-call(bf16[1024,1024]{1,0:T(8,128)(2,1)S(1)} %get-tuple-element.36.high_in, bf16[1024,1024]{1,0:T(8,128)(2,1)S(1)} %get-tuple-element.37.low_in), custom_call_target="tpu_custom_call" | custom-call | flops 402653184 | tf_op jit(solution)/shard_map/pallas_call | solution.py:307
  10.4 1.4 %copy-done = f32[1024,1024]{1,0:T(8,128)S(1)} copy-done((f32[1024,1024]{1,0:T(8,128)S(1)}, f32[1024,1024]{1,0:T(8,128)}, u32[]{:S(2)}) %copy-start) | copy-done | bytes 4194328
  11.8 2.0 %shard_map.68 = (bf16[1024,1024]{1,0:T(8,128)(2,1)S(1)}, bf16[1024,1024]{1,0:T(8,128)(2,1)S(1)}, f32[64,1024]{1,0:T(8,128)S(1)}, f32[64,128]{1,0:T(8,128)S(1)}) custom-call(f32[1024,1024]{1,0:T(8,128)S(1)} %copy-done, f32[64,1024]{1,0:T(8,128)} %start_ref.1, f32[64,1024]{1,0:T(8,128)S(1)} %copy-done.1, f32[1,64]{1,0:T(1,128)S(1)} %bitcast.1), custom_call_target="tpu_custom_call" | custom-call | flops 402653184 | tf_op jit(solution)/shard_map/pallas_call | solution.py:307
  13.8 0.6 shard_map.72.base_ref
  14.4 0.6 shard_map.75
  15.0 2.8 %collective-permute-start.3 = (f32[64,1024]{1,0:T(8,128)S(1)}, f32[64,1024]{1,0:T(8,128)S(1)}, u32[]{:S(2)}, u32[]{:S(2)}) collective-permute-start(f32[64,1024]{1,0:T(8,128)S(1)} %get-tuple-element.47), channel_id=1, source_target_pairs={{0,1},{1,0},{2,3},{3,2},{4,5},{5,4},{6,7},{7,6},{8,9},{9,8},{10,11... | collective-permute-start | bytes 786440 | tf_op jit(solution)/shard_map/ppermute | solution.py:335
  17.8 1.9 %collective-permute-start.4 = (f32[64,1024]{1,0:T(8,128)S(1)}, f32[64,1024]{1,0:T(8,128)S(1)}, u32[]{:S(2)}, u32[]{:S(2)}) collective-permute-start(f32[64,1024]{1,0:T(8,128)S(1)} %get-tuple-element.48), channel_id=1, source_target_pairs={{0,1},{1,2},{2,3},{3,4},{4,5},{5,6},{6,7},{7,8},{8,9},{9,10},{10,1... | collective-permute-start | bytes 786440 | tf_op jit(solution)/shard_map/ppermute | solution.py:335
  19.7 1.3 %collective-permute-start.5 = (f32[64,1024]{1,0:T(8,128)S(1)}, f32[64,1024]{1,0:T(8,128)S(1)}, u32[]{:S(2)}, u32[]{:S(2)}) collective-permute-start(f32[64,1024]{1,0:T(8,128)S(1)} %shard_map.74.even_ref), channel_id=1, source_target_pairs={{1,0},{2,1},{3,2},{4,3},{5,4},{6,5},{7,6},{8,7},{9,8},{10,9},{11,1... | collective-permute-start | bytes 786440 | tf_op jit(solution)/shard_map/ppermute | solution.py:335
  21.0 0.8 %shard_map.76 = (f32[64,1024]{1,0:T(8,128)S(1)}, f32[64,128]{1,0:T(8,128)S(1)}) custom-call(f32[64,1024]{1,0:T(8,128)S(1)} %get-tuple-element.43.field_ref.before_ref.zero_ref, bf16[1024,1024]{1,0:T(8,128)(2,1)S(1)} %get-tuple-element.44.high_ref, bf16[1024,1024]{1,0:T(8,128)(2,1)S(1)} %get-tuple-element.45.low_ref), custom_call_target="tpu_custom_call" | custom-call | flops 402653184 | tf_op jit(solution)/shard_map/pallas_call | solution.py:307
  21.8 0.6 shard_map.77.base_ref
  22.4 3.3 %collective-permute-done.5.got_ref = f32[64,1024]{1,0:T(8,128)S(1)} collective-permute-done((f32[64,1024]{1,0:T(8,128)S(1)}, f32[64,1024]{1,0:T(8,128)S(1)}, u32[]{:S(2)}, u32[]{:S(2)}) %collective-permute-start.5) | collective-permute-done | bytes 262176 | tf_op jit(solution)/shard_map/ppermute | solution.py:335
  25.7 0.6 shard_map.80
  26.3 5.4 %collective-permute-start.6 = (f32[64,1024]{1,0:T(8,128)S(1)}, f32[64,1024]{1,0:T(8,128)S(1)}, u32[]{:S(2)}, u32[]{:S(2)}) collective-permute-start(f32[64,1024]{1,0:T(8,128)S(1)} %get-tuple-element.52), channel_id=1, source_target_pairs={{0,1},{1,0},{2,3},{3,2},{4,5},{5,4},{6,7},{7,6},{8,9},{9,8},{10,11... | collective-permute-start | bytes 786440 | tf_op jit(solution)/shard_map/ppermute | solution.py:335
  31.6 1.3 %collective-permute-start.8 = (f32[64,1024]{1,0:T(8,128)S(1)}, f32[64,1024]{1,0:T(8,128)S(1)}, u32[]{:S(2)}, u32[]{:S(2)}) collective-permute-start(f32[64,1024]{1,0:T(8,128)S(1)} %shard_map.78.after_ref.even_ref), channel_id=1, source_target_pairs={{1,0},{2,1},{3,2},{4,3},{5,4},{6,5},{7,6},{8,7},{9,8},{10,9},{11,1... | collective-permute-start | bytes 786440 | tf_op jit(solution)/shard_map/ppermute | solution.py:335
  32.9 3.0 %collective-permute-start.7 = (f32[64,1024]{1,0:T(8,128)S(1)}, f32[64,1024]{1,0:T(8,128)S(1)}, u32[]{:S(2)}, u32[]{:S(2)}) collective-permute-start(f32[64,1024]{1,0:T(8,128)S(1)} %get-tuple-element.53), channel_id=1, source_target_pairs={{0,1},{1,2},{2,3},{3,4},{4,5},{5,6},{6,7},{7,8},{8,9},{9,10},{10,1... | collective-permute-start | bytes 786440 | tf_op jit(solution)/shard_map/ppermute | solution.py:335
  36.0 0.8 %shard_map.81 = (f32[64,1024]{1,0:T(8,128)S(1)}, f32[64,128]{1,0:T(8,128)S(1)}) custom-call(f32[64,1024]{1,0:T(8,128)S(1)} %get-tuple-element.43.field_ref.before_ref.zero_ref, f32[64,1024]{1,0:T(8,128)S(1)} %get-tuple-element.50.field_ref.before_ref.one_ref, bf16[1024,1024]{1,0:T(8,128)(2,1)S(1)} %get-tuple-element.44.high_ref, ...), custom_call_target="tpu_custom_call" | custom-call | flops 402653184 | tf_op jit(solution)/shard_map/pallas_call | solution.py:307
  36.8 0.6 shard_map.82.base_ref
  37.4 0.6 shard_map.85
  38.0 5.1 %collective-permute-start.9 = (f32[64,1024]{1,0:T(8,128)S(1)}, f32[64,1024]{1,0:T(8,128)S(1)}, u32[]{:S(2)}, u32[]{:S(2)}) collective-permute-start(f32[64,1024]{1,0:T(8,128)S(1)} %get-tuple-element.57), channel_id=1, source_target_pairs={{0,1},{1,0},{2,3},{3,2},{4,5},{5,4},{6,7},{7,6},{8,9},{9,8},{10,11... | collective-permute-start | bytes 786440 | tf_op jit(solution)/shard_map/ppermute | solution.py:335
  43.1 1.9 %collective-permute-start.10 = (f32[64,1024]{1,0:T(8,128)S(1)}, f32[64,1024]{1,0:T(8,128)S(1)}, u32[]{:S(2)}, u32[]{:S(2)}) collective-permute-start(f32[64,1024]{1,0:T(8,128)S(1)} %get-tuple-element.58), channel_id=1, source_target_pairs={{0,1},{1,2},{2,3},{3,4},{4,5},{5,6},{6,7},{7,8},{8,9},{9,10},{10,1... | collective-permute-start | bytes 786440 | tf_op jit(solution)/shard_map/ppermute | solution.py:335
  45.1 1.3 %collective-permute-start.11 = (f32[64,1024]{1,0:T(8,128)S(1)}, f32[64,1024]{1,0:T(8,128)S(1)}, u32[]{:S(2)}, u32[]{:S(2)}) collective-permute-start(f32[64,1024]{1,0:T(8,128)S(1)} %shard_map.84.even_ref), channel_id=1, source_target_pairs={{1,0},{2,1},{3,2},{4,3},{5,4},{6,5},{7,6},{8,7},{9,8},{10,9},{11,1... | collective-permute-start | bytes 786440 | tf_op jit(solution)/shard_map/ppermute | solution.py:335
  46.4 0.8 %shard_map.86 = (f32[64,1024]{1,0:T(8,128)S(1)}, f32[64,128]{1,0:T(8,128)S(1)}) custom-call(f32[64,1024]{1,0:T(8,128)S(1)} %get-tuple-element.50.field_ref.before_ref.one_ref, f32[64,1024]{1,0:T(8,128)S(1)} %get-tuple-element.55.field_ref.two_ref, bf16[1024,1024]{1,0:T(8,128)(2,1)S(1)} %get-tuple-element.44.high_ref, ...), custom_call_target="tpu_custom_call" | custom-call | flops 402653184 | tf_op jit(solution)/shard_map/pallas_call | solution.py:307
  47.2 0.6 shard_map.87.base_ref
  47.7 0.2 shard_map.88
  48.0 17.1 %all_to_all.5.table_ref = f32[16,8,128]{2,1,0:T(8,128)S(1)} all-to-all(f32[16,8,128]{2,1,0:T(8,128)S(1)} %shard_map.88), channel_id=1, replica_groups=mesh['parts'=2,'snp'=16] {'snp'}, dimensions={0} | all-to-all | bytes 131072 | tf_op jit(solution)/shard_map/all_to_all | solution.py:385
  65.1 0.4 shard_map.89.weights_ref
  65.5 2.0 %shard_map.90 = (f32[64,1024]{1,0:T(8,128)}, f32[64,1024]{1,0:T(8,128)}) custom-call(f32[64,128]{1,0:T(8,128)S(1)} %shard_map.89.weights_ref, f32[64,1024]{1,0:T(8,128)} %start_ref.1, f32[64,1024]{1,0:T(8,128)S(1)} %get-tuple-element.43.field_ref.before_ref.zero_ref, f32[64,1024]{1,0:T(8,128)S(1)} %get-tuple-element.50.field_ref.before_ref.one_ref, ...), custom_call_target="tpu_custom_call" | custom-call | tf_op jit(solution)/shard_map/pallas_call | solution.py:307
  (22 shorter events, 0.2 us)
Async XLA Ops:
  1.6 8.8 %copy-start.1 = (f32[64,1024]{1,0:T(8,128)S(1)}, f32[64,1024]{1,0:T(8,128)}, u32[]{:S(2)}) copy-start(f32[64,1024]{1,0:T(8,128)} %marginal_ref.1) | copy-start | bytes 786436
  4.7 9.1 %collective-permute-start = (f32[64,1024]{1,0:T(8,128)S(1)}, f32[64,1024]{1,0:T(8,128)S(1)}, u32[]{:S(2)}, u32[]{:S(2)}) collective-permute-start(f32[64,1024]{1,0:T(8,128)S(1)} %get-tuple-element.35), channel_id=1, source_target_pairs={{0,1},{1,0},{2,3},{3,2},{4,5},{5,4},{6,7},{7,6},{8,9},{9,8},{10,11... | collective-permute-start | bytes 786440 | tf_op jit(solution)/shard_map/ppermute | solution.py:335
  5.3 9.1 %collective-permute-start.2 = (f32[64,1024]{1,0:T(8,128)}, f32[64,1024]{1,0:T(8,128)S(1)}, u32[]{:S(2)}, u32[]{:S(2)}) collective-permute-start(f32[64,1024]{1,0:T(8,128)} %start_ref.1), channel_id=1, source_target_pairs={{1,0},{2,1},{3,2},{4,3},{5,4},{6,5},{7,6},{8,7},{9,8},{10,9},{11,1... | collective-permute-start | bytes 786440 | tf_op jit(solution)/shard_map/ppermute | solution.py:335
  6.6 7.8 %collective-permute-start.1 = (f32[64,1024]{1,0:T(8,128)S(1)}, f32[64,1024]{1,0:T(8,128)S(1)}, u32[]{:S(2)}, u32[]{:S(2)}) collective-permute-start(f32[64,1024]{1,0:T(8,128)S(1)} %get-tuple-element.40), channel_id=1, source_target_pairs={{0,1},{1,2},{2,3},{3,4},{4,5},{5,6},{6,7},{7,8},{8,9},{9,10},{10,1... | collective-permute-start | bytes 786440 | tf_op jit(solution)/shard_map/ppermute | solution.py:335
  9.6 2.2 %copy-start = (f32[1024,1024]{1,0:T(8,128)S(1)}, f32[1024,1024]{1,0:T(8,128)}, u32[]{:S(2)}) copy-start(f32[1024,1024]{1,0:T(8,128)} %local_ref.1) | copy-start | bytes 12582916
  9.6 2.2 %copy-start.2 = (f32[64,1]{0,1:T(1,128)S(1)}, f32[64,1]{0,1:T(1,128)}, u32[]{:S(2)}) copy-start(f32[64,1]{0,1:T(1,128)} %param.7) | copy-start | bytes 772
  15.0 6.8 %collective-permute-start.3 = (f32[64,1024]{1,0:T(8,128)S(1)}, f32[64,1024]{1,0:T(8,128)S(1)}, u32[]{:S(2)}, u32[]{:S(2)}) collective-permute-start(f32[64,1024]{1,0:T(8,128)S(1)} %get-tuple-element.47), channel_id=1, source_target_pairs={{0,1},{1,0},{2,3},{3,2},{4,5},{5,4},{6,7},{7,6},{8,9},{9,8},{10,11... | collective-permute-start | bytes 786440 | tf_op jit(solution)/shard_map/ppermute | solution.py:335
  17.8 4.6 %collective-permute-start.4 = (f32[64,1024]{1,0:T(8,128)S(1)}, f32[64,1024]{1,0:T(8,128)S(1)}, u32[]{:S(2)}, u32[]{:S(2)}) collective-permute-start(f32[64,1024]{1,0:T(8,128)S(1)} %get-tuple-element.48), channel_id=1, source_target_pairs={{0,1},{1,2},{2,3},{3,4},{4,5},{5,6},{6,7},{7,8},{8,9},{9,10},{10,1... | collective-permute-start | bytes 786440 | tf_op jit(solution)/shard_map/ppermute | solution.py:335
  19.7 6.0 %collective-permute-start.5 = (f32[64,1024]{1,0:T(8,128)S(1)}, f32[64,1024]{1,0:T(8,128)S(1)}, u32[]{:S(2)}, u32[]{:S(2)}) collective-permute-start(f32[64,1024]{1,0:T(8,128)S(1)} %shard_map.74.even_ref), channel_id=1, source_target_pairs={{1,0},{2,1},{3,2},{4,3},{5,4},{6,5},{7,6},{8,7},{9,8},{10,9},{11,1... | collective-permute-start | bytes 786440 | tf_op jit(solution)/shard_map/ppermute | solution.py:335
  26.3 10.5 %collective-permute-start.6 = (f32[64,1024]{1,0:T(8,128)S(1)}, f32[64,1024]{1,0:T(8,128)S(1)}, u32[]{:S(2)}, u32[]{:S(2)}) collective-permute-start(f32[64,1024]{1,0:T(8,128)S(1)} %get-tuple-element.52), channel_id=1, source_target_pairs={{0,1},{1,0},{2,3},{3,2},{4,5},{5,4},{6,7},{7,6},{8,9},{9,8},{10,11... | collective-permute-start | bytes 786440 | tf_op jit(solution)/shard_map/ppermute | solution.py:335
  31.6 5.7 %collective-permute-start.8 = (f32[64,1024]{1,0:T(8,128)S(1)}, f32[64,1024]{1,0:T(8,128)S(1)}, u32[]{:S(2)}, u32[]{:S(2)}) collective-permute-start(f32[64,1024]{1,0:T(8,128)S(1)} %shard_map.78.after_ref.even_ref), channel_id=1, source_target_pairs={{1,0},{2,1},{3,2},{4,3},{5,4},{6,5},{7,6},{8,7},{9,8},{10,9},{11,1... | collective-permute-start | bytes 786440 | tf_op jit(solution)/shard_map/ppermute | solution.py:335
  32.9 4.4 %collective-permute-start.7 = (f32[64,1024]{1,0:T(8,128)S(1)}, f32[64,1024]{1,0:T(8,128)S(1)}, u32[]{:S(2)}, u32[]{:S(2)}) collective-permute-start(f32[64,1024]{1,0:T(8,128)S(1)} %get-tuple-element.53), channel_id=1, source_target_pairs={{0,1},{1,2},{2,3},{3,4},{4,5},{5,6},{6,7},{7,8},{8,9},{9,10},{10,1... | collective-permute-start | bytes 786440 | tf_op jit(solution)/shard_map/ppermute | solution.py:335
  38.0 9.2 %collective-permute-start.9 = (f32[64,1024]{1,0:T(8,128)S(1)}, f32[64,1024]{1,0:T(8,128)S(1)}, u32[]{:S(2)}, u32[]{:S(2)}) collective-permute-start(f32[64,1024]{1,0:T(8,128)S(1)} %get-tuple-element.57), channel_id=1, source_target_pairs={{0,1},{1,0},{2,3},{3,2},{4,5},{5,4},{6,7},{7,6},{8,9},{9,8},{10,11... | collective-permute-start | bytes 786440 | tf_op jit(solution)/shard_map/ppermute | solution.py:335
  43.1 4.6 %collective-permute-start.10 = (f32[64,1024]{1,0:T(8,128)S(1)}, f32[64,1024]{1,0:T(8,128)S(1)}, u32[]{:S(2)}, u32[]{:S(2)}) collective-permute-start(f32[64,1024]{1,0:T(8,128)S(1)} %get-tuple-element.58), channel_id=1, source_target_pairs={{0,1},{1,2},{2,3},{3,4},{4,5},{5,6},{6,7},{7,8},{8,9},{9,10},{10,1... | collective-permute-start | bytes 786440 | tf_op jit(solution)/shard_map/ppermute | solution.py:335
  45.1 20.5 %collective-permute-start.11 = (f32[64,1024]{1,0:T(8,128)S(1)}, f32[64,1024]{1,0:T(8,128)S(1)}, u32[]{:S(2)}, u32[]{:S(2)}) collective-permute-start(f32[64,1024]{1,0:T(8,128)S(1)} %shard_map.84.even_ref), channel_id=1, source_target_pairs={{1,0},{2,1},{3,2},{4,3},{5,4},{6,5},{7,6},{8,7},{9,8},{10,9},{11,1... | collective-permute-start | bytes 786440 | tf_op jit(solution)/shard_map/ppermute | solution.py:335

commit v4 on v3

--- a/solution.py
+++ b/solution.py
@@ -58,16 +58,35 @@
         store(start, product(both[:, : start + tile], high[rows, cols], low[rows, cols]))
 
 
-def split_next(next_ref, high_ref, low_ref, field, store, raw, sems):
+def adding(total_ref):
+    def store(start, part):
+        tile = part.shape[1] - start
+        if start:
+            total_ref[:, pl.ds(0, start)] = total_ref[:, pl.ds(0, start)] + part[:, :start]
+        total_ref[:, pl.ds(start, tile)] = part[:, start:]
+
+    return store
+
+
+def load(source_ref, parts, raw, sems):
+    copies = [
+        pltpu.make_async_copy(source_ref.at[part], raw.at[part], sems.at[index]) for index, part in enumerate(parts)
+    ]
+    for copy in copies:
+        copy.start()
+    return copies
+
+
+def take_next(next_ref, field_ref, high_ref, low_ref, out_ref, raw, field, sems):
     size = raw.shape[0]
     tile = tile_of(size)
     starts = list(range(0, size, tile))
     parts = [(pl.ds(start, tile), pl.ds(0, start + tile)) for start in starts]
-    copies = [
-        pltpu.make_async_copy(next_ref.at[part], raw.at[part], sems.at[index]) for index, part in enumerate(parts)
-    ]
-    for copy in copies:
-        copy.start()
+    ours = pltpu.make_async_copy(field_ref, field, sems.at[len(starts)])
+    ours.start()
+    copies = load(next_ref, parts, raw, sems)
+    store = adding(out_ref)
+    ours.wait()
     for start, part, copy in zip(starts, parts, copies):
         copy.wait()
         high, low = halves(raw[part])
@@ -76,32 +95,52 @@
         store(start, product(stacked(field[:, pl.ds(start, tile)]), high, low))
 
 
-def adding(total_ref):
-    def store(start, part):
-        tile = part.shape[1] - start
-        if start:
-            total_ref[:, pl.ds(0, start)] = total_ref[:, pl.ds(0, start)] + part[:, :start]
-        total_ref[:, pl.ds(start, tile)] = part[:, start:]
-
-    return store
-
-
-def begin_odd_kernel(next_ref, field_ref, high_ref, low_ref, cross_ref, raw, sems):
-    @pl.when(is_odd())
-    def _():
-        split_next(next_ref, high_ref, low_ref, field_ref, adding(cross_ref), raw, sems)
-
-
-def begin_even_kernel(next_ref, field_ref, high_in, low_in, high_ref, low_ref, pair_ref, raw, sems):
-    del high_in, low_in
-
-    @pl.when(jnp.logical_not(is_odd()))
-    def _():
-        split_next(next_ref, high_ref, low_ref, field_ref, adding(pair_ref), raw, sems)
-
-    @pl.when(is_odd())
-    def _():
-        pair_ref[...] = field_ref[...]
+def take_local(local_ref, field_ref, high_ref, low_ref, out_ref, raw, field, sems):
+    size = raw.shape[0]
+    tile = tile_of(size)
+    starts = list(range(0, size, tile))
+    parts = [(pl.ds(start, tile), slice(None)) for start in starts]
+    ours = pltpu.make_async_copy(field_ref, field, sems.at[len(starts)])
+    ours.start()
+    copies = load(local_ref, parts, raw, sems)
+    ours.wait()
+    for start, part, copy in zip(starts, parts, copies):
+        copy.wait()
+        row = lax.broadcasted_iota(jnp.int32, (tile, size), 0) + start
+        col = lax.broadcasted_iota(jnp.int32, (tile, size), 1)
+        high, low = halves(raw[part] - jnp.where(row == col, 1.0, 0.0))
+        high_ref[part] = high
+        low_ref[part] = low
+        done = product(stacked(field[:, pl.ds(start, tile)]), high, low)
+        out_ref[...] = done if start == 0 else out_ref[...] + done
+
+
+def begin_odd_kernel(
+    next_ref, local_ref, start_ref, high_n, low_n, high_l, low_l, cross_ref, own_ref, raw, field, sems
+):
+    @pl.when(is_odd())
+    def _():
+        take_next(next_ref, start_ref, high_n, low_n, cross_ref, raw, field, sems)
+
+    @pl.when(jnp.logical_not(is_odd()))
+    def _():
+        take_local(local_ref, start_ref, high_l, low_l, own_ref, raw, field, sems)
+
+
+def begin_even_kernel(
+    next_ref, local_ref, start_ref, high_n_in, low_n_in, high_l_in, low_l_in, own_in,
+    high_n, low_n, high_l, low_l, own_ref, pair_ref, raw, field, sems,
+):
+    del high_n_in, low_n_in, high_l_in, low_l_in, own_in
+
+    @pl.when(is_odd())
+    def _():
+        take_local(local_ref, start_ref, high_l, low_l, own_ref, raw, field, sems)
+        pair_ref[...] = field[...]
+
+    @pl.when(jnp.logical_not(is_odd()))
+    def _():
+        take_next(next_ref, start_ref, high_n, low_n, pair_ref, raw, field, sems)
 
 
 def flip_kernel(high_in, low_in, high_ref, low_ref):
@@ -114,26 +153,12 @@
             low_ref[target] = jnp.transpose(low_in[source])
 
 
-def local_kernel(local_ref, field_ref, marginal_ref, shrinkage_ref, high_ref, low_ref, rest_ref, shift_ref):
-    size = local_ref.shape[0]
-    tile = tile_of(size)
-    both = stacked(field_ref[...])
-    total = None
-    for start in range(0, size, tile):
-        rows = pl.ds(start, tile)
-        row = lax.broadcasted_iota(jnp.int32, (tile, size), 0) + start
-        col = lax.broadcasted_iota(jnp.int32, (tile, size), 1)
-        high, low = halves(local_ref[rows, :] - jnp.where(row == col, 1.0, 0.0))
-        high_ref[rows, :] = high
-        low_ref[rows, :] = low
-        part = product(both[:, start : start + tile], high, low)
-        total = part if total is None else total + part
-    traits = field_ref.shape[0]
+def rest_kernel(own_ref, start_ref, marginal_ref, shrinkage_ref, rest_ref, shift_ref):
+    traits = start_ref.shape[0]
     here = lax.broadcasted_iota(jnp.int32, (traits, traits), 0) == lax.broadcasted_iota(jnp.int32, (traits, traits), 1)
-    ridge = jnp.sum(jnp.where(here, shrinkage_ref[...], 0.0), axis=1, keepdims=True)
-    shift = 1.0 + ridge
+    shift = 1.0 + jnp.sum(jnp.where(here, shrinkage_ref[...], 0.0), axis=1, keepdims=True)
     shift_ref[...] = jnp.broadcast_to(shift, shift_ref.shape)
-    rest_ref[...] = marginal_ref[...] - shift * field_ref[...] - total
+    rest_ref[...] = marginal_ref[...] - shift * start_ref[...] - own_ref[...]
 
 
 def moment(left, right):
@@ -325,11 +350,12 @@
     work = 6 * traits * size * size
     copies = (
         pltpu.VMEM((size, size), F32),
-        pltpu.SemaphoreType.DMA((size // tile_of(size),)),
+        pltpu.VMEM((traits, size), F32),
+        pltpu.SemaphoreType.DMA((size // tile_of(size) + 1,)),
     )
     on_chip = [(i, i ^ 1) for i in range(count) if i ^ 1 < count]
-    downward = [(i + 1, i) for i in range(count - 1)]
-    upward = [(i, i + 1) for i in range(count - 1)]
+    downward = [(i + 1, i) for i in range(1, count - 1, 2)]
+    upward = [(i, i + 1) for i in range(1, count - 1, 2)]
 
     def shift(value, route):
         return lax.ppermute(value, "snp", route)
@@ -338,20 +364,19 @@
         return call(kernel, out, *args, **rest)
 
     down = shift(warm_start, downward)
-    high_n, low_n, cross = run(
-        begin_odd_kernel, [matrix, matrix, field], next_block, warm_start,
-        spaces={0: pltpu.HBM}, scratch=copies, flops=work,
+    places = {0: pltpu.HBM, 1: pltpu.HBM, 2: pltpu.HBM}
+    high_n, low_n, high_l, low_l, cross, own = run(
+        begin_odd_kernel, [matrix, matrix, matrix, matrix, field, field], next_block, local_block, warm_start,
+        spaces=places, scratch=copies, flops=work,
     )
     up = shift(cross, upward)
-    high_n, low_n, pair = run(
-        begin_even_kernel, [matrix, matrix, field], next_block, warm_start, high_n, low_n,
-        spaces={0: pltpu.HBM}, scratch=copies, aliases={2: 0, 3: 1}, flops=work,
+    high_n, low_n, high_l, low_l, own, pair = run(
+        begin_even_kernel, [matrix, matrix, matrix, matrix, field, field],
+        next_block, local_block, warm_start, high_n, low_n, high_l, low_l, own,
+        spaces=places, scratch=copies, aliases={3: 0, 4: 1, 5: 2, 6: 3, 7: 4}, flops=work,
     )
     got_pair = shift(pair, on_chip)
-    high_l, low_l, own, ridge = run(
-        local_kernel, [matrix, matrix, field, table],
-        local_block, warm_start, marginal, shrinkage.reshape(1, traits), flops=work,
-    )
+    own, ridge = run(rest_kernel, [field, table], own, warm_start, marginal, shrinkage.reshape(1, traits), flops=work)
     flipped = run(flip_kernel, [matrix, matrix], high_n, low_n, flops=work)
     sign = -1.0
     fields, tables = [], []

time: 68 us -> 67.7 us (level)
  starting transfers between devices: 29 us -> 33.4 us
  waiting for transfers between devices: 3.3 us -> 0.03 us
  Pallas kernels: 15.8 us -> 13.9 us
  blocking collectives: 17.1 us -> 19 us
  local copies, waits for them, and re-layouts: 1.39 us -> 0.16 us
    ppermute x12, starting transfers between devices: 29 us -> 33.4 us  [shift(): return lax.ppermute(value, 'snp', route)]
    ppermute x12, waiting for transfers between devices: 3.3 us -> 0.03 us  [shift(): return lax.ppermute(value, 'snp', route)]
    pallas_call x23, Pallas kernels: 15.8 us -> 13.9 us  [call(): pl.pallas_call(kernel, out_shape=[make(shape, dtype) for shape, dtype in...]
    all_to_all x1, blocking collectives: 17.1 us -> 19 us  [on_device(): moments = lax.all_to_all(moments, 'snp', 0, 0)]
    unnamed x6, local copies, waits for them, and re-layouts: 1.39 us -> 0.16 us
  transfers between devices with their start and end apart: 12 -> 12, of which waited for: 1 -> 0; matrix products, arithmetic and copies ran while one was open for 0% -> 0% of each run, Pallas kernels for 12% -> 9%
where the time goes in v4:
time: 67.7 us; the launch traced here: 67.4 us
  starting transfers between devices  33.4 us (49%)
  blocking collectives  19 us (28%)
  Pallas kernels  13.9 us (21%)
  between operations  0.93 us (1%)
    ppermute x12, starting transfers between devices, shift(): return lax.ppermute(value, 'snp', route)  33.4 us
    all_to_all x1, blocking collectives, on_device(): moments = lax.all_to_all(moments, 'snp', 0, 0)  19 us
    pallas_call x23, Pallas kernels, call(): pl.pallas_call(kernel, out_shape=[make(shape, dtype) for shape, dtype in...  13.9 us
  transfers between devices with their start and end apart: 12, of which 0 were waited for; matrix products, arithmetic and copies ran while one was open for 0% of the time, Pallas kernels for 9%

profile of v4, /device:TPU:0, one launch (start us, length us, event | category | flops | bytes accessed | tf_op | source)
XLA Modules:
  0.0 67.4 jit_solution(13939105082417583152)
XLA Ops:
  0.6 2.7 %shard_map.68 = (bf16[1024,1024]{1,0:T(8,128)(2,1)S(1)}, bf16[1024,1024]{1,0:T(8,128)(2,1)S(1)}, bf16[1024,1024]{1,0:T(8,128)(2,1)S(1)}, bf16[1024,1024]{1,0:T(8...) custom-call(f32[1024,1024]{1,0:T(8,128)} %next_ref.3, f32[1024,1024]{1,0:T(8,128)} %local_ref.3, ...), custom_call_target="tpu_custom_call" | custom-call | flops 402653184 | tf_op jit(solution)/shard_map/pallas_call | solution.py:332
  3.3 2.2 %shard_map.69 = (bf16[1024,1024]{1,0:T(8,128)(2,1)S(1)}, bf16[1024,1024]{1,0:T(8,128)(2,1)S(1)}, bf16[1024,1024]{1,0:T(8,128)(2,1)S(1)}, bf16[1024,1024]{1,0:T(8...) custom-call(f32[1024,1024]{1,0:T(8,128)} %next_ref.3, ...), custom_call_target="tpu_custom_call", output_to_operand_aliasing={{0}: (3, {}), {1}: (4, {}), {2}: (5, {}), {3}: (6, {}), {4}... | custom-call | flops 402653184 | tf_op jit(solution)/shard_map/pallas_call | solution.py:332
  5.5 0.6 collective-permute-start
  6.1 0.7 collective-permute-start.2
  6.8 0.7 %collective-permute-start.1 = (f32[64,1024]{1,0:T(8,128)S(1)}, f32[64,1024]{1,0:T(8,128)S(1)}, u32[]{:S(2)}, u32[]{:S(2)}) collective-permute-start(f32[64,1024]{1,0:T(8,128)S(1)} %get-tuple-element.48), channel_id=1, source_target_pairs={{1,2},{3,4},{5,6},{7,8},{9,10},{11,12},{13,14},{17,18},{19,20},{21... | collective-permute-start | bytes 786440 | tf_op jit(solution)/shard_map/ppermute | solution.py:361
  7.5 0.0 copy-start.1
  7.5 0.8 %shard_map.71 = (bf16[1024,1024]{1,0:T(8,128)(2,1)S(1)}, bf16[1024,1024]{1,0:T(8,128)(2,1)S(1)}) custom-call(bf16[1024,1024]{1,0:T(8,128)(2,1)S(1)} %get-tuple-element.44.high_in, bf16[1024,1024]{1,0:T(8,128)(2,1)S(1)} %get-tuple-element.45.low_in), custom_call_target="tpu_custom_call" | custom-call | flops 402653184 | tf_op jit(solution)/shard_map/pallas_call | solution.py:332
  8.3 0.1 copy-done.1
  8.4 0.1 shard_map.70
  8.5 0.6 shard_map.72.base_ref
  9.2 0.6 shard_map.75
  9.8 8.4 %collective-permute-start.3 = (f32[64,1024]{1,0:T(8,128)S(1)}, f32[64,1024]{1,0:T(8,128)S(1)}, u32[]{:S(2)}, u32[]{:S(2)}) collective-permute-start(f32[64,1024]{1,0:T(8,128)S(1)} %get-tuple-element.55), channel_id=1, source_target_pairs={{0,1},{1,0},{2,3},{3,2},{4,5},{5,4},{6,7},{7,6},{8,9},{9,8},{10,11... | collective-permute-start | bytes 786440 | tf_op jit(solution)/shard_map/ppermute | solution.py:361
  18.2 0.7 collective-permute-start.4
  18.8 0.7 %collective-permute-start.5 = (f32[64,1024]{1,0:T(8,128)S(1)}, f32[64,1024]{1,0:T(8,128)S(1)}, u32[]{:S(2)}, u32[]{:S(2)}) collective-permute-start(f32[64,1024]{1,0:T(8,128)S(1)} %shard_map.74.even_ref), channel_id=1, source_target_pairs={{2,1},{4,3},{6,5},{8,7},{10,9},{12,11},{14,13},{18,17},{20,19},{22... | collective-permute-start | bytes 786440 | tf_op jit(solution)/shard_map/ppermute | solution.py:361
  19.5 0.8 %shard_map.76 = (f32[64,1024]{1,0:T(8,128)S(1)}, f32[64,128]{1,0:T(8,128)S(1)}) custom-call(f32[64,1024]{1,0:T(8,128)S(1)} %get-tuple-element.51.field_ref.before_ref.zero_ref, bf16[1024,1024]{1,0:T(8,128)(2,1)S(1)} %get-tuple-element.52.high_ref, bf16[1024,1024]{1,0:T(8,128)(2,1)S(1)} %get-tuple-element.53.low_ref), custom_call_target="tpu_custom_call" | custom-call | flops 402653184 | tf_op jit(solution)/shard_map/pallas_call | solution.py:332
  20.3 0.6 shard_map.77.base_ref
  21.0 0.6 shard_map.80
  21.5 10.5 %collective-permute-start.6 = (f32[64,1024]{1,0:T(8,128)S(1)}, f32[64,1024]{1,0:T(8,128)S(1)}, u32[]{:S(2)}, u32[]{:S(2)}) collective-permute-start(f32[64,1024]{1,0:T(8,128)S(1)} %get-tuple-element.60), channel_id=1, source_target_pairs={{0,1},{1,0},{2,3},{3,2},{4,5},{5,4},{6,7},{7,6},{8,9},{9,8},{10,11... | collective-permute-start | bytes 786440 | tf_op jit(solution)/shard_map/ppermute | solution.py:361
  32.0 0.7 collective-permute-start.8
  32.7 0.7 %collective-permute-start.7 = (f32[64,1024]{1,0:T(8,128)S(1)}, f32[64,1024]{1,0:T(8,128)S(1)}, u32[]{:S(2)}, u32[]{:S(2)}) collective-permute-start(f32[64,1024]{1,0:T(8,128)S(1)} %get-tuple-element.61), channel_id=1, source_target_pairs={{1,2},{3,4},{5,6},{7,8},{9,10},{11,12},{13,14},{17,18},{19,20},{21... | collective-permute-start | bytes 786440 | tf_op jit(solution)/shard_map/ppermute | solution.py:361
  33.4 0.8 %shard_map.81 = (f32[64,1024]{1,0:T(8,128)S(1)}, f32[64,128]{1,0:T(8,128)S(1)}) custom-call(f32[64,1024]{1,0:T(8,128)S(1)} %get-tuple-element.51.field_ref.before_ref.zero_ref, f32[64,1024]{1,0:T(8,128)S(1)} %get-tuple-element.58.field_ref.before_ref.one_ref, bf16[1024,1024]{1,0:T(8,128)(2,1)S(1)} %get-tuple-element.52.high_ref, ...), custom_call_target="tpu_custom_call" | custom-call | flops 402653184 | tf_op jit(solution)/shard_map/pallas_call | solution.py:332
  34.2 0.6 shard_map.82.base_ref
  34.8 0.6 shard_map.85
  35.4 8.6 %collective-permute-start.9 = (f32[64,1024]{1,0:T(8,128)S(1)}, f32[64,1024]{1,0:T(8,128)S(1)}, u32[]{:S(2)}, u32[]{:S(2)}) collective-permute-start(f32[64,1024]{1,0:T(8,128)S(1)} %get-tuple-element.65), channel_id=1, source_target_pairs={{0,1},{1,0},{2,3},{3,2},{4,5},{5,4},{6,7},{7,6},{8,9},{9,8},{10,11... | collective-permute-start | bytes 786440 | tf_op jit(solution)/shard_map/ppermute | solution.py:361
  44.0 0.7 collective-permute-start.10
  44.6 0.7 %collective-permute-start.11 = (f32[64,1024]{1,0:T(8,128)S(1)}, f32[64,1024]{1,0:T(8,128)S(1)}, u32[]{:S(2)}, u32[]{:S(2)}) collective-permute-start(f32[64,1024]{1,0:T(8,128)S(1)} %shard_map.84.even_ref), channel_id=1, source_target_pairs={{2,1},{4,3},{6,5},{8,7},{10,9},{12,11},{14,13},{18,17},{20,19},{22... | collective-permute-start | bytes 786440 | tf_op jit(solution)/shard_map/ppermute | solution.py:361
  45.3 0.8 %shard_map.86 = (f32[64,1024]{1,0:T(8,128)S(1)}, f32[64,128]{1,0:T(8,128)S(1)}) custom-call(f32[64,1024]{1,0:T(8,128)S(1)} %get-tuple-element.58.field_ref.before_ref.one_ref, f32[64,1024]{1,0:T(8,128)S(1)} %get-tuple-element.63.field_ref.two_ref, bf16[1024,1024]{1,0:T(8,128)(2,1)S(1)} %get-tuple-element.52.high_ref, ...), custom_call_target="tpu_custom_call" | custom-call | flops 402653184 | tf_op jit(solution)/shard_map/pallas_call | solution.py:332
  46.1 0.6 shard_map.87.base_ref
  46.7 0.2 shard_map.88
  46.9 19.0 %all_to_all.5.table_ref = f32[16,8,128]{2,1,0:T(8,128)S(1)} all-to-all(f32[16,8,128]{2,1,0:T(8,128)S(1)} %shard_map.88), channel_id=1, replica_groups=mesh['parts'=2,'snp'=16] {'snp'}, dimensions={0} | all-to-all | bytes 131072 | tf_op jit(solution)/shard_map/all_to_all | solution.py:410
  66.0 0.4 shard_map.89.weights_ref
  66.4 1.0 %shard_map.90 = (f32[64,1024]{1,0:T(8,128)}, f32[64,1024]{1,0:T(8,128)}) custom-call(f32[64,128]{1,0:T(8,128)S(1)} %shard_map.89.weights_ref, f32[64,1024]{1,0:T(8,128)S(1)} %copy-done, f32[64,1024]{1,0:T(8,128)S(1)} %get-tuple-element.51.field_ref.before_ref.zero_ref, f32[64,1024]{1,0:T(8,128)S(1)} %get-tuple-element.58.field_ref.before_ref.one_ref, ...), custom_call_target="tpu_custom_call" | custom-call | tf_op jit(solution)/shard_map/pallas_call | solution.py:332
  (22 shorter events, 0.2 us)
Async XLA Ops:
  3.3 2.8 %copy-start = (f32[64,1024]{1,0:T(8,128)S(1)}, f32[64,1024]{1,0:T(8,128)}, u32[]{:S(2)}) copy-start(f32[64,1024]{1,0:T(8,128)} %start_ref.7) | copy-start | bytes 786436
  5.5 3.0 %collective-permute-start = (f32[64,1024]{1,0:T(8,128)S(1)}, f32[64,1024]{1,0:T(8,128)S(1)}, u32[]{:S(2)}, u32[]{:S(2)}) collective-permute-start(f32[64,1024]{1,0:T(8,128)S(1)} %get-tuple-element.43), channel_id=1, source_target_pairs={{0,1},{1,0},{2,3},{3,2},{4,5},{5,4},{6,7},{7,6},{8,9},{9,8},{10,11... | collective-permute-start | bytes 786440 | tf_op jit(solution)/shard_map/ppermute | solution.py:361
  6.1 3.0 %collective-permute-start.2 = (f32[64,1024]{1,0:T(8,128)S(1)}, f32[64,1024]{1,0:T(8,128)S(1)}, u32[]{:S(2)}, u32[]{:S(2)}) collective-permute-start(f32[64,1024]{1,0:T(8,128)S(1)} %copy-done), channel_id=1, source_target_pairs={{2,1},{4,3},{6,5},{8,7},{10,9},{12,11},{14,13},{18,17},{20,19},{22... | collective-permute-start | bytes 786440 | tf_op jit(solution)/shard_map/ppermute | solution.py:361
  6.8 2.4 %collective-permute-start.1 = (f32[64,1024]{1,0:T(8,128)S(1)}, f32[64,1024]{1,0:T(8,128)S(1)}, u32[]{:S(2)}, u32[]{:S(2)}) collective-permute-start(f32[64,1024]{1,0:T(8,128)S(1)} %get-tuple-element.48), channel_id=1, source_target_pairs={{1,2},{3,4},{5,6},{7,8},{9,10},{11,12},{13,14},{17,18},{19,20},{21... | collective-permute-start | bytes 786440 | tf_op jit(solution)/shard_map/ppermute | solution.py:361
  7.5 1.0 %copy-start.1 = (f32[64,1024]{1,0:T(8,128)S(1)}, f32[64,1024]{1,0:T(8,128)}, u32[]{:S(2)}) copy-start(f32[64,1024]{1,0:T(8,128)} %marginal_ref.1) | copy-start | bytes 786436
  7.5 0.9 %copy-start.2 = (f32[64,1]{0,1:T(1,128)S(1)}, f32[64,1]{0,1:T(1,128)}, u32[]{:S(2)}) copy-start(f32[64,1]{0,1:T(1,128)} %param.7) | copy-start | bytes 772
  9.8 10.6 %collective-permute-start.3 = (f32[64,1024]{1,0:T(8,128)S(1)}, f32[64,1024]{1,0:T(8,128)S(1)}, u32[]{:S(2)}, u32[]{:S(2)}) collective-permute-start(f32[64,1024]{1,0:T(8,128)S(1)} %get-tuple-element.55), channel_id=1, source_target_pairs={{0,1},{1,0},{2,3},{3,2},{4,5},{5,4},{6,7},{7,6},{8,9},{9,8},{10,11... | collective-permute-start | bytes 786440 | tf_op jit(solution)/shard_map/ppermute | solution.py:361
  18.2 2.7 %collective-permute-start.4 = (f32[64,1024]{1,0:T(8,128)S(1)}, f32[64,1024]{1,0:T(8,128)S(1)}, u32[]{:S(2)}, u32[]{:S(2)}) collective-permute-start(f32[64,1024]{1,0:T(8,128)S(1)} %get-tuple-element.56), channel_id=1, source_target_pairs={{1,2},{3,4},{5,6},{7,8},{9,10},{11,12},{13,14},{17,18},{19,20},{21... | collective-permute-start | bytes 786440 | tf_op jit(solution)/shard_map/ppermute | solution.py:361
  18.8 2.1 %collective-permute-start.5 = (f32[64,1024]{1,0:T(8,128)S(1)}, f32[64,1024]{1,0:T(8,128)S(1)}, u32[]{:S(2)}, u32[]{:S(2)}) collective-permute-start(f32[64,1024]{1,0:T(8,128)S(1)} %shard_map.74.even_ref), channel_id=1, source_target_pairs={{2,1},{4,3},{6,5},{8,7},{10,9},{12,11},{14,13},{18,17},{20,19},{22... | collective-permute-start | bytes 786440 | tf_op jit(solution)/shard_map/ppermute | solution.py:361
  21.5 12.6 %collective-permute-start.6 = (f32[64,1024]{1,0:T(8,128)S(1)}, f32[64,1024]{1,0:T(8,128)S(1)}, u32[]{:S(2)}, u32[]{:S(2)}) collective-permute-start(f32[64,1024]{1,0:T(8,128)S(1)} %get-tuple-element.60), channel_id=1, source_target_pairs={{0,1},{1,0},{2,3},{3,2},{4,5},{5,4},{6,7},{7,6},{8,9},{9,8},{10,11... | collective-permute-start | bytes 786440 | tf_op jit(solution)/shard_map/ppermute | solution.py:361
  32.0 2.7 %collective-permute-start.8 = (f32[64,1024]{1,0:T(8,128)S(1)}, f32[64,1024]{1,0:T(8,128)S(1)}, u32[]{:S(2)}, u32[]{:S(2)}) collective-permute-start(f32[64,1024]{1,0:T(8,128)S(1)} %shard_map.78.after_ref.even_ref), channel_id=1, source_target_pairs={{2,1},{4,3},{6,5},{8,7},{10,9},{12,11},{14,13},{18,17},{20,19},{22... | collective-permute-start | bytes 786440 | tf_op jit(solution)/shard_map/ppermute | solution.py:361
  32.7 2.1 %collective-permute-start.7 = (f32[64,1024]{1,0:T(8,128)S(1)}, f32[64,1024]{1,0:T(8,128)S(1)}, u32[]{:S(2)}, u32[]{:S(2)}) collective-permute-start(f32[64,1024]{1,0:T(8,128)S(1)} %get-tuple-element.61), channel_id=1, source_target_pairs={{1,2},{3,4},{5,6},{7,8},{9,10},{11,12},{13,14},{17,18},{19,20},{21... | collective-permute-start | bytes 786440 | tf_op jit(solution)/shard_map/ppermute | solution.py:361
  35.4 10.7 %collective-permute-start.9 = (f32[64,1024]{1,0:T(8,128)S(1)}, f32[64,1024]{1,0:T(8,128)S(1)}, u32[]{:S(2)}, u32[]{:S(2)}) collective-permute-start(f32[64,1024]{1,0:T(8,128)S(1)} %get-tuple-element.65), channel_id=1, source_target_pairs={{0,1},{1,0},{2,3},{3,2},{4,5},{5,4},{6,7},{7,6},{8,9},{9,8},{10,11... | collective-permute-start | bytes 786440 | tf_op jit(solution)/shard_map/ppermute | solution.py:361
  44.0 2.7 %collective-permute-start.10 = (f32[64,1024]{1,0:T(8,128)S(1)}, f32[64,1024]{1,0:T(8,128)S(1)}, u32[]{:S(2)}, u32[]{:S(2)}) collective-permute-start(f32[64,1024]{1,0:T(8,128)S(1)} %get-tuple-element.66), channel_id=1, source_target_pairs={{1,2},{3,4},{5,6},{7,8},{9,10},{11,12},{13,14},{17,18},{19,20},{21... | collective-permute-start | bytes 786440 | tf_op jit(solution)/shard_map/ppermute | solution.py:361
  44.6 21.7 %collective-permute-start.11 = (f32[64,1024]{1,0:T(8,128)S(1)}, f32[64,1024]{1,0:T(8,128)S(1)}, u32[]{:S(2)}, u32[]{:S(2)}) collective-permute-start(f32[64,1024]{1,0:T(8,128)S(1)} %shard_map.84.even_ref), channel_id=1, source_target_pairs={{2,1},{4,3},{6,5},{8,7},{10,9},{12,11},{14,13},{18,17},{20,19},{22... | collective-permute-start | bytes 786440 | tf_op jit(solution)/shard_map/ppermute | solution.py:361

commit v5 on v4

--- a/solution.py
+++ b/solution.py
@@ -115,23 +115,17 @@
         out_ref[...] = done if start == 0 else out_ref[...] + done
 
 
-def begin_odd_kernel(
-    next_ref, local_ref, start_ref, high_n, low_n, high_l, low_l, cross_ref, own_ref, raw, field, sems
-):
+def begin_odd_kernel(next_ref, start_ref, high_n, low_n, cross_ref, raw, field, sems):
     @pl.when(is_odd())
     def _():
         take_next(next_ref, start_ref, high_n, low_n, cross_ref, raw, field, sems)
 
-    @pl.when(jnp.logical_not(is_odd()))
-    def _():
-        take_local(local_ref, start_ref, high_l, low_l, own_ref, raw, field, sems)
-
 
 def begin_even_kernel(
-    next_ref, local_ref, start_ref, high_n_in, low_n_in, high_l_in, low_l_in, own_in,
+    next_ref, local_ref, start_ref, high_n_in, low_n_in,
     high_n, low_n, high_l, low_l, own_ref, pair_ref, raw, field, sems,
 ):
-    del high_n_in, low_n_in, high_l_in, low_l_in, own_in
+    del high_n_in, low_n_in
 
     @pl.when(is_odd())
     def _():
@@ -143,7 +137,7 @@
         take_next(next_ref, start_ref, high_n, low_n, pair_ref, raw, field, sems)
 
 
-def flip_kernel(high_in, low_in, high_ref, low_ref):
+def flip(high_in, low_in, high_ref, low_ref):
     size = high_in.shape[0]
     tile = tile_of(size)
     for row in range(0, size, tile):
@@ -153,12 +147,38 @@
             low_ref[target] = jnp.transpose(low_in[source])
 
 
-def rest_kernel(own_ref, start_ref, marginal_ref, shrinkage_ref, rest_ref, shift_ref):
-    traits = start_ref.shape[0]
+def ridge_column(shrinkage_ref):
+    traits = shrinkage_ref.shape[1]
     here = lax.broadcasted_iota(jnp.int32, (traits, traits), 0) == lax.broadcasted_iota(jnp.int32, (traits, traits), 1)
-    shift = 1.0 + jnp.sum(jnp.where(here, shrinkage_ref[...], 0.0), axis=1, keepdims=True)
-    shift_ref[...] = jnp.broadcast_to(shift, shift_ref.shape)
-    rest_ref[...] = marginal_ref[...] - shift * start_ref[...] - own_ref[...]
+    return 1.0 + jnp.sum(jnp.where(here, shrinkage_ref[...], 0.0), axis=1, keepdims=True)
+
+
+def prepare_odd_kernel(own_ref, start_ref, marginal_ref, shrinkage_ref, high_n, low_n, rest_ref, high_up, low_up):
+    @pl.when(is_odd())
+    def _():
+        rest_ref[...] = marginal_ref[...] - ridge_column(shrinkage_ref) * start_ref[...] - own_ref[...]
+        flip(high_n, low_n, high_up, low_up)
+
+
+def prepare_even_kernel(
+    local_ref, start_ref, marginal_ref, shrinkage_ref, got_pair_ref, high_n, low_n,
+    high_l_in, low_l_in, high_up_in, low_up_in, after_ref,
+    high_l, low_l, high_up, low_up, base_ref, raw, field, sems,
+):
+    del high_l_in, low_l_in, high_up_in, low_up_in, after_ref
+
+    @pl.when(jnp.logical_not(is_odd()))
+    def _():
+        flip(high_n, low_n, high_up, low_up)
+        take_local(local_ref, start_ref, high_l, low_l, base_ref, raw, field, sems)
+        base_ref[...] = marginal_ref[...] - ridge_column(shrinkage_ref) * field[...] - base_ref[...]
+        tile = tile_of(base_ref.shape[1])
+
+        def store(start, part):
+            cols = pl.ds(start, tile)
+            base_ref[:, cols] = base_ref[:, cols] - part
+
+        forward(stacked(got_pair_ref[...]), high_up, low_up, store)
 
 
 def moment(left, right):
@@ -173,40 +193,36 @@
     moments_ref[...] = jnp.where(lane == 0, moment(field, field), jnp.where(lane == 1, cross, 0.0))
 
 
-def pair_kernel(sign, own_ref, got_pair_ref, high_up, low_up, base_ref):
-    @pl.when(is_odd())
-    def _():
-        base_ref[...] = own_ref[...] + sign * got_pair_ref[...]
-
+def pair_kernel(own_ref, got_pair_ref, high_up, low_up, base_ref):
     @pl.when(jnp.logical_not(is_odd()))
     def _():
         tile = tile_of(own_ref.shape[1])
 
         def store(start, part):
             cols = pl.ds(start, tile)
-            base_ref[:, cols] = own_ref[:, cols] + sign * part
+            base_ref[:, cols] = own_ref[:, cols] + part
 
         forward(stacked(got_pair_ref[...]), high_up, low_up, store)
 
 
-def even_kernel(sign, base_ref, got_ref, after_ref, field_ref):
+def even_kernel(base_ref, got_ref, after_ref, field_ref):
     del after_ref
 
     @pl.when(jnp.logical_not(is_odd()))
     def _():
-        field_ref[...] = base_ref[...] + sign * got_ref[...]
-
-
-def odd_kernel(sign, base_ref, got_ref, high_in, low_in, high_up, low_up, after_ref, field_ref, cross_ref):
+        field_ref[...] = base_ref[...] + got_ref[...]
+
+
+def odd_kernel(sign, own_ref, got_pair_ref, got_ref, high_in, low_in, high_up, low_up, after_ref, field_ref, cross_ref):
     del after_ref
 
     @pl.when(is_odd())
     def _():
-        tile = tile_of(base_ref.shape[1])
+        tile = tile_of(own_ref.shape[1])
 
         def keep(start, part):
             cols = pl.ds(start, tile)
-            field_ref[:, cols] = base_ref[:, cols] + sign * part
+            field_ref[:, cols] = own_ref[:, cols] + sign * (got_pair_ref[:, cols] + part)
 
         def send(start, part):
             cross_ref[:, pl.ds(start, tile)] = part
@@ -215,6 +231,15 @@
         coupling(stacked(field_ref[...]), high_in, low_in, send)
 
 
+def couple_even(field_ref, high_in, low_in, pair_ref):
+    tile = tile_of(field_ref.shape[1])
+
+    def send(start, part):
+        pair_ref[:, pl.ds(start, tile)] = part
+
+    coupling(stacked(field_ref[...]), high_in, low_in, send)
+
+
 def merge_kernel(even_ref, odd_ref, high_in, low_in, field_ref, pair_ref):
     @pl.when(is_odd())
     def _():
@@ -223,17 +248,23 @@
 
     @pl.when(jnp.logical_not(is_odd()))
     def _():
-        tile = tile_of(even_ref.shape[1])
-
-        def send(start, part):
-            pair_ref[:, pl.ds(start, tile)] = part
-
         field_ref[...] = even_ref[...]
-        coupling(stacked(even_ref[...]), high_in, low_in, send)
-
-
-def reduce_kernel(field_ref, own_ref, got_pair_ref, got_up_ref, base_ref, one_ref, two_ref, three_ref, out_ref):
-    del base_ref
+        couple_even(field_ref, high_in, low_in, pair_ref)
+
+
+def join_kernel(sign, base_ref, got_ref, odd_ref, high_in, low_in, field_ref, pair_ref):
+    @pl.when(is_odd())
+    def _():
+        field_ref[...] = odd_ref[...]
+        pair_ref[...] = odd_ref[...]
+
+    @pl.when(jnp.logical_not(is_odd()))
+    def _():
+        field_ref[...] = base_ref[...] + sign * got_ref[...]
+        couple_even(field_ref, high_in, low_in, pair_ref)
+
+
+def reduce_kernel(field_ref, own_ref, got_pair_ref, got_up_ref, one_ref, two_ref, three_ref, out_ref):
     traits = field_ref.shape[0]
     lower = jnp.where(is_odd(), got_pair_ref[...], got_up_ref[...])
     last = moment(field_ref[...], own_ref[...] + 2.0 * lower)
@@ -283,42 +314,37 @@
     return gain, residual
 
 
-def weights_kernel(table_ref, shift_ref, weights_ref):
-    traits = shift_ref.shape[0]
+def weights_kernel(table_ref, shrinkage_ref, weights_ref):
     sums = jnp.sum(table_ref[...], axis=0)
-    square = jnp.concatenate([sums, jnp.zeros((sums.shape[1] - MOMENT_ROWS, sums.shape[1]), F32)], axis=0)
-    columns = jnp.transpose(square)[:traits]
-    moments = [columns[:, i : i + 1] for i in range(2 * ITERS)]
-    gain, residual = coefficients(moments, shift_ref[:, 0:1])
-    lane = lax.broadcasted_iota(jnp.int32, (traits, 128), 1)
-    table = jnp.zeros((traits, 128), F32)
+    traits, lanes = weights_ref.shape[0], sums.shape[1]
+    shift = 1.0 + shrinkage_ref[...]
+    moments = [sums[i : i + 1, :traits] for i in range(2 * ITERS)]
+    gain, residual = coefficients(moments, shift)
+    row = lax.broadcasted_iota(jnp.int32, (lanes, traits), 0)
+    table = jnp.zeros((lanes, traits), F32)
     for index, part in enumerate(gain + residual):
-        table = jnp.where(lane == index, part, table)
-    weights_ref[...] = table
+        table = jnp.where(row == index, part, table)
+    weights_ref[...] = jnp.transpose(table)
 
 
 def final_kernel(
-    weights_ref, start_ref, zero_ref, one_ref, two_ref, base_ref, got_down_ref, got_up_ref, high_up, low_up,
-    solution_ref, residual_ref,
+    weights_ref, start_ref, zero_ref, one_ref, two_ref, own_ref, got_pair_ref, got_down_ref, got_up_ref,
+    high_up, low_up, solution_ref, residual_ref,
 ):
-    tile = tile_of(base_ref.shape[1])
+    tile = tile_of(own_ref.shape[1])
     weights = [weights_ref[:, i : i + 1] for i in range(2 * ITERS + 1)]
     gain, residual = weights[:ITERS], weights[ITERS:]
+    odd = is_odd()
+    upper = jnp.where(odd, got_down_ref[...], got_pair_ref[...])
+    lower = jnp.where(odd, got_pair_ref[...], got_up_ref[...])
     zero, one, two = zero_ref[...], one_ref[...], two_ref[...]
     solution_ref[...] = start_ref[...] + gain[0] * zero + gain[1] * one + gain[2] * two
-    residual_ref[...] = residual[0] * zero + residual[1] * one + residual[2] * two + residual[3] * base_ref[...]
-
-    @pl.when(is_odd())
-    def _():
-        def store(start, part):
-            cols = pl.ds(start, tile)
-            residual_ref[:, cols] = residual_ref[:, cols] + residual[3] * part
-
-        forward(stacked(got_down_ref[...]), high_up, low_up, store)
-
-    @pl.when(jnp.logical_not(is_odd()))
-    def _():
-        residual_ref[...] = residual_ref[...] + residual[3] * got_up_ref[...]
+    base = residual[0] * zero + residual[1] * one + residual[2] * two + residual[3] * (own_ref[...] + lower)
+
+    def store(start, part):
+        residual_ref[:, pl.ds(start, tile)] = base[:, start : start + tile] + residual[3] * part
+
+    forward(stacked(upper), high_up, low_up, store)
 
 
 def call(kernel, out, *args, spaces=None, scratch=(), limit=12, aliases=None, keep=True, flops=0):
@@ -363,56 +389,76 @@
     def run(kernel, out, *args, **rest):
         return call(kernel, out, *args, **rest)
 
+    hbm = pltpu.HBM
+    ridge = shrinkage.reshape(1, traits)
     down = shift(warm_start, downward)
-    places = {0: pltpu.HBM, 1: pltpu.HBM, 2: pltpu.HBM}
-    high_n, low_n, high_l, low_l, cross, own = run(
-        begin_odd_kernel, [matrix, matrix, matrix, matrix, field, field], next_block, local_block, warm_start,
-        spaces=places, scratch=copies, flops=work,
+    high_n, low_n, cross = run(
+        begin_odd_kernel, [matrix, matrix, field], next_block, warm_start,
+        spaces={0: hbm, 1: hbm}, scratch=copies, flops=work,
     )
     up = shift(cross, upward)
     high_n, low_n, high_l, low_l, own, pair = run(
         begin_even_kernel, [matrix, matrix, matrix, matrix, field, field],
-        next_block, local_block, warm_start, high_n, low_n, high_l, low_l, own,
-        spaces=places, scratch=copies, aliases={3: 0, 4: 1, 5: 2, 6: 3, 7: 4}, flops=work,
+        next_block, local_block, warm_start, high_n, low_n,
+        spaces={0: hbm, 1: hbm, 2: hbm}, scratch=copies, aliases={3: 0, 4: 1}, flops=work,
     )
     got_pair = shift(pair, on_chip)
-    own, ridge = run(rest_kernel, [field, table], own, warm_start, marginal, shrinkage.reshape(1, traits), flops=work)
-    flipped = run(flip_kernel, [matrix, matrix], high_n, low_n, flops=work)
-    sign = -1.0
-    fields, tables = [], []
-    for step in range(1, ITERS + 1):
-        (base,) = run(functools.partial(pair_kernel, sign), [field], own, got_pair, *flipped, flops=work)
-        even = functools.partial(even_kernel, sign)
-        odd = functools.partial(odd_kernel, sign)
-        if step % 2:
-            odd_field, cross = run(odd, [field, field], base, down, high_n, low_n, *flipped, ridge, flops=work)
-            next_up = shift(cross, upward)
-            (even_field,) = run(even, [field], base, up, odd_field, flops=work)
-            down = shift(even_field, downward)
-        else:
-            (even_field,) = run(even, [field], base, up, ridge, flops=work)
-            next_down = shift(even_field, downward)
-            odd_field, cross = run(odd, [field, field], base, down, high_n, low_n, *flipped, even_field, flops=work)
-            next_up = shift(cross, upward)
-            down = next_down
-        up = next_up
-        merged, pair = run(merge_kernel, [field, field], even_field, odd_field, high_n, low_n, flops=work)
+    rest, high_up, low_up = run(
+        prepare_odd_kernel, [field, matrix, matrix],
+        own, warm_start, marginal, ridge, high_n, low_n, flops=work,
+    )
+    odd = functools.partial(odd_kernel, -1.0)
+    odd_field, cross = run(odd, [field, field], rest, got_pair, down, high_n, low_n, high_up, low_up, ridge, flops=work)
+    next_up = shift(cross, upward)
+    high_l, low_l, high_up, low_up, base = run(
+        prepare_even_kernel, [matrix, matrix, matrix, matrix, field],
+        local_block, warm_start, marginal, ridge, got_pair, high_n, low_n,
+        high_l, low_l, high_up, low_up, odd_field,
+        spaces={0: hbm, 1: hbm}, scratch=copies, aliases={7: 0, 8: 1, 9: 2, 10: 3}, flops=work,
+    )
+    join = functools.partial(join_kernel, -1.0)
+    merged, pair = run(join, [field, field], base, up, odd_field, high_n, low_n, flops=work)
+    up = next_up
+    fields, tables = [merged], []
+    odd, join = functools.partial(odd_kernel, 1.0), functools.partial(join_kernel, 1.0)
+    for step in range(2, ITERS + 2):
         got_pair = shift(pair, on_chip)
-        before = fields[-1:]
+        if step % 2 == 0:
+            down = shift(merged, downward)
+        before = fields[-2:-1]
         kernel = own_kernel if before else functools.partial(own_kernel, None)
         own, part = run(kernel, [field, table], *before, merged, high_l, low_l, flops=work)
+        tables.append(part)
+        if step > ITERS:
+            break
+        (base,) = run(pair_kernel, [field], own, got_pair, high_up, low_up, flops=work)
+        if step % 2 == 0:
+            (even_field,) = run(even_kernel, [field], base, up, ridge, flops=work)
+            next_down = shift(even_field, downward)
+            odd_field, cross = run(
+                odd, [field, field],
+                own, got_pair, down, high_n, low_n, high_up, low_up, even_field, flops=work,
+            )
+            up = shift(cross, upward)
+            down = next_down
+            merged, pair = run(merge_kernel, [field, field], even_field, odd_field, high_n, low_n, flops=work)
+        else:
+            odd_field, cross = run(
+                odd, [field, field],
+                own, got_pair, down, high_n, low_n, high_up, low_up, base, flops=work,
+            )
+            next_up = shift(cross, upward)
+            merged, pair = run(join, [field, field], base, up, odd_field, high_n, low_n, flops=work)
+            up = next_up
         fields.append(merged)
-        tables.append(part)
-        sign = 1.0
-    (base,) = run(functools.partial(pair_kernel, sign), [field], own, got_pair, *flipped, flops=work)
     lanes = -(-traits // 128) * 128
-    (moments,) = run(reduce_kernel, [((count, MOMENT_ROWS, lanes), F32)], fields[-1], own, got_pair, up, base, *tables)
+    (moments,) = run(reduce_kernel, [((count, MOMENT_ROWS, lanes), F32)], fields[-1], own, got_pair, up, *tables)
     moments = lax.all_to_all(moments, "snp", 0, 0)
     (weights,) = run(weights_kernel, [table], moments, ridge)
     return tuple(
         run(
             final_kernel, [field, field],
-            weights, warm_start, *fields, base, down, up, *flipped,
+            weights, warm_start, *fields, own, got_pair, down, up, high_up, low_up,
             keep=False,
         )
     )

time: 67.7 us -> 65.5 us (0.968)
  starting transfers between devices: 33.4 us -> 31.2 us
  Pallas kernels: 13.9 us -> 13.1 us
    ppermute x12, starting transfers between devices: 33.4 us -> 31.2 us  [shift(): return lax.ppermute(value, 'snp', route)]
    pallas_call x23 -> x19, Pallas kernels: 13.9 us -> 13.1 us  [call(): pl.pallas_call(kernel, out_shape=[make(shape, dtype) for shape, dtype in...]
  transfers between devices with their start and end apart: 12 -> 12, of which waited for: 0 -> 1; matrix products, arithmetic and copies ran while one was open for 0% -> 0% of each run, Pallas kernels for 9% -> 15%
where the time goes in v5:
time: 65.5 us; the launch traced here: 65.2 us
  starting transfers between devices  31.2 us (48%)
  blocking collectives  19.4 us (30%)
  Pallas kernels  13.1 us (20%)
  between operations  0.94 us (1%)
    ppermute x12, starting transfers between devices, shift(): return lax.ppermute(value, 'snp', route)  31.2 us
    all_to_all x1, blocking collectives, on_device(): moments = lax.all_to_all(moments, 'snp', 0, 0)  19.4 us
    pallas_call x19, Pallas kernels, call(): pl.pallas_call(kernel, out_shape=[make(shape, dtype) for shape, dtype in...  13.1 us
  transfers between devices with their start and end apart: 12, of which 1 were waited for; matrix products, arithmetic and copies ran while one was open for 0% of the time, Pallas kernels for 15%

profile of v5, /device:TPU:0, one launch (start us, length us, event | category | flops | bytes accessed | tf_op | source)
XLA Modules:
  0.0 65.2 jit_solution(197575153660691694)
XLA Ops:
  0.6 0.7 %collective-permute-start.1 = (f32[64,1024]{1,0:T(8,128)}, f32[64,1024]{1,0:T(8,128)S(1)}, u32[]{:S(2)}, u32[]{:S(2)}) collective-permute-start(f32[64,1024]{1,0:T(8,128)} %start_ref.9), channel_id=1, source_target_pairs={{2,1},{4,3},{6,5},{8,7},{10,9},{12,11},{14,13},{18,17},{20,19},{22... | collective-permute-start | bytes 786440 | tf_op jit(solution)/shard_map/ppermute | solution.py:387
  1.3 0.1 shard_map.68
  1.4 0.0 copy-start
  1.4 0.0 copy-start.2
  1.4 0.0 copy-start.3
  1.4 2.2 %shard_map.69 = (bf16[1024,1024]{1,0:T(8,128)(2,1)S(1)}, bf16[1024,1024]{1,0:T(8,128)(2,1)S(1)}, bf16[1024,1024]{1,0:T(8,128)(2,1)S(1)}, bf16[1024,1024]{1,0:T(8...) custom-call(f32[1024,1024]{1,0:T(8,128)} %next_ref.3, ...), custom_call_target="tpu_custom_call", output_to_operand_aliasing={{0}: (3, {}), {1}: (4, {})} | custom-call | flops 402653184 | tf_op jit(solution)/shard_map/pallas_call | solution.py:358
  3.7 3.8 %collective-permute-start = (f32[64,1024]{1,0:T(8,128)S(1)}, f32[64,1024]{1,0:T(8,128)S(1)}, u32[]{:S(2)}, u32[]{:S(2)}) collective-permute-start(f32[64,1024]{1,0:T(8,128)S(1)} %get-tuple-element.39), channel_id=1, source_target_pairs={{0,1},{1,0},{2,3},{3,2},{4,5},{5,4},{6,7},{7,6},{8,9},{9,8},{10,11... | collective-permute-start | bytes 786440 | tf_op jit(solution)/shard_map/ppermute | solution.py:387
  7.4 0.7 %collective-permute-start.2 = (f32[64,1024]{1,0:T(8,128)S(1)}, f32[64,1024]{1,0:T(8,128)S(1)}, u32[]{:S(2)}, u32[]{:S(2)}) collective-permute-start(f32[64,1024]{1,0:T(8,128)S(1)} %get-tuple-element.50), channel_id=1, source_target_pairs={{1,2},{3,4},{5,6},{7,8},{9,10},{11,12},{13,14},{17,18},{19,20},{21... | collective-permute-start | bytes 786440 | tf_op jit(solution)/shard_map/ppermute | solution.py:387
  8.2 0.4 collective-permute-done.got_pair_ref
  8.6 3.8 %shard_map.72 = (bf16[1024,1024]{1,0:T(8,128)(2,1)S(1)}, bf16[1024,1024]{1,0:T(8,128)(2,1)S(1)}, bf16[1024,1024]{1,0:T(8,128)(2,1)S(1)}, bf16[1024,1024]{1,0:T(8,128)(2,1)S(1)}, f32[64,1024]{1,0:T(8,128)S(1)}) custom-call(f32[1024,1024]{1,0:T(8,128)} %local_ref.3, ...), custom_call_target="tpu_custom_call", output_to_operand_aliasing={{0}: (7, {}), {1}: (8, {}), {2}: (9, {}), {3}: (10, {})} | custom-call | flops 402653184 | tf_op jit(solution)/shard_map/pallas_call | solution.py:358
  12.4 0.6 shard_map.73
  13.0 2.2 %collective-permute-start.3 = (f32[64,1024]{1,0:T(8,128)S(1)}, f32[64,1024]{1,0:T(8,128)S(1)}, u32[]{:S(2)}, u32[]{:S(2)}) collective-permute-start(f32[64,1024]{1,0:T(8,128)S(1)} %get-tuple-element.55), channel_id=1, source_target_pairs={{0,1},{1,0},{2,3},{3,2},{4,5},{5,4},{6,7},{7,6},{8,9},{9,8},{10,11... | collective-permute-start | bytes 786440 | tf_op jit(solution)/shard_map/ppermute | solution.py:387
  15.2 0.7 %collective-permute-start.4 = (f32[64,1024]{1,0:T(8,128)S(1)}, f32[64,1024]{1,0:T(8,128)S(1)}, u32[]{:S(2)}, u32[]{:S(2)}) collective-permute-start(f32[64,1024]{1,0:T(8,128)S(1)} %get-tuple-element.58), channel_id=1, source_target_pairs={{1,2},{3,4},{5,6},{7,8},{9,10},{11,12},{13,14},{17,18},{19,20},{21... | collective-permute-start | bytes 786440 | tf_op jit(solution)/shard_map/ppermute | solution.py:387
  15.9 0.7 %collective-permute-start.5 = (f32[64,1024]{1,0:T(8,128)S(1)}, f32[64,1024]{1,0:T(8,128)S(1)}, u32[]{:S(2)}, u32[]{:S(2)}) collective-permute-start(f32[64,1024]{1,0:T(8,128)S(1)} %get-tuple-element.51.field_ref.before_ref.zero_ref), channel_id=1, source_target_pairs={{2,1},{4,3},{6,5},{8,7},{10,9},{12,11},{14,13},{18,17},{20,19},{22... | collective-permute-start | bytes 786440 | tf_op jit(solution)/shard_map/ppermute | solution.py:387
  16.5 0.8 %shard_map.74 = (f32[64,1024]{1,0:T(8,128)S(1)}, f32[64,128]{1,0:T(8,128)S(1)}) custom-call(f32[64,1024]{1,0:T(8,128)S(1)} %get-tuple-element.51.field_ref.before_ref.zero_ref, bf16[1024,1024]{1,0:T(8,128)(2,1)S(1)} %get-tuple-element.52.high_ref, bf16[1024,1024]{1,0:T(8,128)(2,1)S(1)} %get-tuple-element.53.low_ref), custom_call_target="tpu_custom_call" | custom-call | flops 402653184 | tf_op jit(solution)/shard_map/pallas_call | solution.py:358
  17.3 0.6 shard_map.75.base_ref
  18.0 0.6 shard_map.78
  18.6 10.4 %collective-permute-start.6 = (f32[64,1024]{1,0:T(8,128)S(1)}, f32[64,1024]{1,0:T(8,128)S(1)}, u32[]{:S(2)}, u32[]{:S(2)}) collective-permute-start(f32[64,1024]{1,0:T(8,128)S(1)} %get-tuple-element.62), channel_id=1, source_target_pairs={{0,1},{1,0},{2,3},{3,2},{4,5},{5,4},{6,7},{7,6},{8,9},{9,8},{10,11... | collective-permute-start | bytes 786440 | tf_op jit(solution)/shard_map/ppermute | solution.py:387
  29.0 0.7 %collective-permute-start.8 = (f32[64,1024]{1,0:T(8,128)S(1)}, f32[64,1024]{1,0:T(8,128)S(1)}, u32[]{:S(2)}, u32[]{:S(2)}) collective-permute-start(f32[64,1024]{1,0:T(8,128)S(1)} %shard_map.76.after_ref.even_ref), channel_id=1, source_target_pairs={{2,1},{4,3},{6,5},{8,7},{10,9},{12,11},{14,13},{18,17},{20,19},{22... | collective-permute-start | bytes 786440 | tf_op jit(solution)/shard_map/ppermute | solution.py:387
  29.7 0.7 %collective-permute-start.7 = (f32[64,1024]{1,0:T(8,128)S(1)}, f32[64,1024]{1,0:T(8,128)S(1)}, u32[]{:S(2)}, u32[]{:S(2)}) collective-permute-start(f32[64,1024]{1,0:T(8,128)S(1)} %get-tuple-element.63), channel_id=1, source_target_pairs={{1,2},{3,4},{5,6},{7,8},{9,10},{11,12},{13,14},{17,18},{19,20},{21... | collective-permute-start | bytes 786440 | tf_op jit(solution)/shard_map/ppermute | solution.py:387
  30.4 0.8 %shard_map.79 = (f32[64,1024]{1,0:T(8,128)S(1)}, f32[64,128]{1,0:T(8,128)S(1)}) custom-call(f32[64,1024]{1,0:T(8,128)S(1)} %get-tuple-element.51.field_ref.before_ref.zero_ref, f32[64,1024]{1,0:T(8,128)S(1)} %get-tuple-element.60.field_ref.before_ref.one_ref, bf16[1024,1024]{1,0:T(8,128)(2,1)S(1)} %get-tuple-element.52.high_ref, ...), custom_call_target="tpu_custom_call" | custom-call | flops 402653184 | tf_op jit(solution)/shard_map/pallas_call | solution.py:358
  31.2 0.6 shard_map.80.after_ref.base_ref
  31.8 0.6 shard_map.82
  32.3 9.3 %collective-permute-start.9 = (f32[64,1024]{1,0:T(8,128)S(1)}, f32[64,1024]{1,0:T(8,128)S(1)}, u32[]{:S(2)}, u32[]{:S(2)}) collective-permute-start(f32[64,1024]{1,0:T(8,128)S(1)} %get-tuple-element.67), channel_id=1, source_target_pairs={{0,1},{1,0},{2,3},{3,2},{4,5},{5,4},{6,7},{7,6},{8,9},{9,8},{10,11... | collective-permute-start | bytes 786440 | tf_op jit(solution)/shard_map/ppermute | solution.py:387
  41.7 0.7 %collective-permute-start.10 = (f32[64,1024]{1,0:T(8,128)S(1)}, f32[64,1024]{1,0:T(8,128)S(1)}, u32[]{:S(2)}, u32[]{:S(2)}) collective-permute-start(f32[64,1024]{1,0:T(8,128)S(1)} %get-tuple-element.68), channel_id=1, source_target_pairs={{1,2},{3,4},{5,6},{7,8},{9,10},{11,12},{13,14},{17,18},{19,20},{21... | collective-permute-start | bytes 786440 | tf_op jit(solution)/shard_map/ppermute | solution.py:387
  42.3 0.0 copy-start.1
  42.4 0.8 %collective-permute-start.11 = (f32[64,1024]{1,0:T(8,128)S(1)}, f32[64,1024]{1,0:T(8,128)S(1)}, u32[]{:S(2)}, u32[]{:S(2)}) collective-permute-start(f32[64,1024]{1,0:T(8,128)S(1)} %get-tuple-element.65.field_ref.two_ref), channel_id=1, source_target_pairs={{2,1},{4,3},{6,5},{8,7},{10,9},{12,11},{14,13},{18,17},{20,19},{22... | collective-permute-start | bytes 786440 | tf_op jit(solution)/shard_map/ppermute | solution.py:387
  43.2 0.8 %shard_map.83 = (f32[64,1024]{1,0:T(8,128)S(1)}, f32[64,128]{1,0:T(8,128)S(1)}) custom-call(f32[64,1024]{1,0:T(8,128)S(1)} %get-tuple-element.60.field_ref.before_ref.one_ref, f32[64,1024]{1,0:T(8,128)S(1)} %get-tuple-element.65.field_ref.two_ref, bf16[1024,1024]{1,0:T(8,128)(2,1)S(1)} %get-tuple-element.52.high_ref, ...), custom_call_target="tpu_custom_call" | custom-call | flops 402653184 | tf_op jit(solution)/shard_map/pallas_call | solution.py:358
  44.0 0.2 shard_map.84
  44.2 19.4 %all_to_all.5.table_ref = f32[16,8,128]{2,1,0:T(8,128)S(1)} all-to-all(f32[16,8,128]{2,1,0:T(8,128)S(1)} %shard_map.84), channel_id=1, replica_groups=mesh['parts'=2,'snp'=16] {'snp'}, dimensions={0} | all-to-all | bytes 131072 | tf_op jit(solution)/shard_map/all_to_all | solution.py:456
  63.6 0.2 shard_map.85.weights_ref
  63.8 1.4 %shard_map.86 = (f32[64,1024]{1,0:T(8,128)}, f32[64,1024]{1,0:T(8,128)}) custom-call(f32[64,128]{1,0:T(8,128)S(1)} %shard_map.85.weights_ref, f32[64,1024]{1,0:T(8,128)S(1)} %copy-done.1, f32[64,1024]{1,0:T(8,128)S(1)} %get-tuple-element.51.field_ref.before_ref.zero_ref, f32[64,1024]{1,0:T(8,128)S(1)} %get-tuple-element.60.field_ref.before_ref.one_ref, ...), custom_call_target="tpu_custom_call" | custom-call | tf_op jit(solution)/shard_map/pallas_call | solution.py:358
  (20 shorter events, 0.1 us)
Async XLA Ops:
  0.6 7.5 %collective-permute-start.1 = (f32[64,1024]{1,0:T(8,128)}, f32[64,1024]{1,0:T(8,128)S(1)}, u32[]{:S(2)}, u32[]{:S(2)}) collective-permute-start(f32[64,1024]{1,0:T(8,128)} %start_ref.9), channel_id=1, source_target_pairs={{2,1},{4,3},{6,5},{8,7},{10,9},{12,11},{14,13},{18,17},{20,19},{22... | collective-permute-start | bytes 786440 | tf_op jit(solution)/shard_map/ppermute | solution.py:387
  1.4 6.7 %copy-start = (f32[64,1024]{1,0:T(8,128)S(1)}, f32[64,1024]{1,0:T(8,128)}, u32[]{:S(2)}) copy-start(f32[64,1024]{1,0:T(8,128)} %start_ref.9) | copy-start | bytes 786436
  1.4 6.7 %copy-start.2 = (f32[64,1024]{1,0:T(8,128)S(1)}, f32[64,1024]{1,0:T(8,128)}, u32[]{:S(2)}) copy-start(f32[64,1024]{1,0:T(8,128)} %marginal_ref.3) | copy-start | bytes 786436
  1.4 6.7 %copy-start.3 = (f32[64,1]{0,1:T(1,128)S(1)}, f32[64,1]{0,1:T(1,128)}, u32[]{:S(2)}) copy-start(f32[64,1]{0,1:T(1,128)} %param.7) | copy-start | bytes 772
  3.7 4.9 %collective-permute-start = (f32[64,1024]{1,0:T(8,128)S(1)}, f32[64,1024]{1,0:T(8,128)S(1)}, u32[]{:S(2)}, u32[]{:S(2)}) collective-permute-start(f32[64,1024]{1,0:T(8,128)S(1)} %get-tuple-element.39), channel_id=1, source_target_pairs={{0,1},{1,0},{2,3},{3,2},{4,5},{5,4},{6,7},{7,6},{8,9},{9,8},{10,11... | collective-permute-start | bytes 786440 | tf_op jit(solution)/shard_map/ppermute | solution.py:387
  7.4 5.0 %collective-permute-start.2 = (f32[64,1024]{1,0:T(8,128)S(1)}, f32[64,1024]{1,0:T(8,128)S(1)}, u32[]{:S(2)}, u32[]{:S(2)}) collective-permute-start(f32[64,1024]{1,0:T(8,128)S(1)} %get-tuple-element.50), channel_id=1, source_target_pairs={{1,2},{3,4},{5,6},{7,8},{9,10},{11,12},{13,14},{17,18},{19,20},{21... | collective-permute-start | bytes 786440 | tf_op jit(solution)/shard_map/ppermute | solution.py:387
  13.0 4.3 %collective-permute-start.3 = (f32[64,1024]{1,0:T(8,128)S(1)}, f32[64,1024]{1,0:T(8,128)S(1)}, u32[]{:S(2)}, u32[]{:S(2)}) collective-permute-start(f32[64,1024]{1,0:T(8,128)S(1)} %get-tuple-element.55), channel_id=1, source_target_pairs={{0,1},{1,0},{2,3},{3,2},{4,5},{5,4},{6,7},{7,6},{8,9},{9,8},{10,11... | collective-permute-start | bytes 786440 | tf_op jit(solution)/shard_map/ppermute | solution.py:387
  15.2 2.7 %collective-permute-start.4 = (f32[64,1024]{1,0:T(8,128)S(1)}, f32[64,1024]{1,0:T(8,128)S(1)}, u32[]{:S(2)}, u32[]{:S(2)}) collective-permute-start(f32[64,1024]{1,0:T(8,128)S(1)} %get-tuple-element.58), channel_id=1, source_target_pairs={{1,2},{3,4},{5,6},{7,8},{9,10},{11,12},{13,14},{17,18},{19,20},{21... | collective-permute-start | bytes 786440 | tf_op jit(solution)/shard_map/ppermute | solution.py:387
  15.9 2.1 %collective-permute-start.5 = (f32[64,1024]{1,0:T(8,128)S(1)}, f32[64,1024]{1,0:T(8,128)S(1)}, u32[]{:S(2)}, u32[]{:S(2)}) collective-permute-start(f32[64,1024]{1,0:T(8,128)S(1)} %get-tuple-element.51.field_ref.before_ref.zero_ref), channel_id=1, source_target_pairs={{2,1},{4,3},{6,5},{8,7},{10,9},{12,11},{14,13},{18,17},{20,19},{22... | collective-permute-start | bytes 786440 | tf_op jit(solution)/shard_map/ppermute | solution.py:387
  18.6 12.6 %collective-permute-start.6 = (f32[64,1024]{1,0:T(8,128)S(1)}, f32[64,1024]{1,0:T(8,128)S(1)}, u32[]{:S(2)}, u32[]{:S(2)}) collective-permute-start(f32[64,1024]{1,0:T(8,128)S(1)} %get-tuple-element.62), channel_id=1, source_target_pairs={{0,1},{1,0},{2,3},{3,2},{4,5},{5,4},{6,7},{7,6},{8,9},{9,8},{10,11... | collective-permute-start | bytes 786440 | tf_op jit(solution)/shard_map/ppermute | solution.py:387
  29.0 2.7 %collective-permute-start.8 = (f32[64,1024]{1,0:T(8,128)S(1)}, f32[64,1024]{1,0:T(8,128)S(1)}, u32[]{:S(2)}, u32[]{:S(2)}) collective-permute-start(f32[64,1024]{1,0:T(8,128)S(1)} %shard_map.76.after_ref.even_ref), channel_id=1, source_target_pairs={{2,1},{4,3},{6,5},{8,7},{10,9},{12,11},{14,13},{18,17},{20,19},{22... | collective-permute-start | bytes 786440 | tf_op jit(solution)/shard_map/ppermute | solution.py:387
  29.7 2.1 %collective-permute-start.7 = (f32[64,1024]{1,0:T(8,128)S(1)}, f32[64,1024]{1,0:T(8,128)S(1)}, u32[]{:S(2)}, u32[]{:S(2)}) collective-permute-start(f32[64,1024]{1,0:T(8,128)S(1)} %get-tuple-element.63), channel_id=1, source_target_pairs={{1,2},{3,4},{5,6},{7,8},{9,10},{11,12},{13,14},{17,18},{19,20},{21... | collective-permute-start | bytes 786440 | tf_op jit(solution)/shard_map/ppermute | solution.py:387
  32.3 11.6 %collective-permute-start.9 = (f32[64,1024]{1,0:T(8,128)S(1)}, f32[64,1024]{1,0:T(8,128)S(1)}, u32[]{:S(2)}, u32[]{:S(2)}) collective-permute-start(f32[64,1024]{1,0:T(8,128)S(1)} %get-tuple-element.67), channel_id=1, source_target_pairs={{0,1},{1,0},{2,3},{3,2},{4,5},{5,4},{6,7},{7,6},{8,9},{9,8},{10,11... | collective-permute-start | bytes 786440 | tf_op jit(solution)/shard_map/ppermute | solution.py:387
  41.7 2.3 %collective-permute-start.10 = (f32[64,1024]{1,0:T(8,128)S(1)}, f32[64,1024]{1,0:T(8,128)S(1)}, u32[]{:S(2)}, u32[]{:S(2)}) collective-permute-start(f32[64,1024]{1,0:T(8,128)S(1)} %get-tuple-element.68), channel_id=1, source_target_pairs={{1,2},{3,4},{5,6},{7,8},{9,10},{11,12},{13,14},{17,18},{19,20},{21... | collective-permute-start | bytes 786440 | tf_op jit(solution)/shard_map/ppermute | solution.py:387
  42.3 21.5 %copy-start.1 = (f32[64,1024]{1,0:T(8,128)S(1)}, f32[64,1024]{1,0:T(8,128)}, u32[]{:S(2)}) copy-start(f32[64,1024]{1,0:T(8,128)} %start_ref.9) | copy-start | bytes 786436
  42.4 21.4 %collective-permute-start.11 = (f32[64,1024]{1,0:T(8,128)S(1)}, f32[64,1024]{1,0:T(8,128)S(1)}, u32[]{:S(2)}, u32[]{:S(2)}) collective-permute-start(f32[64,1024]{1,0:T(8,128)S(1)} %get-tuple-element.65.field_ref.two_ref), channel_id=1, source_target_pairs={{2,1},{4,3},{6,5},{8,7},{10,9},{12,11},{14,13},{18,17},{20,19},{22... | collective-permute-start | bytes 786440 | tf_op jit(solution)/shard_map/ppermute | solution.py:387

commit v6 on v5

--- a/solution.py
+++ b/solution.py
@@ -77,64 +77,62 @@
     return copies
 
 
-def take_next(next_ref, field_ref, high_ref, low_ref, out_ref, raw, field, sems):
+def take_next(next_ref, field_ref, high_ref, low_ref, out_ref, raw, sems, field=None):
     size = raw.shape[0]
     tile = tile_of(size)
     starts = list(range(0, size, tile))
     parts = [(pl.ds(start, tile), pl.ds(0, start + tile)) for start in starts]
-    ours = pltpu.make_async_copy(field_ref, field, sems.at[len(starts)])
-    ours.start()
+    if field is not None:
+        ours = pltpu.make_async_copy(field_ref, field, sems.at[len(starts)])
+        ours.start()
     copies = load(next_ref, parts, raw, sems)
     store = adding(out_ref)
-    ours.wait()
+    if field is not None:
+        ours.wait()
+        field_ref = field
     for start, part, copy in zip(starts, parts, copies):
         copy.wait()
         high, low = halves(raw[part])
         high_ref[part] = high
         low_ref[part] = low
-        store(start, product(stacked(field[:, pl.ds(start, tile)]), high, low))
-
-
-def take_local(local_ref, field_ref, high_ref, low_ref, out_ref, raw, field, sems):
-    size = raw.shape[0]
+        store(start, product(stacked(field_ref[:, pl.ds(start, tile)]), high, low))
+
+
+def take_local(local_ref, field_ref, high_ref, low_ref, out_ref):
+    size = local_ref.shape[0]
     tile = tile_of(size)
-    starts = list(range(0, size, tile))
-    parts = [(pl.ds(start, tile), slice(None)) for start in starts]
-    ours = pltpu.make_async_copy(field_ref, field, sems.at[len(starts)])
-    ours.start()
-    copies = load(local_ref, parts, raw, sems)
-    ours.wait()
-    for start, part, copy in zip(starts, parts, copies):
-        copy.wait()
+    both = stacked(field_ref[...])
+    for start in range(0, size, tile):
+        rows = pl.ds(start, tile)
         row = lax.broadcasted_iota(jnp.int32, (tile, size), 0) + start
         col = lax.broadcasted_iota(jnp.int32, (tile, size), 1)
-        high, low = halves(raw[part] - jnp.where(row == col, 1.0, 0.0))
-        high_ref[part] = high
-        low_ref[part] = low
-        done = product(stacked(field[:, pl.ds(start, tile)]), high, low)
+        high, low = halves(local_ref[rows, :] - jnp.where(row == col, 1.0, 0.0))
+        high_ref[rows, :] = high
+        low_ref[rows, :] = low
+        done = product(both[:, start : start + tile], high, low)
         out_ref[...] = done if start == 0 else out_ref[...] + done
 
 
 def begin_odd_kernel(next_ref, start_ref, high_n, low_n, cross_ref, raw, field, sems):
     @pl.when(is_odd())
     def _():
-        take_next(next_ref, start_ref, high_n, low_n, cross_ref, raw, field, sems)
+        take_next(next_ref, start_ref, high_n, low_n, cross_ref, raw, sems, field)
 
 
 def begin_even_kernel(
     next_ref, local_ref, start_ref, high_n_in, low_n_in,
-    high_n, low_n, high_l, low_l, own_ref, pair_ref, raw, field, sems,
+    high_n, low_n, high_l, low_l, own_ref, pair_ref, raw, sems,
 ):
     del high_n_in, low_n_in
 
     @pl.when(is_odd())
     def _():
-        take_local(local_ref, start_ref, high_l, low_l, own_ref, raw, field, sems)
-        pair_ref[...] = field[...]
-
-    @pl.when(jnp.logical_not(is_odd()))
-    def _():
-        take_next(next_ref, start_ref, high_n, low_n, pair_ref, raw, field, sems)
+        take_local(local_ref, start_ref, high_l, low_l, own_ref)
+        pair_ref[...] = start_ref[...]
+
+    @pl.when(jnp.logical_not(is_odd()))
+    def _():
+        take_next(next_ref, start_ref, high_n, low_n, pair_ref, raw, sems)
 
 
 def flip(high_in, low_in, high_ref, low_ref):
@@ -163,15 +161,15 @@
 def prepare_even_kernel(
     local_ref, start_ref, marginal_ref, shrinkage_ref, got_pair_ref, high_n, low_n,
     high_l_in, low_l_in, high_up_in, low_up_in, after_ref,
-    high_l, low_l, high_up, low_up, base_ref, raw, field, sems,
+    high_l, low_l, high_up, low_up, base_ref,
 ):
     del high_l_in, low_l_in, high_up_in, low_up_in, after_ref
 
     @pl.when(jnp.logical_not(is_odd()))
     def _():
         flip(high_n, low_n, high_up, low_up)
-        take_local(local_ref, start_ref, high_l, low_l, base_ref, raw, field, sems)
-        base_ref[...] = marginal_ref[...] - ridge_column(shrinkage_ref) * field[...] - base_ref[...]
+        take_local(local_ref, start_ref, high_l, low_l, base_ref)
+        base_ref[...] = marginal_ref[...] - ridge_column(shrinkage_ref) * start_ref[...] - base_ref[...]
         tile = tile_of(base_ref.shape[1])
 
         def store(start, part):
@@ -400,7 +398,7 @@
     high_n, low_n, high_l, low_l, own, pair = run(
         begin_even_kernel, [matrix, matrix, matrix, matrix, field, field],
         next_block, local_block, warm_start, high_n, low_n,
-        spaces={0: hbm, 1: hbm, 2: hbm}, scratch=copies, aliases={3: 0, 4: 1}, flops=work,
+        spaces={0: hbm}, scratch=copies[::2], aliases={3: 0, 4: 1}, flops=work,
     )
     got_pair = shift(pair, on_chip)
     rest, high_up, low_up = run(
@@ -414,7 +412,7 @@
         prepare_even_kernel, [matrix, matrix, matrix, matrix, field],
         local_block, warm_start, marginal, ridge, got_pair, high_n, low_n,
         high_l, low_l, high_up, low_up, odd_field,
-        spaces={0: hbm, 1: hbm}, scratch=copies, aliases={7: 0, 8: 1, 9: 2, 10: 3}, flops=work,
+        aliases={7: 0, 8: 1, 9: 2, 10: 3}, flops=work,
     )
     join = functools.partial(join_kernel, -1.0)
     merged, pair = run(join, [field, field], base, up, odd_field, high_n, low_n, flops=work)

time: 65.5 us -> 64.7 us (0.988)
  Pallas kernels: 13.1 us -> 11 us
  local copies, waits for them, and re-layouts: 0.03 us -> 1.39 us
    pallas_call x19, Pallas kernels: 13.1 us -> 11 us  [call(): pl.pallas_call(kernel, out_shape=[make(shape, dtype) for shape, dtype in...]
    unnamed x8, local copies, waits for them, and re-layouts: 0.03 us -> 1.39 us
  transfers between devices with their start and end apart: 12 -> 12, of which waited for: 1 -> 1; matrix products, arithmetic and copies ran while one was open for 0% -> 0% of each run, Pallas kernels for 15% -> 12%
where the time goes in v6:
time: 64.7 us; the launch traced here: 64.4 us
  starting transfers between devices  31.1 us (48%)
  blocking collectives  19.5 us (30%)
  Pallas kernels  11 us (17%)
  local copies, waits for them, and re-layouts  1.39 us (2%)
  between operations  0.91 us (1%)
    ppermute x12, starting transfers between devices, shift(): return lax.ppermute(value, 'snp', route)  31.1 us
    all_to_all x1, blocking collectives, on_device(): moments = lax.all_to_all(moments, 'snp', 0, 0)  19.5 us
    pallas_call x19, Pallas kernels, call(): pl.pallas_call(kernel, out_shape=[make(shape, dtype) for shape, dtype in...  11 us
    unnamed x8, local copies, waits for them, and re-layouts  1.39 us
  transfers between devices with their start and end apart: 12, of which 1 were waited for; matrix products, arithmetic and copies ran while one was open for 0% of the time, Pallas kernels for 12%

profile of v6, /device:TPU:0, one launch (start us, length us, event | category | flops | bytes accessed | tf_op | source)
XLA Modules:
  0.0 64.4 jit_solution(3164277777547669438)
XLA Ops:
  0.6 0.8 %collective-permute-start.1 = (f32[64,1024]{1,0:T(8,128)}, f32[64,1024]{1,0:T(8,128)S(1)}, u32[]{:S(2)}, u32[]{:S(2)}) collective-permute-start(f32[64,1024]{1,0:T(8,128)} %start_ref.9), channel_id=1, source_target_pairs={{2,1},{4,3},{6,5},{8,7},{10,9},{12,11},{14,13},{18,17},{20,19},{22... | collective-permute-start | bytes 786440 | tf_op jit(solution)/shard_map/ppermute | solution.py:385
  1.5 0.1 shard_map.68
  1.5 0.0 copy-done.1
  1.6 1.3 %copy-done = f32[1024,1024]{1,0:T(8,128)S(1)} copy-done((f32[1024,1024]{1,0:T(8,128)S(1)}, f32[1024,1024]{1,0:T(8,128)}, u32[]{:S(2)}) %copy-start) | copy-done | bytes 4194328
  2.9 2.1 %shard_map.69 = (bf16[1024,1024]{1,0:T(8,128)(2,1)S(1)}, bf16[1024,1024]{1,0:T(8,128)(2,1)S(1)}, bf16[1024,1024]{1,0:T(8,128)(2,1)S(1)}, bf16[1024,1024]{1,0:T(8...) custom-call(f32[1024,1024]{1,0:T(8,128)} %next_ref.3, ...), custom_call_target="tpu_custom_call", output_to_operand_aliasing={{0}: (3, {}), {1}: (4, {})} | custom-call | flops 402653184 | tf_op jit(solution)/shard_map/pallas_call | solution.py:356
  5.0 1.1 %collective-permute-start = (f32[64,1024]{1,0:T(8,128)S(1)}, f32[64,1024]{1,0:T(8,128)S(1)}, u32[]{:S(2)}, u32[]{:S(2)}) collective-permute-start(f32[64,1024]{1,0:T(8,128)S(1)} %get-tuple-element.39), channel_id=1, source_target_pairs={{0,1},{1,0},{2,3},{3,2},{4,5},{5,4},{6,7},{7,6},{8,9},{9,8},{10,11... | collective-permute-start | bytes 786440 | tf_op jit(solution)/shard_map/ppermute | solution.py:385
  6.1 0.7 %collective-permute-start.2 = (f32[64,1024]{1,0:T(8,128)S(1)}, f32[64,1024]{1,0:T(8,128)S(1)}, u32[]{:S(2)}, u32[]{:S(2)}) collective-permute-start(f32[64,1024]{1,0:T(8,128)S(1)} %get-tuple-element.50), channel_id=1, source_target_pairs={{1,2},{3,4},{5,6},{7,8},{9,10},{11,12},{13,14},{17,18},{19,20},{21... | collective-permute-start | bytes 786440 | tf_op jit(solution)/shard_map/ppermute | solution.py:385
  6.9 0.4 collective-permute-done.got_pair_ref
  7.3 1.9 %shard_map.72 = (bf16[1024,1024]{1,0:T(8,128)(2,1)S(1)}, bf16[1024,1024]{1,0:T(8,128)(2,1)S(1)}, bf16[1024,1024]{1,0:T(8,128)(2,1)S(1)}, bf16[1024,1024]{1,0:T(8,128)(2,1)S(1)}, f32[64,1024]{1,0:T(8,128)S(1)}) custom-call(f32[1024,1024]{1,0:T(8,128)S(1)} %copy-done, ...), custom_call_target="tpu_custom_call", output_to_operand_aliasing={{0}: (7, {}), {1}: (8, {}), {2}: (9, {}), {3}: (10, {})} | custom-call | flops 402653184 | tf_op jit(solution)/shard_map/pallas_call | solution.py:356
  9.2 0.0 collective-permute-done.2.got_ref
  9.2 0.6 shard_map.73
  9.8 4.2 %collective-permute-start.3 = (f32[64,1024]{1,0:T(8,128)S(1)}, f32[64,1024]{1,0:T(8,128)S(1)}, u32[]{:S(2)}, u32[]{:S(2)}) collective-permute-start(f32[64,1024]{1,0:T(8,128)S(1)} %get-tuple-element.55), channel_id=1, source_target_pairs={{0,1},{1,0},{2,3},{3,2},{4,5},{5,4},{6,7},{7,6},{8,9},{9,8},{10,11... | collective-permute-start | bytes 786440 | tf_op jit(solution)/shard_map/ppermute | solution.py:385
  13.9 0.7 %collective-permute-start.4 = (f32[64,1024]{1,0:T(8,128)S(1)}, f32[64,1024]{1,0:T(8,128)S(1)}, u32[]{:S(2)}, u32[]{:S(2)}) collective-permute-start(f32[64,1024]{1,0:T(8,128)S(1)} %get-tuple-element.58), channel_id=1, source_target_pairs={{1,2},{3,4},{5,6},{7,8},{9,10},{11,12},{13,14},{17,18},{19,20},{21... | collective-permute-start | bytes 786440 | tf_op jit(solution)/shard_map/ppermute | solution.py:385
  14.6 0.7 %collective-permute-start.5 = (f32[64,1024]{1,0:T(8,128)S(1)}, f32[64,1024]{1,0:T(8,128)S(1)}, u32[]{:S(2)}, u32[]{:S(2)}) collective-permute-start(f32[64,1024]{1,0:T(8,128)S(1)} %get-tuple-element.51.field_ref.before_ref.zero_ref), channel_id=1, source_target_pairs={{2,1},{4,3},{6,5},{8,7},{10,9},{12,11},{14,13},{18,17},{20,19},{22... | collective-permute-start | bytes 786440 | tf_op jit(solution)/shard_map/ppermute | solution.py:385
  15.3 0.8 %shard_map.74 = (f32[64,1024]{1,0:T(8,128)S(1)}, f32[64,128]{1,0:T(8,128)S(1)}) custom-call(f32[64,1024]{1,0:T(8,128)S(1)} %get-tuple-element.51.field_ref.before_ref.zero_ref, bf16[1024,1024]{1,0:T(8,128)(2,1)S(1)} %get-tuple-element.52.high_ref, bf16[1024,1024]{1,0:T(8,128)(2,1)S(1)} %get-tuple-element.53.low_ref), custom_call_target="tpu_custom_call" | custom-call | flops 402653184 | tf_op jit(solution)/shard_map/pallas_call | solution.py:356
  16.1 0.6 shard_map.75.base_ref
  16.6 0.0 collective-permute-done.4.got_ref
  16.7 0.6 shard_map.78
  17.3 10.4 %collective-permute-start.6 = (f32[64,1024]{1,0:T(8,128)S(1)}, f32[64,1024]{1,0:T(8,128)S(1)}, u32[]{:S(2)}, u32[]{:S(2)}) collective-permute-start(f32[64,1024]{1,0:T(8,128)S(1)} %get-tuple-element.62), channel_id=1, source_target_pairs={{0,1},{1,0},{2,3},{3,2},{4,5},{5,4},{6,7},{7,6},{8,9},{9,8},{10,11... | collective-permute-start | bytes 786440 | tf_op jit(solution)/shard_map/ppermute | solution.py:385
  27.7 0.7 %collective-permute-start.8 = (f32[64,1024]{1,0:T(8,128)S(1)}, f32[64,1024]{1,0:T(8,128)S(1)}, u32[]{:S(2)}, u32[]{:S(2)}) collective-permute-start(f32[64,1024]{1,0:T(8,128)S(1)} %shard_map.76.after_ref.even_ref), channel_id=1, source_target_pairs={{2,1},{4,3},{6,5},{8,7},{10,9},{12,11},{14,13},{18,17},{20,19},{22... | collective-permute-start | bytes 786440 | tf_op jit(solution)/shard_map/ppermute | solution.py:385
  28.4 0.7 %collective-permute-start.7 = (f32[64,1024]{1,0:T(8,128)S(1)}, f32[64,1024]{1,0:T(8,128)S(1)}, u32[]{:S(2)}, u32[]{:S(2)}) collective-permute-start(f32[64,1024]{1,0:T(8,128)S(1)} %get-tuple-element.63), channel_id=1, source_target_pairs={{1,2},{3,4},{5,6},{7,8},{9,10},{11,12},{13,14},{17,18},{19,20},{21... | collective-permute-start | bytes 786440 | tf_op jit(solution)/shard_map/ppermute | solution.py:385
  29.1 0.8 %shard_map.79 = (f32[64,1024]{1,0:T(8,128)S(1)}, f32[64,128]{1,0:T(8,128)S(1)}) custom-call(f32[64,1024]{1,0:T(8,128)S(1)} %get-tuple-element.51.field_ref.before_ref.zero_ref, f32[64,1024]{1,0:T(8,128)S(1)} %get-tuple-element.60.field_ref.before_ref.one_ref, bf16[1024,1024]{1,0:T(8,128)(2,1)S(1)} %get-tuple-element.52.high_ref, ...), custom_call_target="tpu_custom_call" | custom-call | flops 402653184 | tf_op jit(solution)/shard_map/pallas_call | solution.py:356
  29.9 0.6 shard_map.80.after_ref.base_ref
  30.5 0.6 shard_map.82
  31.0 9.9 %collective-permute-start.9 = (f32[64,1024]{1,0:T(8,128)S(1)}, f32[64,1024]{1,0:T(8,128)S(1)}, u32[]{:S(2)}, u32[]{:S(2)}) collective-permute-start(f32[64,1024]{1,0:T(8,128)S(1)} %get-tuple-element.67), channel_id=1, source_target_pairs={{0,1},{1,0},{2,3},{3,2},{4,5},{5,4},{6,7},{7,6},{8,9},{9,8},{10,11... | collective-permute-start | bytes 786440 | tf_op jit(solution)/shard_map/ppermute | solution.py:385
  40.9 0.7 %collective-permute-start.10 = (f32[64,1024]{1,0:T(8,128)S(1)}, f32[64,1024]{1,0:T(8,128)S(1)}, u32[]{:S(2)}, u32[]{:S(2)}) collective-permute-start(f32[64,1024]{1,0:T(8,128)S(1)} %get-tuple-element.68), channel_id=1, source_target_pairs={{1,2},{3,4},{5,6},{7,8},{9,10},{11,12},{13,14},{17,18},{19,20},{21... | collective-permute-start | bytes 786440 | tf_op jit(solution)/shard_map/ppermute | solution.py:385
  41.6 0.7 %collective-permute-start.11 = (f32[64,1024]{1,0:T(8,128)S(1)}, f32[64,1024]{1,0:T(8,128)S(1)}, u32[]{:S(2)}, u32[]{:S(2)}) collective-permute-start(f32[64,1024]{1,0:T(8,128)S(1)} %get-tuple-element.65.field_ref.two_ref), channel_id=1, source_target_pairs={{2,1},{4,3},{6,5},{8,7},{10,9},{12,11},{14,13},{18,17},{20,19},{22... | collective-permute-start | bytes 786440 | tf_op jit(solution)/shard_map/ppermute | solution.py:385
  42.3 0.8 %shard_map.83 = (f32[64,1024]{1,0:T(8,128)S(1)}, f32[64,128]{1,0:T(8,128)S(1)}) custom-call(f32[64,1024]{1,0:T(8,128)S(1)} %get-tuple-element.60.field_ref.before_ref.one_ref, f32[64,1024]{1,0:T(8,128)S(1)} %get-tuple-element.65.field_ref.two_ref, bf16[1024,1024]{1,0:T(8,128)(2,1)S(1)} %get-tuple-element.52.high_ref, ...), custom_call_target="tpu_custom_call" | custom-call | flops 402653184 | tf_op jit(solution)/shard_map/pallas_call | solution.py:356
  43.1 0.3 shard_map.84
  43.3 19.5 %all_to_all.5.table_ref = f32[16,8,128]{2,1,0:T(8,128)S(1)} all-to-all(f32[16,8,128]{2,1,0:T(8,128)S(1)} %shard_map.84), channel_id=1, replica_groups=mesh['parts'=2,'snp'=16] {'snp'}, dimensions={0} | all-to-all | bytes 131072 | tf_op jit(solution)/shard_map/all_to_all | solution.py:454
  62.9 0.2 shard_map.85.weights_ref
  63.0 1.3 %shard_map.86 = (f32[64,1024]{1,0:T(8,128)}, f32[64,1024]{1,0:T(8,128)}) custom-call(f32[64,128]{1,0:T(8,128)S(1)} %shard_map.85.weights_ref, f32[64,1024]{1,0:T(8,128)S(1)} %copy-done.1, f32[64,1024]{1,0:T(8,128)S(1)} %get-tuple-element.51.field_ref.before_ref.zero_ref, f32[64,1024]{1,0:T(8,128)S(1)} %get-tuple-element.60.field_ref.before_ref.one_ref, ...), custom_call_target="tpu_custom_call" | custom-call | tf_op jit(solution)/shard_map/pallas_call | solution.py:356
  (20 shorter events, 0.1 us)
Async XLA Ops:
  0.6 1.0 %copy-start.1 = (f32[64,1024]{1,0:T(8,128)S(1)}, f32[64,1024]{1,0:T(8,128)}, u32[]{:S(2)}) copy-start(f32[64,1024]{1,0:T(8,128)} %start_ref.9) | copy-start | bytes 786436
  0.6 2.3 %copy-start = (f32[1024,1024]{1,0:T(8,128)S(1)}, f32[1024,1024]{1,0:T(8,128)}, u32[]{:S(2)}) copy-start(f32[1024,1024]{1,0:T(8,128)} %local_ref.3) | copy-start | bytes 12582916
  0.6 6.2 %collective-permute-start.1 = (f32[64,1024]{1,0:T(8,128)}, f32[64,1024]{1,0:T(8,128)S(1)}, u32[]{:S(2)}, u32[]{:S(2)}) collective-permute-start(f32[64,1024]{1,0:T(8,128)} %start_ref.9), channel_id=1, source_target_pairs={{2,1},{4,3},{6,5},{8,7},{10,9},{12,11},{14,13},{18,17},{20,19},{22... | collective-permute-start | bytes 786440 | tf_op jit(solution)/shard_map/ppermute | solution.py:385
  2.9 3.9 %copy-start.2 = (f32[64,1024]{1,0:T(8,128)S(1)}, f32[64,1024]{1,0:T(8,128)}, u32[]{:S(2)}) copy-start(f32[64,1024]{1,0:T(8,128)} %marginal_ref.3) | copy-start | bytes 786436
  2.9 3.9 %copy-start.3 = (f32[64,1]{0,1:T(1,128)S(1)}, f32[64,1]{0,1:T(1,128)}, u32[]{:S(2)}) copy-start(f32[64,1]{0,1:T(1,128)} %param.7) | copy-start | bytes 772
  5.0 2.3 %collective-permute-start = (f32[64,1024]{1,0:T(8,128)S(1)}, f32[64,1024]{1,0:T(8,128)S(1)}, u32[]{:S(2)}, u32[]{:S(2)}) collective-permute-start(f32[64,1024]{1,0:T(8,128)S(1)} %get-tuple-element.39), channel_id=1, source_target_pairs={{0,1},{1,0},{2,3},{3,2},{4,5},{5,4},{6,7},{7,6},{8,9},{9,8},{10,11... | collective-permute-start | bytes 786440 | tf_op jit(solution)/shard_map/ppermute | solution.py:385
  6.1 3.0 %collective-permute-start.2 = (f32[64,1024]{1,0:T(8,128)S(1)}, f32[64,1024]{1,0:T(8,128)S(1)}, u32[]{:S(2)}, u32[]{:S(2)}) collective-permute-start(f32[64,1024]{1,0:T(8,128)S(1)} %get-tuple-element.50), channel_id=1, source_target_pairs={{1,2},{3,4},{5,6},{7,8},{9,10},{11,12},{13,14},{17,18},{19,20},{21... | collective-permute-start | bytes 786440 | tf_op jit(solution)/shard_map/ppermute | solution.py:385
  9.8 6.3 %collective-permute-start.3 = (f32[64,1024]{1,0:T(8,128)S(1)}, f32[64,1024]{1,0:T(8,128)S(1)}, u32[]{:S(2)}, u32[]{:S(2)}) collective-permute-start(f32[64,1024]{1,0:T(8,128)S(1)} %get-tuple-element.55), channel_id=1, source_target_pairs={{0,1},{1,0},{2,3},{3,2},{4,5},{5,4},{6,7},{7,6},{8,9},{9,8},{10,11... | collective-permute-start | bytes 786440 | tf_op jit(solution)/shard_map/ppermute | solution.py:385
  13.9 2.7 %collective-permute-start.4 = (f32[64,1024]{1,0:T(8,128)S(1)}, f32[64,1024]{1,0:T(8,128)S(1)}, u32[]{:S(2)}, u32[]{:S(2)}) collective-permute-start(f32[64,1024]{1,0:T(8,128)S(1)} %get-tuple-element.58), channel_id=1, source_target_pairs={{1,2},{3,4},{5,6},{7,8},{9,10},{11,12},{13,14},{17,18},{19,20},{21... | collective-permute-start | bytes 786440 | tf_op jit(solution)/shard_map/ppermute | solution.py:385
  14.6 2.1 %collective-permute-start.5 = (f32[64,1024]{1,0:T(8,128)S(1)}, f32[64,1024]{1,0:T(8,128)S(1)}, u32[]{:S(2)}, u32[]{:S(2)}) collective-permute-start(f32[64,1024]{1,0:T(8,128)S(1)} %get-tuple-element.51.field_ref.before_ref.zero_ref), channel_id=1, source_target_pairs={{2,1},{4,3},{6,5},{8,7},{10,9},{12,11},{14,13},{18,17},{20,19},{22... | collective-permute-start | bytes 786440 | tf_op jit(solution)/shard_map/ppermute | solution.py:385
  17.3 12.6 %collective-permute-start.6 = (f32[64,1024]{1,0:T(8,128)S(1)}, f32[64,1024]{1,0:T(8,128)S(1)}, u32[]{:S(2)}, u32[]{:S(2)}) collective-permute-start(f32[64,1024]{1,0:T(8,128)S(1)} %get-tuple-element.62), channel_id=1, source_target_pairs={{0,1},{1,0},{2,3},{3,2},{4,5},{5,4},{6,7},{7,6},{8,9},{9,8},{10,11... | collective-permute-start | bytes 786440 | tf_op jit(solution)/shard_map/ppermute | solution.py:385
  27.7 2.7 %collective-permute-start.8 = (f32[64,1024]{1,0:T(8,128)S(1)}, f32[64,1024]{1,0:T(8,128)S(1)}, u32[]{:S(2)}, u32[]{:S(2)}) collective-permute-start(f32[64,1024]{1,0:T(8,128)S(1)} %shard_map.76.after_ref.even_ref), channel_id=1, source_target_pairs={{2,1},{4,3},{6,5},{8,7},{10,9},{12,11},{14,13},{18,17},{20,19},{22... | collective-permute-start | bytes 786440 | tf_op jit(solution)/shard_map/ppermute | solution.py:385
  28.4 2.1 %collective-permute-start.7 = (f32[64,1024]{1,0:T(8,128)S(1)}, f32[64,1024]{1,0:T(8,128)S(1)}, u32[]{:S(2)}, u32[]{:S(2)}) collective-permute-start(f32[64,1024]{1,0:T(8,128)S(1)} %get-tuple-element.63), channel_id=1, source_target_pairs={{1,2},{3,4},{5,6},{7,8},{9,10},{11,12},{13,14},{17,18},{19,20},{21... | collective-permute-start | bytes 786440 | tf_op jit(solution)/shard_map/ppermute | solution.py:385
  31.0 12.0 %collective-permute-start.9 = (f32[64,1024]{1,0:T(8,128)S(1)}, f32[64,1024]{1,0:T(8,128)S(1)}, u32[]{:S(2)}, u32[]{:S(2)}) collective-permute-start(f32[64,1024]{1,0:T(8,128)S(1)} %get-tuple-element.67), channel_id=1, source_target_pairs={{0,1},{1,0},{2,3},{3,2},{4,5},{5,4},{6,7},{7,6},{8,9},{9,8},{10,11... | collective-permute-start | bytes 786440 | tf_op jit(solution)/shard_map/ppermute | solution.py:385
  40.9 2.2 %collective-permute-start.10 = (f32[64,1024]{1,0:T(8,128)S(1)}, f32[64,1024]{1,0:T(8,128)S(1)}, u32[]{:S(2)}, u32[]{:S(2)}) collective-permute-start(f32[64,1024]{1,0:T(8,128)S(1)} %get-tuple-element.68), channel_id=1, source_target_pairs={{1,2},{3,4},{5,6},{7,8},{9,10},{11,12},{13,14},{17,18},{19,20},{21... | collective-permute-start | bytes 786440 | tf_op jit(solution)/shard_map/ppermute | solution.py:385
  41.6 21.5 %collective-permute-start.11 = (f32[64,1024]{1,0:T(8,128)S(1)}, f32[64,1024]{1,0:T(8,128)S(1)}, u32[]{:S(2)}, u32[]{:S(2)}) collective-permute-start(f32[64,1024]{1,0:T(8,128)S(1)} %get-tuple-element.65.field_ref.two_ref), channel_id=1, source_target_pairs={{2,1},{4,3},{6,5},{8,7},{10,9},{12,11},{14,13},{18,17},{20,19},{22... | collective-permute-start | bytes 786440 | tf_op jit(solution)/shard_map/ppermute | solution.py:385

commit v7 on v6

--- a/solution.py
+++ b/solution.py
@@ -118,6 +118,12 @@
     def _():
         take_next(next_ref, start_ref, high_n, low_n, cross_ref, raw, sems, field)
 
+    @pl.when(jnp.logical_not(is_odd()))
+    def _():
+        copy = pltpu.make_async_copy(start_ref, cross_ref, sems.at[0])
+        copy.start()
+        copy.wait()
+
 
 def begin_even_kernel(
     next_ref, local_ref, start_ref, high_n_in, low_n_in,
@@ -151,23 +157,20 @@
     return 1.0 + jnp.sum(jnp.where(here, shrinkage_ref[...], 0.0), axis=1, keepdims=True)
 
 
-def prepare_odd_kernel(own_ref, start_ref, marginal_ref, shrinkage_ref, high_n, low_n, rest_ref, high_up, low_up):
-    @pl.when(is_odd())
-    def _():
-        rest_ref[...] = marginal_ref[...] - ridge_column(shrinkage_ref) * start_ref[...] - own_ref[...]
-        flip(high_n, low_n, high_up, low_up)
-
-
-def prepare_even_kernel(
-    local_ref, start_ref, marginal_ref, shrinkage_ref, got_pair_ref, high_n, low_n,
-    high_l_in, low_l_in, high_up_in, low_up_in, after_ref,
+def prepare_kernel(
+    own_ref, local_ref, start_ref, marginal_ref, shrinkage_ref, got_pair_ref, high_n, low_n, high_l_in, low_l_in,
     high_l, low_l, high_up, low_up, base_ref,
 ):
-    del high_l_in, low_l_in, high_up_in, low_up_in, after_ref
-
-    @pl.when(jnp.logical_not(is_odd()))
-    def _():
-        flip(high_n, low_n, high_up, low_up)
+    del high_l_in, low_l_in
+    flip(high_n, low_n, high_up, low_up)
+
+    @pl.when(is_odd())
+    def _():
+        rest = marginal_ref[...] - ridge_column(shrinkage_ref) * start_ref[...]
+        base_ref[...] = rest - own_ref[...] - got_pair_ref[...]
+
+    @pl.when(jnp.logical_not(is_odd()))
+    def _():
         take_local(local_ref, start_ref, high_l, low_l, base_ref)
         base_ref[...] = marginal_ref[...] - ridge_column(shrinkage_ref) * start_ref[...] - base_ref[...]
         tile = tile_of(base_ref.shape[1])
@@ -177,6 +180,29 @@
             base_ref[:, cols] = base_ref[:, cols] - part
 
         forward(stacked(got_pair_ref[...]), high_up, low_up, store)
+
+
+def field_then_coupling(base, got, high_in, low_in, high_up, low_up, keep, send):
+    size = high_up.shape[0]
+    tile = tile_of(size)
+    both = stacked(got)
+    done = []
+    waiting = None
+
+    def couple(start):
+        rows, cols = pl.ds(start, size - start), pl.ds(start, tile)
+        send(start, product(jnp.concatenate(done, axis=1), high_in[rows, cols], low_in[rows, cols]))
+
+    for start in reversed(range(0, size, tile)):
+        rows, cols = pl.ds(0, start + tile), pl.ds(start, tile)
+        part = product(both[:, : start + tile], high_up[rows, cols], low_up[rows, cols])
+        if waiting is not None:
+            couple(waiting)
+        field = base(cols, part)
+        keep(cols, field)
+        done.insert(0, stacked(field))
+        waiting = start
+    couple(waiting)
 
 
 def moment(left, right):
@@ -211,22 +237,46 @@
         field_ref[...] = base_ref[...] + got_ref[...]
 
 
-def odd_kernel(sign, own_ref, got_pair_ref, got_ref, high_in, low_in, high_up, low_up, after_ref, field_ref, cross_ref):
+def odd_kernel(own_ref, got_pair_ref, got_ref, high_in, low_in, high_up, low_up, after_ref, field_ref, cross_ref):
     del after_ref
 
     @pl.when(is_odd())
     def _():
         tile = tile_of(own_ref.shape[1])
 
-        def keep(start, part):
-            cols = pl.ds(start, tile)
-            field_ref[:, cols] = own_ref[:, cols] + sign * (got_pair_ref[:, cols] + part)
+        def base(cols, part):
+            return own_ref[:, cols] + (got_pair_ref[:, cols] + part)
+
+        def keep(cols, field):
+            field_ref[:, cols] = field
 
         def send(start, part):
             cross_ref[:, pl.ds(start, tile)] = part
 
-        forward(stacked(got_ref[...]), high_up, low_up, keep)
-        coupling(stacked(field_ref[...]), high_in, low_in, send)
+        field_then_coupling(base, got_ref[...], high_in, low_in, high_up, low_up, keep, send)
+
+
+def first_kernel(base_ref, got_ref, high_in, low_in, high_up, low_up, field_ref, pair_ref, cross_ref):
+    tile = tile_of(base_ref.shape[1])
+
+    @pl.when(is_odd())
+    def _():
+        def base(cols, part):
+            return base_ref[:, cols] - part
+
+        def keep(cols, field):
+            field_ref[:, cols] = field
+            pair_ref[:, cols] = field
+
+        def send(start, part):
+            cross_ref[:, pl.ds(start, tile)] = part
+
+        field_then_coupling(base, got_ref[...], high_in, low_in, high_up, low_up, keep, send)
+
+    @pl.when(jnp.logical_not(is_odd()))
+    def _():
+        field_ref[...] = base_ref[...] - got_ref[...]
+        couple_even(field_ref, high_in, low_in, pair_ref)
 
 
 def couple_even(field_ref, high_in, low_in, pair_ref):
@@ -250,7 +300,7 @@
         couple_even(field_ref, high_in, low_in, pair_ref)
 
 
-def join_kernel(sign, base_ref, got_ref, odd_ref, high_in, low_in, field_ref, pair_ref):
+def join_kernel(base_ref, got_ref, odd_ref, high_in, low_in, field_ref, pair_ref):
     @pl.when(is_odd())
     def _():
         field_ref[...] = odd_ref[...]
@@ -258,7 +308,7 @@
 
     @pl.when(jnp.logical_not(is_odd()))
     def _():
-        field_ref[...] = base_ref[...] + sign * got_ref[...]
+        field_ref[...] = base_ref[...] + got_ref[...]
         couple_even(field_ref, high_in, low_in, pair_ref)
 
 
@@ -327,22 +377,34 @@
 
 def final_kernel(
     weights_ref, start_ref, zero_ref, one_ref, two_ref, own_ref, got_pair_ref, got_down_ref, got_up_ref,
-    high_up, low_up, solution_ref, residual_ref,
+    high_up, low_up, solution_ref, residual_ref, solution, residual, sems,
 ):
-    tile = tile_of(own_ref.shape[1])
+    size = own_ref.shape[1]
+    tile = tile_of(size)
     weights = [weights_ref[:, i : i + 1] for i in range(2 * ITERS + 1)]
-    gain, residual = weights[:ITERS], weights[ITERS:]
+    gain, rest = weights[:ITERS], weights[ITERS:]
     odd = is_odd()
-    upper = jnp.where(odd, got_down_ref[...], got_pair_ref[...])
-    lower = jnp.where(odd, got_pair_ref[...], got_up_ref[...])
-    zero, one, two = zero_ref[...], one_ref[...], two_ref[...]
-    solution_ref[...] = start_ref[...] + gain[0] * zero + gain[1] * one + gain[2] * two
-    base = residual[0] * zero + residual[1] * one + residual[2] * two + residual[3] * (own_ref[...] + lower)
-
-    def store(start, part):
-        residual_ref[:, pl.ds(start, tile)] = base[:, start : start + tile] + residual[3] * part
-
-    forward(stacked(upper), high_up, low_up, store)
+    copies = []
+
+    def write(held, target, cols):
+        copies.append(pltpu.make_async_copy(held.at[:, cols], target.at[:, cols], sems.at[len(copies)]))
+        copies[-1].start()
+
+    for start in range(0, size, tile):
+        cols = pl.ds(start, tile)
+        steps = gain[0] * zero_ref[:, cols] + gain[1] * one_ref[:, cols] + gain[2] * two_ref[:, cols]
+        solution[:, cols] = start_ref[:, cols] + steps
+        write(solution, solution_ref, cols)
+    upper = stacked(jnp.where(odd, got_down_ref[...], got_pair_ref[...]))
+    for start in range(0, size, tile):
+        rows, cols = pl.ds(0, start + tile), pl.ds(start, tile)
+        part = product(upper[:, : start + tile], high_up[rows, cols], low_up[rows, cols])
+        lower = jnp.where(odd, got_pair_ref[:, cols], got_up_ref[:, cols])
+        steps = rest[0] * zero_ref[:, cols] + rest[1] * one_ref[:, cols] + rest[2] * two_ref[:, cols]
+        residual[:, cols] = steps + rest[3] * (own_ref[:, cols] + lower + part)
+        write(residual, residual_ref, cols)
+    for copy in copies:
+        copy.wait()
 
 
 def call(kernel, out, *args, spaces=None, scratch=(), limit=12, aliases=None, keep=True, flops=0):
@@ -357,7 +419,7 @@
         kernel,
         out_shape=[make(shape, dtype) for shape, dtype in out],
         in_specs=[pl.BlockSpec(memory_space=place) for place in places],
-        out_specs=[pl.BlockSpec(memory_space=VMEM) for _ in out],
+        out_specs=[pl.BlockSpec(memory_space=VMEM if keep else pltpu.HBM) for _ in out],
         scratch_shapes=scratch,
         input_output_aliases=aliases or {},
         cost_estimate=pl.CostEstimate(flops=flops, bytes_accessed=0, transcendentals=0) if flops else None,
@@ -378,6 +440,7 @@
         pltpu.SemaphoreType.DMA((size // tile_of(size) + 1,)),
     )
     on_chip = [(i, i ^ 1) for i in range(count) if i ^ 1 < count]
+    off_chip = [(i, ((i - 1) ^ 1) + 1) for i in range(1, count) if ((i - 1) ^ 1) + 1 < count]
     downward = [(i + 1, i) for i in range(1, count - 1, 2)]
     upward = [(i, i + 1) for i in range(1, count - 1, 2)]
 
@@ -389,36 +452,27 @@
 
     hbm = pltpu.HBM
     ridge = shrinkage.reshape(1, traits)
-    down = shift(warm_start, downward)
     high_n, low_n, cross = run(
         begin_odd_kernel, [matrix, matrix, field], next_block, warm_start,
         spaces={0: hbm, 1: hbm}, scratch=copies, flops=work,
     )
-    up = shift(cross, upward)
+    got = shift(cross, off_chip)
     high_n, low_n, high_l, low_l, own, pair = run(
         begin_even_kernel, [matrix, matrix, matrix, matrix, field, field],
         next_block, local_block, warm_start, high_n, low_n,
         spaces={0: hbm}, scratch=copies[::2], aliases={3: 0, 4: 1}, flops=work,
     )
     got_pair = shift(pair, on_chip)
-    rest, high_up, low_up = run(
-        prepare_odd_kernel, [field, matrix, matrix],
-        own, warm_start, marginal, ridge, high_n, low_n, flops=work,
-    )
-    odd = functools.partial(odd_kernel, -1.0)
-    odd_field, cross = run(odd, [field, field], rest, got_pair, down, high_n, low_n, high_up, low_up, ridge, flops=work)
-    next_up = shift(cross, upward)
     high_l, low_l, high_up, low_up, base = run(
-        prepare_even_kernel, [matrix, matrix, matrix, matrix, field],
-        local_block, warm_start, marginal, ridge, got_pair, high_n, low_n,
-        high_l, low_l, high_up, low_up, odd_field,
-        aliases={7: 0, 8: 1, 9: 2, 10: 3}, flops=work,
-    )
-    join = functools.partial(join_kernel, -1.0)
-    merged, pair = run(join, [field, field], base, up, odd_field, high_n, low_n, flops=work)
-    up = next_up
+        prepare_kernel, [matrix, matrix, matrix, matrix, field],
+        own, local_block, warm_start, marginal, ridge, got_pair, high_n, low_n, high_l, low_l,
+        aliases={8: 0, 9: 1}, flops=work,
+    )
+    merged, pair, cross = run(
+        first_kernel, [field, field, field], base, got, high_n, low_n, high_up, low_up, flops=work
+    )
+    up = shift(cross, upward)
     fields, tables = [merged], []
-    odd, join = functools.partial(odd_kernel, 1.0), functools.partial(join_kernel, 1.0)
     for step in range(2, ITERS + 2):
         got_pair = shift(pair, on_chip)
         if step % 2 == 0:
@@ -434,7 +488,7 @@
             (even_field,) = run(even_kernel, [field], base, up, ridge, flops=work)
             next_down = shift(even_field, downward)
             odd_field, cross = run(
-                odd, [field, field],
+                odd_kernel, [field, field],
                 own, got_pair, down, high_n, low_n, high_up, low_up, even_field, flops=work,
             )
             up = shift(cross, upward)
@@ -442,11 +496,11 @@
             merged, pair = run(merge_kernel, [field, field], even_field, odd_field, high_n, low_n, flops=work)
         else:
             odd_field, cross = run(
-                odd, [field, field],
+                odd_kernel, [field, field],
                 own, got_pair, down, high_n, low_n, high_up, low_up, base, flops=work,
             )
             next_up = shift(cross, upward)
-            merged, pair = run(join, [field, field], base, up, odd_field, high_n, low_n, flops=work)
+            merged, pair = run(join_kernel, [field, field], base, up, odd_field, high_n, low_n, flops=work)
             up = next_up
         fields.append(merged)
     lanes = -(-traits // 128) * 128
@@ -458,6 +512,11 @@
             final_kernel, [field, field],
             weights, warm_start, *fields, own, got_pair, down, up, high_up, low_up,
             keep=False,
+            scratch=(
+                pltpu.VMEM((traits, size), F32),
+                pltpu.VMEM((traits, size), F32),
+                pltpu.SemaphoreType.DMA((2 * (size // tile_of(size)),)),
+            ),
         )
     )
 

time: 64.7 us -> 66.7 us (1.031)
  Pallas kernels: 11 us -> 12.8 us
    pallas_call x19 -> x17, Pallas kernels: 11 us -> 12.8 us  [call(): pl.pallas_call(kernel, out_shape=[make(shape, dtype) for shape, dtype in...]
    ppermute x12 -> x11, starting transfers between devices: 31.1 us -> 31.5 us  [shift(): return lax.ppermute(value, 'snp', route)]
  transfers between devices with their start and end apart: 12 -> 11, of which waited for: 1 -> 1; matrix products, arithmetic and copies ran while one was open for 0% -> 0% of each run, Pallas kernels for 12% -> 10%
where the time goes in v7:
time: 66.7 us; the launch traced here: 66.4 us
  starting transfers between devices  31.5 us (47%)
  blocking collectives  19.5 us (29%)
  Pallas kernels  12.8 us (19%)
  local copies, waits for them, and re-layouts  1.18 us (2%)
  between operations  0.87 us (1%)
    ppermute x11, starting transfers between devices, shift(): return lax.ppermute(value, 'snp', route)  31.5 us
    all_to_all x1, blocking collectives, on_device(): moments = lax.all_to_all(moments, 'snp', 0, 0)  19.5 us
    pallas_call x17, Pallas kernels, call(): pl.pallas_call(kernel, out_shape=[make(shape, dtype) for shape, dtype in...  12.8 us
  transfers between devices with their start and end apart: 11, of which 1 were waited for; matrix products, arithmetic and copies ran while one was open for 0% of the time, Pallas kernels for 10%

profile of v7, /device:TPU:0, one launch (start us, length us, event | category | flops | bytes accessed | tf_op | source)
XLA Modules:
  0.0 66.4 jit_solution(10864430087155490323)
XLA Ops:
  0.6 1.2 %shard_map.68 = (bf16[1024,1024]{1,0:T(8,128)(2,1)S(1)}, bf16[1024,1024]{1,0:T(8,128)(2,1)S(1)}, f32[64,1024]{1,0:T(8,128)S(1)}) custom-call(f32[1024,1024]{1,0:T(8,128)} %next_ref.3, f32[64,1024]{1,0:T(8,128)} %start_ref.7), custom_call_target="tpu_custom_call" | custom-call | flops 402653184 | tf_op jit(solution)/shard_map/pallas_call | solution.py:418
  1.8 1.2 %copy-done = f32[1024,1024]{1,0:T(8,128)S(1)} copy-done((f32[1024,1024]{1,0:T(8,128)S(1)}, f32[1024,1024]{1,0:T(8,128)}, u32[]{:S(2)}) %copy-start) | copy-done | bytes 4194328
  3.0 2.1 %shard_map.69 = (bf16[1024,1024]{1,0:T(8,128)(2,1)S(1)}, bf16[1024,1024]{1,0:T(8,128)(2,1)S(1)}, bf16[1024,1024]{1,0:T(8,128)(2,1)S(1)}, bf16[1024,1024]{1,0:T(8...) custom-call(f32[1024,1024]{1,0:T(8,128)} %next_ref.3, ...), custom_call_target="tpu_custom_call", output_to_operand_aliasing={{0}: (3, {}), {1}: (4, {})} | custom-call | flops 402653184 | tf_op jit(solution)/shard_map/pallas_call | solution.py:418
  5.1 0.4 collective-permute-start
  5.5 0.7 %collective-permute-start.1 = (f32[64,1024]{1,0:T(8,128)S(1)}, f32[64,1024]{1,0:T(8,128)S(1)}, u32[]{:S(2)}, u32[]{:S(2)}) collective-permute-start(f32[64,1024]{1,0:T(8,128)S(1)} %get-tuple-element.42), channel_id=1, source_target_pairs={{1,2},{2,1},{3,4},{4,3},{5,6},{6,5},{7,8},{8,7},{9,10},{10,9},{11,... | collective-permute-start | bytes 786440 | tf_op jit(solution)/shard_map/ppermute | solution.py:448
  6.1 0.6 collective-permute-done.got_pair_ref
  6.7 2.4 %shard_map.70 = (bf16[1024,1024]{1,0:T(8,128)(2,1)S(1)}, bf16[1024,1024]{1,0:T(8,128)(2,1)S(1)}, bf16[1024,1024]{1,0:T(8,128)(2,1)S(1)}, bf16[1024,1024]{1,0:T(8,128)(2,1)S(1)}, f32[64,1024]{1,0:T(8,128)S(1)}) custom-call(f32[64,1024]{1,0:T(8,128)S(1)} %get-tuple-element.35.own_ref, ...), custom_call_target="tpu_custom_call", output_to_operand_aliasing={{0}: (8, {}), {1}: (9, {})} | custom-call | flops 402653184 | tf_op jit(solution)/shard_map/pallas_call | solution.py:418
  9.1 0.0 collective-permute-done.1.got_ref
  9.1 0.6 shard_map.71
  9.7 7.7 %collective-permute-start.2 = (f32[64,1024]{1,0:T(8,128)S(1)}, f32[64,1024]{1,0:T(8,128)S(1)}, u32[]{:S(2)}, u32[]{:S(2)}) collective-permute-start(f32[64,1024]{1,0:T(8,128)S(1)} %get-tuple-element.49), channel_id=1, source_target_pairs={{0,1},{1,0},{2,3},{3,2},{4,5},{5,4},{6,7},{7,6},{8,9},{9,8},{10,11... | collective-permute-start | bytes 786440 | tf_op jit(solution)/shard_map/ppermute | solution.py:448
  17.4 0.7 %collective-permute-start.3 = (f32[64,1024]{1,0:T(8,128)S(1)}, f32[64,1024]{1,0:T(8,128)S(1)}, u32[]{:S(2)}, u32[]{:S(2)}) collective-permute-start(f32[64,1024]{1,0:T(8,128)S(1)} %get-tuple-element.50), channel_id=1, source_target_pairs={{1,2},{3,4},{5,6},{7,8},{9,10},{11,12},{13,14},{17,18},{19,20},{21... | collective-permute-start | bytes 786440 | tf_op jit(solution)/shard_map/ppermute | solution.py:448
  18.1 0.7 %collective-permute-start.4 = (f32[64,1024]{1,0:T(8,128)S(1)}, f32[64,1024]{1,0:T(8,128)S(1)}, u32[]{:S(2)}, u32[]{:S(2)}) collective-permute-start(f32[64,1024]{1,0:T(8,128)S(1)} %get-tuple-element.45.field_ref.before_ref.zero_ref), channel_id=1, source_target_pairs={{2,1},{4,3},{6,5},{8,7},{10,9},{12,11},{14,13},{18,17},{20,19},{22... | collective-permute-start | bytes 786440 | tf_op jit(solution)/shard_map/ppermute | solution.py:448
  18.8 0.8 %shard_map.72 = (f32[64,1024]{1,0:T(8,128)S(1)}, f32[64,128]{1,0:T(8,128)S(1)}) custom-call(f32[64,1024]{1,0:T(8,128)S(1)} %get-tuple-element.45.field_ref.before_ref.zero_ref, bf16[1024,1024]{1,0:T(8,128)(2,1)S(1)} %get-tuple-element.46.high_ref, bf16[1024,1024]{1,0:T(8,128)(2,1)S(1)} %get-tuple-element.47.low_ref), custom_call_target="tpu_custom_call" | custom-call | flops 402653184 | tf_op jit(solution)/shard_map/pallas_call | solution.py:418
  19.6 0.0 collective-permute-done.2.got_pair_ref
  19.6 0.6 shard_map.73.base_ref
  20.1 0.0 collective-permute-done.3.got_ref
  20.2 0.6 shard_map.76
  20.8 9.4 %collective-permute-start.5 = (f32[64,1024]{1,0:T(8,128)S(1)}, f32[64,1024]{1,0:T(8,128)S(1)}, u32[]{:S(2)}, u32[]{:S(2)}) collective-permute-start(f32[64,1024]{1,0:T(8,128)S(1)} %get-tuple-element.54), channel_id=1, source_target_pairs={{0,1},{1,0},{2,3},{3,2},{4,5},{5,4},{6,7},{7,6},{8,9},{9,8},{10,11... | collective-permute-start | bytes 786440 | tf_op jit(solution)/shard_map/ppermute | solution.py:448
  30.2 0.7 %collective-permute-start.7 = (f32[64,1024]{1,0:T(8,128)S(1)}, f32[64,1024]{1,0:T(8,128)S(1)}, u32[]{:S(2)}, u32[]{:S(2)}) collective-permute-start(f32[64,1024]{1,0:T(8,128)S(1)} %shard_map.74.after_ref.even_ref), channel_id=1, source_target_pairs={{2,1},{4,3},{6,5},{8,7},{10,9},{12,11},{14,13},{18,17},{20,19},{22... | collective-permute-start | bytes 786440 | tf_op jit(solution)/shard_map/ppermute | solution.py:448
  30.9 0.7 %collective-permute-start.6 = (f32[64,1024]{1,0:T(8,128)S(1)}, f32[64,1024]{1,0:T(8,128)S(1)}, u32[]{:S(2)}, u32[]{:S(2)}) collective-permute-start(f32[64,1024]{1,0:T(8,128)S(1)} %get-tuple-element.55), channel_id=1, source_target_pairs={{1,2},{3,4},{5,6},{7,8},{9,10},{11,12},{13,14},{17,18},{19,20},{21... | collective-permute-start | bytes 786440 | tf_op jit(solution)/shard_map/ppermute | solution.py:448
  31.6 0.8 %shard_map.77 = (f32[64,1024]{1,0:T(8,128)S(1)}, f32[64,128]{1,0:T(8,128)S(1)}) custom-call(f32[64,1024]{1,0:T(8,128)S(1)} %get-tuple-element.45.field_ref.before_ref.zero_ref, f32[64,1024]{1,0:T(8,128)S(1)} %get-tuple-element.52.field_ref.before_ref.one_ref, bf16[1024,1024]{1,0:T(8,128)(2,1)S(1)} %get-tuple-element.46.high_ref, ...), custom_call_target="tpu_custom_call" | custom-call | flops 402653184 | tf_op jit(solution)/shard_map/pallas_call | solution.py:418
  32.4 0.6 shard_map.78.after_ref.base_ref
  33.0 0.6 shard_map.80
  33.6 9.3 %collective-permute-start.8 = (f32[64,1024]{1,0:T(8,128)S(1)}, f32[64,1024]{1,0:T(8,128)S(1)}, u32[]{:S(2)}, u32[]{:S(2)}) collective-permute-start(f32[64,1024]{1,0:T(8,128)S(1)} %get-tuple-element.59), channel_id=1, source_target_pairs={{0,1},{1,0},{2,3},{3,2},{4,5},{5,4},{6,7},{7,6},{8,9},{9,8},{10,11... | collective-permute-start | bytes 786440 | tf_op jit(solution)/shard_map/ppermute | solution.py:448
  42.9 0.7 %collective-permute-start.9 = (f32[64,1024]{1,0:T(8,128)S(1)}, f32[64,1024]{1,0:T(8,128)S(1)}, u32[]{:S(2)}, u32[]{:S(2)}) collective-permute-start(f32[64,1024]{1,0:T(8,128)S(1)} %get-tuple-element.60), channel_id=1, source_target_pairs={{1,2},{3,4},{5,6},{7,8},{9,10},{11,12},{13,14},{17,18},{19,20},{21... | collective-permute-start | bytes 786440 | tf_op jit(solution)/shard_map/ppermute | solution.py:448
  43.6 0.7 %collective-permute-start.10 = (f32[64,1024]{1,0:T(8,128)S(1)}, f32[64,1024]{1,0:T(8,128)S(1)}, u32[]{:S(2)}, u32[]{:S(2)}) collective-permute-start(f32[64,1024]{1,0:T(8,128)S(1)} %get-tuple-element.57.field_ref.two_ref), channel_id=1, source_target_pairs={{2,1},{4,3},{6,5},{8,7},{10,9},{12,11},{14,13},{18,17},{20,19},{22... | collective-permute-start | bytes 786440 | tf_op jit(solution)/shard_map/ppermute | solution.py:448
  44.3 0.8 %shard_map.81 = (f32[64,1024]{1,0:T(8,128)S(1)}, f32[64,128]{1,0:T(8,128)S(1)}) custom-call(f32[64,1024]{1,0:T(8,128)S(1)} %get-tuple-element.52.field_ref.before_ref.one_ref, f32[64,1024]{1,0:T(8,128)S(1)} %get-tuple-element.57.field_ref.two_ref, bf16[1024,1024]{1,0:T(8,128)(2,1)S(1)} %get-tuple-element.46.high_ref, ...), custom_call_target="tpu_custom_call" | custom-call | flops 402653184 | tf_op jit(solution)/shard_map/pallas_call | solution.py:418
  45.1 0.0 collective-permute-done.8.got_pair_ref
  45.1 0.2 shard_map.82
  45.3 19.5 %all_to_all.5.table_ref = f32[16,8,128]{2,1,0:T(8,128)S(1)} all-to-all(f32[16,8,128]{2,1,0:T(8,128)S(1)} %shard_map.82), channel_id=1, replica_groups=mesh['parts'=2,'snp'=16] {'snp'}, dimensions={0} | all-to-all | bytes 131072 | tf_op jit(solution)/shard_map/all_to_all | solution.py:508
  64.9 0.2 shard_map.83.weights_ref
  65.0 1.4 %shard_map.84 = (f32[64,1024]{1,0:T(8,128)}, f32[64,1024]{1,0:T(8,128)}) custom-call(f32[64,128]{1,0:T(8,128)S(1)} %shard_map.83.weights_ref, f32[64,1024]{1,0:T(8,128)S(1)} %copy-done.1, f32[64,1024]{1,0:T(8,128)S(1)} %get-tuple-element.45.field_ref.before_ref.zero_ref, f32[64,1024]{1,0:T(8,128)S(1)} %get-tuple-element.52.field_ref.before_ref.one_ref, ...), custom_call_target="tpu_custom_call" | custom-call | tf_op jit(solution)/shard_map/pallas_call | solution.py:418
  (16 shorter events, 0.1 us)
Async XLA Ops:
  0.6 1.2 %copy-start.1 = (f32[64,1024]{1,0:T(8,128)S(1)}, f32[64,1024]{1,0:T(8,128)}, u32[]{:S(2)}) copy-start(f32[64,1024]{1,0:T(8,128)} %start_ref.7) | copy-start | bytes 786436
  0.6 2.4 %copy-start = (f32[1024,1024]{1,0:T(8,128)S(1)}, f32[1024,1024]{1,0:T(8,128)}, u32[]{:S(2)}) copy-start(f32[1024,1024]{1,0:T(8,128)} %local_ref.3) | copy-start | bytes 12582916
  3.0 3.7 %copy-start.2 = (f32[64,1024]{1,0:T(8,128)S(1)}, f32[64,1024]{1,0:T(8,128)}, u32[]{:S(2)}) copy-start(f32[64,1024]{1,0:T(8,128)} %marginal_ref.1) | copy-start | bytes 786436
  3.0 3.7 %copy-start.3 = (f32[64,1]{0,1:T(1,128)S(1)}, f32[64,1]{0,1:T(1,128)}, u32[]{:S(2)}) copy-start(f32[64,1]{0,1:T(1,128)} %param.7) | copy-start | bytes 772
  5.1 1.6 %collective-permute-start = (f32[64,1024]{1,0:T(8,128)S(1)}, f32[64,1024]{1,0:T(8,128)S(1)}, u32[]{:S(2)}, u32[]{:S(2)}) collective-permute-start(f32[64,1024]{1,0:T(8,128)S(1)} %get-tuple-element.36), channel_id=1, source_target_pairs={{0,1},{1,0},{2,3},{3,2},{4,5},{5,4},{6,7},{7,6},{8,9},{9,8},{10,11... | collective-permute-start | bytes 786440 | tf_op jit(solution)/shard_map/ppermute | solution.py:448
  5.5 3.6 %collective-permute-start.1 = (f32[64,1024]{1,0:T(8,128)S(1)}, f32[64,1024]{1,0:T(8,128)S(1)}, u32[]{:S(2)}, u32[]{:S(2)}) collective-permute-start(f32[64,1024]{1,0:T(8,128)S(1)} %get-tuple-element.42), channel_id=1, source_target_pairs={{1,2},{2,1},{3,4},{4,3},{5,6},{6,5},{7,8},{8,7},{9,10},{10,9},{11,... | collective-permute-start | bytes 786440 | tf_op jit(solution)/shard_map/ppermute | solution.py:448
  9.7 9.9 %collective-permute-start.2 = (f32[64,1024]{1,0:T(8,128)S(1)}, f32[64,1024]{1,0:T(8,128)S(1)}, u32[]{:S(2)}, u32[]{:S(2)}) collective-permute-start(f32[64,1024]{1,0:T(8,128)S(1)} %get-tuple-element.49), channel_id=1, source_target_pairs={{0,1},{1,0},{2,3},{3,2},{4,5},{5,4},{6,7},{7,6},{8,9},{9,8},{10,11... | collective-permute-start | bytes 786440 | tf_op jit(solution)/shard_map/ppermute | solution.py:448
  17.4 2.7 %collective-permute-start.3 = (f32[64,1024]{1,0:T(8,128)S(1)}, f32[64,1024]{1,0:T(8,128)S(1)}, u32[]{:S(2)}, u32[]{:S(2)}) collective-permute-start(f32[64,1024]{1,0:T(8,128)S(1)} %get-tuple-element.50), channel_id=1, source_target_pairs={{1,2},{3,4},{5,6},{7,8},{9,10},{11,12},{13,14},{17,18},{19,20},{21... | collective-permute-start | bytes 786440 | tf_op jit(solution)/shard_map/ppermute | solution.py:448
  18.1 2.1 %collective-permute-start.4 = (f32[64,1024]{1,0:T(8,128)S(1)}, f32[64,1024]{1,0:T(8,128)S(1)}, u32[]{:S(2)}, u32[]{:S(2)}) collective-permute-start(f32[64,1024]{1,0:T(8,128)S(1)} %get-tuple-element.45.field_ref.before_ref.zero_ref), channel_id=1, source_target_pairs={{2,1},{4,3},{6,5},{8,7},{10,9},{12,11},{14,13},{18,17},{20,19},{22... | collective-permute-start | bytes 786440 | tf_op jit(solution)/shard_map/ppermute | solution.py:448
  20.8 11.6 %collective-permute-start.5 = (f32[64,1024]{1,0:T(8,128)S(1)}, f32[64,1024]{1,0:T(8,128)S(1)}, u32[]{:S(2)}, u32[]{:S(2)}) collective-permute-start(f32[64,1024]{1,0:T(8,128)S(1)} %get-tuple-element.54), channel_id=1, source_target_pairs={{0,1},{1,0},{2,3},{3,2},{4,5},{5,4},{6,7},{7,6},{8,9},{9,8},{10,11... | collective-permute-start | bytes 786440 | tf_op jit(solution)/shard_map/ppermute | solution.py:448
  30.2 2.7 %collective-permute-start.7 = (f32[64,1024]{1,0:T(8,128)S(1)}, f32[64,1024]{1,0:T(8,128)S(1)}, u32[]{:S(2)}, u32[]{:S(2)}) collective-permute-start(f32[64,1024]{1,0:T(8,128)S(1)} %shard_map.74.after_ref.even_ref), channel_id=1, source_target_pairs={{2,1},{4,3},{6,5},{8,7},{10,9},{12,11},{14,13},{18,17},{20,19},{22... | collective-permute-start | bytes 786440 | tf_op jit(solution)/shard_map/ppermute | solution.py:448
  30.9 2.1 %collective-permute-start.6 = (f32[64,1024]{1,0:T(8,128)S(1)}, f32[64,1024]{1,0:T(8,128)S(1)}, u32[]{:S(2)}, u32[]{:S(2)}) collective-permute-start(f32[64,1024]{1,0:T(8,128)S(1)} %get-tuple-element.55), channel_id=1, source_target_pairs={{1,2},{3,4},{5,6},{7,8},{9,10},{11,12},{13,14},{17,18},{19,20},{21... | collective-permute-start | bytes 786440 | tf_op jit(solution)/shard_map/ppermute | solution.py:448
  33.6 11.5 %collective-permute-start.8 = (f32[64,1024]{1,0:T(8,128)S(1)}, f32[64,1024]{1,0:T(8,128)S(1)}, u32[]{:S(2)}, u32[]{:S(2)}) collective-permute-start(f32[64,1024]{1,0:T(8,128)S(1)} %get-tuple-element.59), channel_id=1, source_target_pairs={{0,1},{1,0},{2,3},{3,2},{4,5},{5,4},{6,7},{7,6},{8,9},{9,8},{10,11... | collective-permute-start | bytes 786440 | tf_op jit(solution)/shard_map/ppermute | solution.py:448
  42.9 2.2 %collective-permute-start.9 = (f32[64,1024]{1,0:T(8,128)S(1)}, f32[64,1024]{1,0:T(8,128)S(1)}, u32[]{:S(2)}, u32[]{:S(2)}) collective-permute-start(f32[64,1024]{1,0:T(8,128)S(1)} %get-tuple-element.60), channel_id=1, source_target_pairs={{1,2},{3,4},{5,6},{7,8},{9,10},{11,12},{13,14},{17,18},{19,20},{21... | collective-permute-start | bytes 786440 | tf_op jit(solution)/shard_map/ppermute | solution.py:448
  43.6 21.4 %collective-permute-start.10 = (f32[64,1024]{1,0:T(8,128)S(1)}, f32[64,1024]{1,0:T(8,128)S(1)}, u32[]{:S(2)}, u32[]{:S(2)}) collective-permute-start(f32[64,1024]{1,0:T(8,128)S(1)} %get-tuple-element.57.field_ref.two_ref), channel_id=1, source_target_pairs={{2,1},{4,3},{6,5},{8,7},{10,9},{12,11},{14,13},{18,17},{20,19},{22... | collective-permute-start | bytes 786440 | tf_op jit(solution)/shard_map/ppermute | solution.py:448

commit v8 on v6

--- a/solution.py
+++ b/solution.py
@@ -119,16 +119,17 @@
         take_next(next_ref, start_ref, high_n, low_n, cross_ref, raw, sems, field)
 
 
-def begin_even_kernel(
-    next_ref, local_ref, start_ref, high_n_in, low_n_in,
-    high_n, low_n, high_l, low_l, own_ref, pair_ref, raw, sems,
-):
-    del high_n_in, low_n_in
+def local_odd_kernel(local_ref, start_ref, after_ref, high_l, low_l, own_ref, pair_ref):
+    del after_ref
 
     @pl.when(is_odd())
     def _():
         take_local(local_ref, start_ref, high_l, low_l, own_ref)
         pair_ref[...] = start_ref[...]
+
+
+def begin_even_kernel(next_ref, start_ref, high_n_in, low_n_in, pair_in, high_n, low_n, pair_ref, raw, sems):
+    del high_n_in, low_n_in, pair_in
 
     @pl.when(jnp.logical_not(is_odd()))
     def _():
@@ -394,11 +395,13 @@
         begin_odd_kernel, [matrix, matrix, field], next_block, warm_start,
         spaces={0: hbm, 1: hbm}, scratch=copies, flops=work,
     )
+    high_l, low_l, own, pair = run(
+        local_odd_kernel, [matrix, matrix, field, field], local_block, warm_start, cross, flops=work
+    )
     up = shift(cross, upward)
-    high_n, low_n, high_l, low_l, own, pair = run(
-        begin_even_kernel, [matrix, matrix, matrix, matrix, field, field],
-        next_block, local_block, warm_start, high_n, low_n,
-        spaces={0: hbm}, scratch=copies[::2], aliases={3: 0, 4: 1}, flops=work,
+    high_n, low_n, pair = run(
+        begin_even_kernel, [matrix, matrix, field], next_block, warm_start, high_n, low_n, pair,
+        spaces={0: hbm}, scratch=copies[::2], aliases={2: 0, 3: 1, 4: 2}, flops=work,
     )
     got_pair = shift(pair, on_chip)
     rest, high_up, low_up = run(
@@ -443,7 +446,7 @@
         else:
             odd_field, cross = run(
                 odd, [field, field],
-                own, got_pair, down, high_n, low_n, high_up, low_up, base, flops=work,
+                own, got_pair, down, high_n, low_n, high_up, low_up, own, flops=work,
             )
             next_up = shift(cross, upward)
             merged, pair = run(join, [field, field], base, up, odd_field, high_n, low_n, flops=work)

time: 64.7 us -> 64.7 us (level)
    pallas_call x19 -> x20, Pallas kernels: 11 us -> 11.1 us  [call(): pl.pallas_call(kernel, out_shape=[make(shape, dtype) for shape, dtype in...]
where the time goes in v8:
time: 64.7 us; the launch traced here: 64.4 us
  starting transfers between devices  31.1 us (48%)
  blocking collectives  19.5 us (30%)
  Pallas kernels  11.1 us (17%)
  local copies, waits for them, and re-layouts  1.39 us (2%)
  between operations  0.91 us (1%)
    ppermute x12, starting transfers between devices, shift(): return lax.ppermute(value, 'snp', route)  31.1 us
    all_to_all x1, blocking collectives, on_device(): moments = lax.all_to_all(moments, 'snp', 0, 0)  19.5 us
    pallas_call x20, Pallas kernels, call(): pl.pallas_call(kernel, out_shape=[make(shape, dtype) for shape, dtype in...  11.1 us
    unnamed x8, local copies, waits for them, and re-layouts  1.39 us
  transfers between devices with their start and end apart: 12, of which 1 were waited for; matrix products, arithmetic and copies ran while one was open for 0% of the time, Pallas kernels for 12%

profile of v8, /device:TPU:0, one launch (start us, length us, event | category | flops | bytes accessed | tf_op | source)
XLA Modules:
  0.0 64.4 jit_solution(15539983316708284031)
XLA Ops:
  0.6 0.8 %collective-permute-start.1 = (f32[64,1024]{1,0:T(8,128)}, f32[64,1024]{1,0:T(8,128)S(1)}, u32[]{:S(2)}, u32[]{:S(2)}) collective-permute-start(f32[64,1024]{1,0:T(8,128)} %start_ref.11), channel_id=1, source_target_pairs={{2,1},{4,3},{6,5},{8,7},{10,9},{12,11},{14,13},{18,17},{20,19},{22... | collective-permute-start | bytes 786440 | tf_op jit(solution)/shard_map/ppermute | solution.py:386
  1.5 0.1 shard_map.68
  1.5 0.0 copy-done.1
  1.6 1.3 %copy-done = f32[1024,1024]{1,0:T(8,128)S(1)} copy-done((f32[1024,1024]{1,0:T(8,128)S(1)}, f32[1024,1024]{1,0:T(8,128)}, u32[]{:S(2)}) %copy-start) | copy-done | bytes 4194328
  2.9 2.1 %shard_map.70 = (bf16[1024,1024]{1,0:T(8,128)(2,1)S(1)}, bf16[1024,1024]{1,0:T(8,128)(2,1)S(1)}, f32[64,1024]{1,0:T(8,128)S(1)}) custom-call(f32[1024,1024]{1,0:T(8,128)} %next_ref.3, f32[64,1024]{1,0:T(8,128)S(1)} %copy-done.1, bf16[1024,1024]{1,0:T(8,128)(2,1)S(1)} %get-tuple-element.38.high_n_in, ...), custom_call_target="tpu_custom_call", output_to_operand_aliasing={{0}: (2, {}), {1}: (3, {}), {2}: (4, {})} | custom-call | flops 402653184 | tf_op jit(solution)/shard_map/pallas_call | solution.py:357
  5.0 1.1 %collective-permute-start = (f32[64,1024]{1,0:T(8,128)S(1)}, f32[64,1024]{1,0:T(8,128)S(1)}, u32[]{:S(2)}, u32[]{:S(2)}) collective-permute-start(f32[64,1024]{1,0:T(8,128)S(1)} %get-tuple-element.42), channel_id=1, source_target_pairs={{0,1},{1,0},{2,3},{3,2},{4,5},{5,4},{6,7},{7,6},{8,9},{9,8},{10,11... | collective-permute-start | bytes 786440 | tf_op jit(solution)/shard_map/ppermute | solution.py:386
  6.2 0.7 %collective-permute-start.2 = (f32[64,1024]{1,0:T(8,128)S(1)}, f32[64,1024]{1,0:T(8,128)S(1)}, u32[]{:S(2)}, u32[]{:S(2)}) collective-permute-start(f32[64,1024]{1,0:T(8,128)S(1)} %get-tuple-element.40.after_ref), channel_id=1, source_target_pairs={{1,2},{3,4},{5,6},{7,8},{9,10},{11,12},{13,14},{17,18},{19,20},{21... | collective-permute-start | bytes 786440 | tf_op jit(solution)/shard_map/ppermute | solution.py:386
  6.9 0.0 collective-permute-done.1.got_ref
  6.9 0.4 collective-permute-done.got_pair_ref
  7.3 1.9 %shard_map.73 = (bf16[1024,1024]{1,0:T(8,128)(2,1)S(1)}, bf16[1024,1024]{1,0:T(8,128)(2,1)S(1)}, bf16[1024,1024]{1,0:T(8,128)(2,1)S(1)}, bf16[1024,1024]{1,0:T(8,128)(2,1)S(1)}, f32[64,1024]{1,0:T(8,128)S(1)}) custom-call(f32[1024,1024]{1,0:T(8,128)S(1)} %copy-done, ...), custom_call_target="tpu_custom_call", output_to_operand_aliasing={{0}: (7, {}), {1}: (8, {}), {2}: (9, {}), {3}: (10, {})} | custom-call | flops 402653184 | tf_op jit(solution)/shard_map/pallas_call | solution.py:357
  9.2 0.0 collective-permute-done.2.got_ref
  9.2 0.6 shard_map.74
  9.8 4.1 %collective-permute-start.3 = (f32[64,1024]{1,0:T(8,128)S(1)}, f32[64,1024]{1,0:T(8,128)S(1)}, u32[]{:S(2)}, u32[]{:S(2)}) collective-permute-start(f32[64,1024]{1,0:T(8,128)S(1)} %get-tuple-element.57), channel_id=1, source_target_pairs={{0,1},{1,0},{2,3},{3,2},{4,5},{5,4},{6,7},{7,6},{8,9},{9,8},{10,11... | collective-permute-start | bytes 786440 | tf_op jit(solution)/shard_map/ppermute | solution.py:386
  13.9 0.7 %collective-permute-start.4 = (f32[64,1024]{1,0:T(8,128)S(1)}, f32[64,1024]{1,0:T(8,128)S(1)}, u32[]{:S(2)}, u32[]{:S(2)}) collective-permute-start(f32[64,1024]{1,0:T(8,128)S(1)} %get-tuple-element.60), channel_id=1, source_target_pairs={{1,2},{3,4},{5,6},{7,8},{9,10},{11,12},{13,14},{17,18},{19,20},{21... | collective-permute-start | bytes 786440 | tf_op jit(solution)/shard_map/ppermute | solution.py:386
  14.6 0.7 %collective-permute-start.5 = (f32[64,1024]{1,0:T(8,128)S(1)}, f32[64,1024]{1,0:T(8,128)S(1)}, u32[]{:S(2)}, u32[]{:S(2)}) collective-permute-start(f32[64,1024]{1,0:T(8,128)S(1)} %get-tuple-element.53.field_ref.before_ref.zero_ref), channel_id=1, source_target_pairs={{2,1},{4,3},{6,5},{8,7},{10,9},{12,11},{14,13},{18,17},{20,19},{22... | collective-permute-start | bytes 786440 | tf_op jit(solution)/shard_map/ppermute | solution.py:386
  15.3 0.8 %shard_map.75 = (f32[64,1024]{1,0:T(8,128)S(1)}, f32[64,128]{1,0:T(8,128)S(1)}) custom-call(f32[64,1024]{1,0:T(8,128)S(1)} %get-tuple-element.53.field_ref.before_ref.zero_ref, bf16[1024,1024]{1,0:T(8,128)(2,1)S(1)} %get-tuple-element.54.high_ref, bf16[1024,1024]{1,0:T(8,128)(2,1)S(1)} %get-tuple-element.55.low_ref), custom_call_target="tpu_custom_call" | custom-call | flops 402653184 | tf_op jit(solution)/shard_map/pallas_call | solution.py:357
  16.1 0.6 shard_map.76.base_ref
  16.7 0.6 shard_map.79
  17.3 10.4 %collective-permute-start.6 = (f32[64,1024]{1,0:T(8,128)S(1)}, f32[64,1024]{1,0:T(8,128)S(1)}, u32[]{:S(2)}, u32[]{:S(2)}) collective-permute-start(f32[64,1024]{1,0:T(8,128)S(1)} %get-tuple-element.64), channel_id=1, source_target_pairs={{0,1},{1,0},{2,3},{3,2},{4,5},{5,4},{6,7},{7,6},{8,9},{9,8},{10,11... | collective-permute-start | bytes 786440 | tf_op jit(solution)/shard_map/ppermute | solution.py:386
  27.7 0.7 %collective-permute-start.8 = (f32[64,1024]{1,0:T(8,128)S(1)}, f32[64,1024]{1,0:T(8,128)S(1)}, u32[]{:S(2)}, u32[]{:S(2)}) collective-permute-start(f32[64,1024]{1,0:T(8,128)S(1)} %shard_map.77.after_ref.even_ref), channel_id=1, source_target_pairs={{2,1},{4,3},{6,5},{8,7},{10,9},{12,11},{14,13},{18,17},{20,19},{22... | collective-permute-start | bytes 786440 | tf_op jit(solution)/shard_map/ppermute | solution.py:386
  28.4 0.7 %collective-permute-start.7 = (f32[64,1024]{1,0:T(8,128)S(1)}, f32[64,1024]{1,0:T(8,128)S(1)}, u32[]{:S(2)}, u32[]{:S(2)}) collective-permute-start(f32[64,1024]{1,0:T(8,128)S(1)} %get-tuple-element.65), channel_id=1, source_target_pairs={{1,2},{3,4},{5,6},{7,8},{9,10},{11,12},{13,14},{17,18},{19,20},{21... | collective-permute-start | bytes 786440 | tf_op jit(solution)/shard_map/ppermute | solution.py:386
  29.1 0.8 %shard_map.80 = (f32[64,1024]{1,0:T(8,128)S(1)}, f32[64,128]{1,0:T(8,128)S(1)}) custom-call(f32[64,1024]{1,0:T(8,128)S(1)} %get-tuple-element.53.field_ref.before_ref.zero_ref, f32[64,1024]{1,0:T(8,128)S(1)} %get-tuple-element.62.field_ref.before_ref.one_ref, bf16[1024,1024]{1,0:T(8,128)(2,1)S(1)} %get-tuple-element.54.high_ref, ...), custom_call_target="tpu_custom_call" | custom-call | flops 402653184 | tf_op jit(solution)/shard_map/pallas_call | solution.py:357
  29.9 0.6 shard_map.81.base_ref
  30.5 0.6 shard_map.83
  31.1 9.9 %collective-permute-start.9 = (f32[64,1024]{1,0:T(8,128)S(1)}, f32[64,1024]{1,0:T(8,128)S(1)}, u32[]{:S(2)}, u32[]{:S(2)}) collective-permute-start(f32[64,1024]{1,0:T(8,128)S(1)} %get-tuple-element.69), channel_id=1, source_target_pairs={{0,1},{1,0},{2,3},{3,2},{4,5},{5,4},{6,7},{7,6},{8,9},{9,8},{10,11... | collective-permute-start | bytes 786440 | tf_op jit(solution)/shard_map/ppermute | solution.py:386
  40.9 0.7 %collective-permute-start.10 = (f32[64,1024]{1,0:T(8,128)S(1)}, f32[64,1024]{1,0:T(8,128)S(1)}, u32[]{:S(2)}, u32[]{:S(2)}) collective-permute-start(f32[64,1024]{1,0:T(8,128)S(1)} %get-tuple-element.70), channel_id=1, source_target_pairs={{1,2},{3,4},{5,6},{7,8},{9,10},{11,12},{13,14},{17,18},{19,20},{21... | collective-permute-start | bytes 786440 | tf_op jit(solution)/shard_map/ppermute | solution.py:386
  41.6 0.7 %collective-permute-start.11 = (f32[64,1024]{1,0:T(8,128)S(1)}, f32[64,1024]{1,0:T(8,128)S(1)}, u32[]{:S(2)}, u32[]{:S(2)}) collective-permute-start(f32[64,1024]{1,0:T(8,128)S(1)} %get-tuple-element.67.field_ref.two_ref), channel_id=1, source_target_pairs={{2,1},{4,3},{6,5},{8,7},{10,9},{12,11},{14,13},{18,17},{20,19},{22... | collective-permute-start | bytes 786440 | tf_op jit(solution)/shard_map/ppermute | solution.py:386
  42.3 0.8 %shard_map.84 = (f32[64,1024]{1,0:T(8,128)S(1)}, f32[64,128]{1,0:T(8,128)S(1)}) custom-call(f32[64,1024]{1,0:T(8,128)S(1)} %get-tuple-element.62.field_ref.before_ref.one_ref, f32[64,1024]{1,0:T(8,128)S(1)} %get-tuple-element.67.field_ref.two_ref, bf16[1024,1024]{1,0:T(8,128)(2,1)S(1)} %get-tuple-element.54.high_ref, ...), custom_call_target="tpu_custom_call" | custom-call | flops 402653184 | tf_op jit(solution)/shard_map/pallas_call | solution.py:357
  43.1 0.3 shard_map.85
  43.4 19.5 %all_to_all.5.table_ref = f32[16,8,128]{2,1,0:T(8,128)S(1)} all-to-all(f32[16,8,128]{2,1,0:T(8,128)S(1)} %shard_map.85), channel_id=1, replica_groups=mesh['parts'=2,'snp'=16] {'snp'}, dimensions={0} | all-to-all | bytes 131072 | tf_op jit(solution)/shard_map/all_to_all | solution.py:457
  62.9 0.2 shard_map.86.weights_ref
  63.1 1.4 %shard_map.87 = (f32[64,1024]{1,0:T(8,128)}, f32[64,1024]{1,0:T(8,128)}) custom-call(f32[64,128]{1,0:T(8,128)S(1)} %shard_map.86.weights_ref, f32[64,1024]{1,0:T(8,128)S(1)} %copy-done.1, f32[64,1024]{1,0:T(8,128)S(1)} %get-tuple-element.53.field_ref.before_ref.zero_ref, f32[64,1024]{1,0:T(8,128)S(1)} %get-tuple-element.62.field_ref.before_ref.one_ref, ...), custom_call_target="tpu_custom_call" | custom-call | tf_op jit(solution)/shard_map/pallas_call | solution.py:357
  (21 shorter events, 0.1 us)
Async XLA Ops:
  0.6 1.0 %copy-start.1 = (f32[64,1024]{1,0:T(8,128)S(1)}, f32[64,1024]{1,0:T(8,128)}, u32[]{:S(2)}) copy-start(f32[64,1024]{1,0:T(8,128)} %start_ref.11) | copy-start | bytes 786436
  0.6 2.3 %copy-start = (f32[1024,1024]{1,0:T(8,128)S(1)}, f32[1024,1024]{1,0:T(8,128)}, u32[]{:S(2)}) copy-start(f32[1024,1024]{1,0:T(8,128)} %local_ref.3) | copy-start | bytes 12582916
  0.6 6.2 %collective-permute-start.1 = (f32[64,1024]{1,0:T(8,128)}, f32[64,1024]{1,0:T(8,128)S(1)}, u32[]{:S(2)}, u32[]{:S(2)}) collective-permute-start(f32[64,1024]{1,0:T(8,128)} %start_ref.11), channel_id=1, source_target_pairs={{2,1},{4,3},{6,5},{8,7},{10,9},{12,11},{14,13},{18,17},{20,19},{22... | collective-permute-start | bytes 786440 | tf_op jit(solution)/shard_map/ppermute | solution.py:386
  2.9 3.9 %copy-start.2 = (f32[64,1024]{1,0:T(8,128)S(1)}, f32[64,1024]{1,0:T(8,128)}, u32[]{:S(2)}) copy-start(f32[64,1024]{1,0:T(8,128)} %marginal_ref.3) | copy-start | bytes 786436
  2.9 3.9 %copy-start.3 = (f32[64,1]{0,1:T(1,128)S(1)}, f32[64,1]{0,1:T(1,128)}, u32[]{:S(2)}) copy-start(f32[64,1]{0,1:T(1,128)} %param.7) | copy-start | bytes 772
  5.0 2.3 %collective-permute-start = (f32[64,1024]{1,0:T(8,128)S(1)}, f32[64,1024]{1,0:T(8,128)S(1)}, u32[]{:S(2)}, u32[]{:S(2)}) collective-permute-start(f32[64,1024]{1,0:T(8,128)S(1)} %get-tuple-element.42), channel_id=1, source_target_pairs={{0,1},{1,0},{2,3},{3,2},{4,5},{5,4},{6,7},{7,6},{8,9},{9,8},{10,11... | collective-permute-start | bytes 786440 | tf_op jit(solution)/shard_map/ppermute | solution.py:386
  6.2 3.0 %collective-permute-start.2 = (f32[64,1024]{1,0:T(8,128)S(1)}, f32[64,1024]{1,0:T(8,128)S(1)}, u32[]{:S(2)}, u32[]{:S(2)}) collective-permute-start(f32[64,1024]{1,0:T(8,128)S(1)} %get-tuple-element.40.after_ref), channel_id=1, source_target_pairs={{1,2},{3,4},{5,6},{7,8},{9,10},{11,12},{13,14},{17,18},{19,20},{21... | collective-permute-start | bytes 786440 | tf_op jit(solution)/shard_map/ppermute | solution.py:386
  9.8 6.3 %collective-permute-start.3 = (f32[64,1024]{1,0:T(8,128)S(1)}, f32[64,1024]{1,0:T(8,128)S(1)}, u32[]{:S(2)}, u32[]{:S(2)}) collective-permute-start(f32[64,1024]{1,0:T(8,128)S(1)} %get-tuple-element.57), channel_id=1, source_target_pairs={{0,1},{1,0},{2,3},{3,2},{4,5},{5,4},{6,7},{7,6},{8,9},{9,8},{10,11... | collective-permute-start | bytes 786440 | tf_op jit(solution)/shard_map/ppermute | solution.py:386
  13.9 2.7 %collective-permute-start.4 = (f32[64,1024]{1,0:T(8,128)S(1)}, f32[64,1024]{1,0:T(8,128)S(1)}, u32[]{:S(2)}, u32[]{:S(2)}) collective-permute-start(f32[64,1024]{1,0:T(8,128)S(1)} %get-tuple-element.60), channel_id=1, source_target_pairs={{1,2},{3,4},{5,6},{7,8},{9,10},{11,12},{13,14},{17,18},{19,20},{21... | collective-permute-start | bytes 786440 | tf_op jit(solution)/shard_map/ppermute | solution.py:386
  14.6 2.1 %collective-permute-start.5 = (f32[64,1024]{1,0:T(8,128)S(1)}, f32[64,1024]{1,0:T(8,128)S(1)}, u32[]{:S(2)}, u32[]{:S(2)}) collective-permute-start(f32[64,1024]{1,0:T(8,128)S(1)} %get-tuple-element.53.field_ref.before_ref.zero_ref), channel_id=1, source_target_pairs={{2,1},{4,3},{6,5},{8,7},{10,9},{12,11},{14,13},{18,17},{20,19},{22... | collective-permute-start | bytes 786440 | tf_op jit(solution)/shard_map/ppermute | solution.py:386
  17.3 12.6 %collective-permute-start.6 = (f32[64,1024]{1,0:T(8,128)S(1)}, f32[64,1024]{1,0:T(8,128)S(1)}, u32[]{:S(2)}, u32[]{:S(2)}) collective-permute-start(f32[64,1024]{1,0:T(8,128)S(1)} %get-tuple-element.64), channel_id=1, source_target_pairs={{0,1},{1,0},{2,3},{3,2},{4,5},{5,4},{6,7},{7,6},{8,9},{9,8},{10,11... | collective-permute-start | bytes 786440 | tf_op jit(solution)/shard_map/ppermute | solution.py:386
  27.7 2.7 %collective-permute-start.8 = (f32[64,1024]{1,0:T(8,128)S(1)}, f32[64,1024]{1,0:T(8,128)S(1)}, u32[]{:S(2)}, u32[]{:S(2)}) collective-permute-start(f32[64,1024]{1,0:T(8,128)S(1)} %shard_map.77.after_ref.even_ref), channel_id=1, source_target_pairs={{2,1},{4,3},{6,5},{8,7},{10,9},{12,11},{14,13},{18,17},{20,19},{22... | collective-permute-start | bytes 786440 | tf_op jit(solution)/shard_map/ppermute | solution.py:386
  28.4 2.1 %collective-permute-start.7 = (f32[64,1024]{1,0:T(8,128)S(1)}, f32[64,1024]{1,0:T(8,128)S(1)}, u32[]{:S(2)}, u32[]{:S(2)}) collective-permute-start(f32[64,1024]{1,0:T(8,128)S(1)} %get-tuple-element.65), channel_id=1, source_target_pairs={{1,2},{3,4},{5,6},{7,8},{9,10},{11,12},{13,14},{17,18},{19,20},{21... | collective-permute-start | bytes 786440 | tf_op jit(solution)/shard_map/ppermute | solution.py:386
  31.1 12.0 %collective-permute-start.9 = (f32[64,1024]{1,0:T(8,128)S(1)}, f32[64,1024]{1,0:T(8,128)S(1)}, u32[]{:S(2)}, u32[]{:S(2)}) collective-permute-start(f32[64,1024]{1,0:T(8,128)S(1)} %get-tuple-element.69), channel_id=1, source_target_pairs={{0,1},{1,0},{2,3},{3,2},{4,5},{5,4},{6,7},{7,6},{8,9},{9,8},{10,11... | collective-permute-start | bytes 786440 | tf_op jit(solution)/shard_map/ppermute | solution.py:386
  40.9 2.2 %collective-permute-start.10 = (f32[64,1024]{1,0:T(8,128)S(1)}, f32[64,1024]{1,0:T(8,128)S(1)}, u32[]{:S(2)}, u32[]{:S(2)}) collective-permute-start(f32[64,1024]{1,0:T(8,128)S(1)} %get-tuple-element.70), channel_id=1, source_target_pairs={{1,2},{3,4},{5,6},{7,8},{9,10},{11,12},{13,14},{17,18},{19,20},{21... | collective-permute-start | bytes 786440 | tf_op jit(solution)/shard_map/ppermute | solution.py:386
  41.6 21.5 %collective-permute-start.11 = (f32[64,1024]{1,0:T(8,128)S(1)}, f32[64,1024]{1,0:T(8,128)S(1)}, u32[]{:S(2)}, u32[]{:S(2)}) collective-permute-start(f32[64,1024]{1,0:T(8,128)S(1)} %get-tuple-element.67.field_ref.two_ref), channel_id=1, source_target_pairs={{2,1},{4,3},{6,5},{8,7},{10,9},{12,11},{14,13},{18,17},{20,19},{22... | collective-permute-start | bytes 786440 | tf_op jit(solution)/shard_map/ppermute | solution.py:386

commit v9 on v8

--- a/solution.py
+++ b/solution.py
@@ -192,6 +192,14 @@
     moments_ref[...] = jnp.where(lane == 0, moment(field, field), jnp.where(lane == 1, cross, 0.0))
 
 
+def own_part_kernel(wanted, before_ref, field_ref, high_ref, low_ref, *refs):
+    own_ref, moments_ref = refs[-2:]
+
+    @pl.when(is_odd() if wanted else jnp.logical_not(is_odd()))
+    def _():
+        own_kernel(before_ref, field_ref, high_ref, low_ref, own_ref, moments_ref)
+
+
 def pair_kernel(own_ref, got_pair_ref, high_up, low_up, base_ref):
     @pl.when(jnp.logical_not(is_odd()))
     def _():
@@ -239,16 +247,20 @@
     coupling(stacked(field_ref[...]), high_in, low_in, send)
 
 
-def merge_kernel(even_ref, odd_ref, high_in, low_in, field_ref, pair_ref):
+def couple_kernel(field_ref, high_in, low_in, pair_ref):
+    @pl.when(jnp.logical_not(is_odd()))
+    def _():
+        couple_even(field_ref, high_in, low_in, pair_ref)
+
+
+def merge_kernel(even_ref, odd_ref, field_ref):
     @pl.when(is_odd())
     def _():
         field_ref[...] = odd_ref[...]
-        pair_ref[...] = odd_ref[...]
 
     @pl.when(jnp.logical_not(is_odd()))
     def _():
         field_ref[...] = even_ref[...]
-        couple_even(field_ref, high_in, low_in, pair_ref)
 
 
 def join_kernel(sign, base_ref, got_ref, odd_ref, high_in, low_in, field_ref, pair_ref):
@@ -428,7 +440,15 @@
             down = shift(merged, downward)
         before = fields[-2:-1]
         kernel = own_kernel if before else functools.partial(own_kernel, None)
-        own, part = run(kernel, [field, table], *before, merged, high_l, low_l, flops=work)
+        if step == 3:
+            inputs = (*before, merged, high_l, low_l)
+            own, part = run(functools.partial(own_part_kernel, False), [field, table], *inputs, flops=work)
+            own, part = run(
+                functools.partial(own_part_kernel, True), [field, table], *inputs, own, part,
+                aliases={4: 0, 5: 1}, flops=work,
+            )
+        else:
+            own, part = run(kernel, [field, table], *before, merged, high_l, low_l, flops=work)
         tables.append(part)
         if step > ITERS:
             break
@@ -436,17 +456,20 @@
         if step % 2 == 0:
             (even_field,) = run(even_kernel, [field], base, up, ridge, flops=work)
             next_down = shift(even_field, downward)
+            (early,) = run(couple_kernel, [field], even_field, high_n, low_n, flops=work)
+            got_early = shift(early, on_chip)
             odd_field, cross = run(
                 odd, [field, field],
                 own, got_pair, down, high_n, low_n, high_up, low_up, even_field, flops=work,
             )
             up = shift(cross, upward)
             down = next_down
-            merged, pair = run(merge_kernel, [field, field], even_field, odd_field, high_n, low_n, flops=work)
+            (merged,) = run(merge_kernel, [field], even_field, odd_field, flops=work)
+            pair = merged
         else:
             odd_field, cross = run(
                 odd, [field, field],
-                own, got_pair, down, high_n, low_n, high_up, low_up, own, flops=work,
+                own, got_early, down, high_n, low_n, high_up, low_up, own, flops=work,
             )
             next_up = shift(cross, upward)
             merged, pair = run(join, [field, field], base, up, odd_field, high_n, low_n, flops=work)

time: 64.7 us -> 65.8 us (1.017)
  starting transfers between devices: 31.1 us -> 31.8 us
    ppermute x12 -> x13, starting transfers between devices: 31.1 us -> 31.8 us  [shift(): return lax.ppermute(value, 'snp', route)]
    pallas_call x20 -> x22, Pallas kernels: 11.1 us -> 11.1 us  [call(): pl.pallas_call(kernel, out_shape=[make(shape, dtype) for shape, dtype in...]
  transfers between devices with their start and end apart: 12 -> 13, of which waited for: 1 -> 1; matrix products, arithmetic and copies ran while one was open for 0% -> 0% of each run, Pallas kernels for 12% -> 13%
where the time goes in v9:
time: 65.8 us; the launch traced here: 65.5 us
  starting transfers between devices  31.8 us (48%)
  blocking collectives  19.8 us (30%)
  Pallas kernels  11.1 us (17%)
  local copies, waits for them, and re-layouts  1.39 us (2%)
  between operations  0.94 us (1%)
    ppermute x13, starting transfers between devices, shift(): return lax.ppermute(value, 'snp', route)  31.8 us
    all_to_all x1, blocking collectives, on_device(): moments = lax.all_to_all(moments, 'snp', 0, 0)  19.8 us
    pallas_call x22, Pallas kernels, call(): pl.pallas_call(kernel, out_shape=[make(shape, dtype) for shape, dtype in...  11.1 us
    unnamed x8, local copies, waits for them, and re-layouts  1.39 us
  transfers between devices with their start and end apart: 13, of which 1 were waited for; matrix products, arithmetic and copies ran while one was open for 0% of the time, Pallas kernels for 13%

profile of v9, /device:TPU:0, one launch (start us, length us, event | category | flops | bytes accessed | tf_op | source)
XLA Modules:
  0.0 65.5 jit_solution(13659152047372975512)
XLA Ops:
  0.6 0.8 %collective-permute-start.1 = (f32[64,1024]{1,0:T(8,128)}, f32[64,1024]{1,0:T(8,128)S(1)}, u32[]{:S(2)}, u32[]{:S(2)}) collective-permute-start(f32[64,1024]{1,0:T(8,128)} %start_ref.11), channel_id=1, source_target_pairs={{2,1},{4,3},{6,5},{8,7},{10,9},{12,11},{14,13},{18,17},{20,19},{22... | collective-permute-start | bytes 786440 | tf_op jit(solution)/shard_map/ppermute | solution.py:398
  1.5 0.1 shard_map.68
  1.5 0.0 copy-done.1
  1.6 1.3 %copy-done = f32[1024,1024]{1,0:T(8,128)S(1)} copy-done((f32[1024,1024]{1,0:T(8,128)S(1)}, f32[1024,1024]{1,0:T(8,128)}, u32[]{:S(2)}) %copy-start) | copy-done | bytes 4194328
  2.9 2.1 %shard_map.70 = (bf16[1024,1024]{1,0:T(8,128)(2,1)S(1)}, bf16[1024,1024]{1,0:T(8,128)(2,1)S(1)}, f32[64,1024]{1,0:T(8,128)S(1)}) custom-call(f32[1024,1024]{1,0:T(8,128)} %next_ref.3, f32[64,1024]{1,0:T(8,128)S(1)} %copy-done.1, bf16[1024,1024]{1,0:T(8,128)(2,1)S(1)} %get-tuple-element.38.high_n_in, ...), custom_call_target="tpu_custom_call", output_to_operand_aliasing={{0}: (2, {}), {1}: (3, {}), {2}: (4, {})} | custom-call | flops 402653184 | tf_op jit(solution)/shard_map/pallas_call | solution.py:369
  5.0 1.1 %collective-permute-start = (f32[64,1024]{1,0:T(8,128)S(1)}, f32[64,1024]{1,0:T(8,128)S(1)}, u32[]{:S(2)}, u32[]{:S(2)}) collective-permute-start(f32[64,1024]{1,0:T(8,128)S(1)} %get-tuple-element.42), channel_id=1, source_target_pairs={{0,1},{1,0},{2,3},{3,2},{4,5},{5,4},{6,7},{7,6},{8,9},{9,8},{10,11... | collective-permute-start | bytes 786440 | tf_op jit(solution)/shard_map/ppermute | solution.py:398
  6.2 0.7 %collective-permute-start.2 = (f32[64,1024]{1,0:T(8,128)S(1)}, f32[64,1024]{1,0:T(8,128)S(1)}, u32[]{:S(2)}, u32[]{:S(2)}) collective-permute-start(f32[64,1024]{1,0:T(8,128)S(1)} %get-tuple-element.40.after_ref), channel_id=1, source_target_pairs={{1,2},{3,4},{5,6},{7,8},{9,10},{11,12},{13,14},{17,18},{19,20},{21... | collective-permute-start | bytes 786440 | tf_op jit(solution)/shard_map/ppermute | solution.py:398
  6.9 0.0 collective-permute-done.1.got_ref
  6.9 0.4 collective-permute-done.got_pair_ref
  7.3 1.9 %shard_map.73 = (bf16[1024,1024]{1,0:T(8,128)(2,1)S(1)}, bf16[1024,1024]{1,0:T(8,128)(2,1)S(1)}, bf16[1024,1024]{1,0:T(8,128)(2,1)S(1)}, bf16[1024,1024]{1,0:T(8,128)(2,1)S(1)}, f32[64,1024]{1,0:T(8,128)S(1)}) custom-call(f32[1024,1024]{1,0:T(8,128)S(1)} %copy-done, ...), custom_call_target="tpu_custom_call", output_to_operand_aliasing={{0}: (7, {}), {1}: (8, {}), {2}: (9, {}), {3}: (10, {})} | custom-call | flops 402653184 | tf_op jit(solution)/shard_map/pallas_call | solution.py:369
  9.2 0.6 shard_map.74
  9.8 4.1 %collective-permute-start.3 = (f32[64,1024]{1,0:T(8,128)S(1)}, f32[64,1024]{1,0:T(8,128)S(1)}, u32[]{:S(2)}, u32[]{:S(2)}) collective-permute-start(f32[64,1024]{1,0:T(8,128)S(1)} %get-tuple-element.57), channel_id=1, source_target_pairs={{0,1},{1,0},{2,3},{3,2},{4,5},{5,4},{6,7},{7,6},{8,9},{9,8},{10,11... | collective-permute-start | bytes 786440 | tf_op jit(solution)/shard_map/ppermute | solution.py:398
  13.9 0.7 %collective-permute-start.4 = (f32[64,1024]{1,0:T(8,128)S(1)}, f32[64,1024]{1,0:T(8,128)S(1)}, u32[]{:S(2)}, u32[]{:S(2)}) collective-permute-start(f32[64,1024]{1,0:T(8,128)S(1)} %get-tuple-element.60), channel_id=1, source_target_pairs={{1,2},{3,4},{5,6},{7,8},{9,10},{11,12},{13,14},{17,18},{19,20},{21... | collective-permute-start | bytes 786440 | tf_op jit(solution)/shard_map/ppermute | solution.py:398
  14.6 0.7 %collective-permute-start.5 = (f32[64,1024]{1,0:T(8,128)S(1)}, f32[64,1024]{1,0:T(8,128)S(1)}, u32[]{:S(2)}, u32[]{:S(2)}) collective-permute-start(f32[64,1024]{1,0:T(8,128)S(1)} %get-tuple-element.53.field_ref.before_ref.zero_ref), channel_id=1, source_target_pairs={{2,1},{4,3},{6,5},{8,7},{10,9},{12,11},{14,13},{18,17},{20,19},{22... | collective-permute-start | bytes 786440 | tf_op jit(solution)/shard_map/ppermute | solution.py:398
  15.3 0.8 %shard_map.75 = (f32[64,1024]{1,0:T(8,128)S(1)}, f32[64,128]{1,0:T(8,128)S(1)}) custom-call(f32[64,1024]{1,0:T(8,128)S(1)} %get-tuple-element.53.field_ref.before_ref.zero_ref, bf16[1024,1024]{1,0:T(8,128)(2,1)S(1)} %get-tuple-element.54.high_ref, bf16[1024,1024]{1,0:T(8,128)(2,1)S(1)} %get-tuple-element.55.low_ref), custom_call_target="tpu_custom_call" | custom-call | flops 402653184 | tf_op jit(solution)/shard_map/pallas_call | solution.py:369
  16.1 0.6 shard_map.76.base_ref
  16.8 10.9 %collective-permute-start.6 = (f32[64,1024]{1,0:T(8,128)S(1)}, f32[64,1024]{1,0:T(8,128)S(1)}, u32[]{:S(2)}, u32[]{:S(2)}) collective-permute-start(f32[64,1024]{1,0:T(8,128)S(1)} %shard_map.79.field_ref.before_ref.one_ref), channel_id=1, source_target_pairs={{0,1},{1,0},{2,3},{3,2},{4,5},{5,4},{6,7},{7,6},{8,9},{9,8},{10,11... | collective-permute-start | bytes 786440 | tf_op jit(solution)/shard_map/ppermute | solution.py:398
  27.7 0.5 shard_map.83
  28.3 0.1 collective-permute-start.8
  28.3 0.7 %collective-permute-start.9 = (f32[64,1024]{1,0:T(8,128)S(1)}, f32[64,1024]{1,0:T(8,128)S(1)}, u32[]{:S(2)}, u32[]{:S(2)}) collective-permute-start(f32[64,1024]{1,0:T(8,128)S(1)} %shard_map.77.after_ref.even_ref.field_ref), channel_id=1, source_target_pairs={{2,1},{4,3},{6,5},{8,7},{10,9},{12,11},{14,13},{18,17},{20,19},{22... | collective-permute-start | bytes 786440 | tf_op jit(solution)/shard_map/ppermute | solution.py:398
  29.0 0.7 %collective-permute-start.7 = (f32[64,1024]{1,0:T(8,128)S(1)}, f32[64,1024]{1,0:T(8,128)S(1)}, u32[]{:S(2)}, u32[]{:S(2)}) collective-permute-start(f32[64,1024]{1,0:T(8,128)S(1)} %get-tuple-element.65), channel_id=1, source_target_pairs={{1,2},{3,4},{5,6},{7,8},{9,10},{11,12},{13,14},{17,18},{19,20},{21... | collective-permute-start | bytes 786440 | tf_op jit(solution)/shard_map/ppermute | solution.py:398
  29.7 0.8 %shard_map.80 = (f32[64,1024]{1,0:T(8,128)S(1)}, f32[64,128]{1,0:T(8,128)S(1)}) custom-call(f32[64,1024]{1,0:T(8,128)S(1)} %get-tuple-element.53.field_ref.before_ref.zero_ref, f32[64,1024]{1,0:T(8,128)S(1)} %shard_map.79.field_ref.before_ref.one_ref, bf16[1024,1024]{1,0:T(8,128)(2,1)S(1)} %get-tuple-element.54.high_ref, ...), custom_call_target="tpu_custom_call" | custom-call | flops 402653184 | tf_op jit(solution)/shard_map/pallas_call | solution.py:369
  30.6 0.6 shard_map.82.base_ref
  31.2 0.6 shard_map.85
  31.7 10.0 %collective-permute-start.10 = (f32[64,1024]{1,0:T(8,128)S(1)}, f32[64,1024]{1,0:T(8,128)S(1)}, u32[]{:S(2)}, u32[]{:S(2)}) collective-permute-start(f32[64,1024]{1,0:T(8,128)S(1)} %get-tuple-element.69), channel_id=1, source_target_pairs={{0,1},{1,0},{2,3},{3,2},{4,5},{5,4},{6,7},{7,6},{8,9},{9,8},{10,11... | collective-permute-start | bytes 786440 | tf_op jit(solution)/shard_map/ppermute | solution.py:398
  41.8 0.7 %collective-permute-start.11 = (f32[64,1024]{1,0:T(8,128)S(1)}, f32[64,1024]{1,0:T(8,128)S(1)}, u32[]{:S(2)}, u32[]{:S(2)}) collective-permute-start(f32[64,1024]{1,0:T(8,128)S(1)} %get-tuple-element.70), channel_id=1, source_target_pairs={{1,2},{3,4},{5,6},{7,8},{9,10},{11,12},{13,14},{17,18},{19,20},{21... | collective-permute-start | bytes 786440 | tf_op jit(solution)/shard_map/ppermute | solution.py:398
  42.4 0.7 %collective-permute-start.12 = (f32[64,1024]{1,0:T(8,128)S(1)}, f32[64,1024]{1,0:T(8,128)S(1)}, u32[]{:S(2)}, u32[]{:S(2)}) collective-permute-start(f32[64,1024]{1,0:T(8,128)S(1)} %get-tuple-element.67.field_ref.two_ref), channel_id=1, source_target_pairs={{2,1},{4,3},{6,5},{8,7},{10,9},{12,11},{14,13},{18,17},{20,19},{22... | collective-permute-start | bytes 786440 | tf_op jit(solution)/shard_map/ppermute | solution.py:398
  43.1 0.8 %shard_map.86 = (f32[64,1024]{1,0:T(8,128)S(1)}, f32[64,128]{1,0:T(8,128)S(1)}) custom-call(f32[64,1024]{1,0:T(8,128)S(1)} %shard_map.79.field_ref.before_ref.one_ref, f32[64,1024]{1,0:T(8,128)S(1)} %get-tuple-element.67.field_ref.two_ref, bf16[1024,1024]{1,0:T(8,128)(2,1)S(1)} %get-tuple-element.54.high_ref, bf16[1024,1024]{1,0:T(8,128)(2,1)S(1)} %get-tuple-element.55.low_ref), custom_call_target="tpu_custom_call" | custom-call | flops 402653184 | tf_op jit(solution)/shard_map/pallas_call | solution.py:369
  44.0 0.3 shard_map.87
  44.2 19.8 %all_to_all.5.table_ref = f32[16,8,128]{2,1,0:T(8,128)S(1)} all-to-all(f32[16,8,128]{2,1,0:T(8,128)S(1)} %shard_map.87), channel_id=1, replica_groups=mesh['parts'=2,'snp'=16] {'snp'}, dimensions={0} | all-to-all | bytes 131072 | tf_op jit(solution)/shard_map/all_to_all | solution.py:480
  64.0 0.2 shard_map.88.weights_ref
  64.2 1.3 %shard_map.89 = (f32[64,1024]{1,0:T(8,128)}, f32[64,1024]{1,0:T(8,128)}) custom-call(f32[64,128]{1,0:T(8,128)S(1)} %shard_map.88.weights_ref, f32[64,1024]{1,0:T(8,128)S(1)} %copy-done.1, f32[64,1024]{1,0:T(8,128)S(1)} %get-tuple-element.53.field_ref.before_ref.zero_ref, f32[64,1024]{1,0:T(8,128)S(1)} %shard_map.79.field_ref.before_ref.one_ref, ...), custom_call_target="tpu_custom_call" | custom-call | tf_op jit(solution)/shard_map/pallas_call | solution.py:369
  (25 shorter events, 0.2 us)
Async XLA Ops:
  0.6 1.0 %copy-start.1 = (f32[64,1024]{1,0:T(8,128)S(1)}, f32[64,1024]{1,0:T(8,128)}, u32[]{:S(2)}) copy-start(f32[64,1024]{1,0:T(8,128)} %start_ref.11) | copy-start | bytes 786436
  0.6 2.3 %copy-start = (f32[1024,1024]{1,0:T(8,128)S(1)}, f32[1024,1024]{1,0:T(8,128)}, u32[]{:S(2)}) copy-start(f32[1024,1024]{1,0:T(8,128)} %local_ref.3) | copy-start | bytes 12582916
  0.6 6.2 %collective-permute-start.1 = (f32[64,1024]{1,0:T(8,128)}, f32[64,1024]{1,0:T(8,128)S(1)}, u32[]{:S(2)}, u32[]{:S(2)}) collective-permute-start(f32[64,1024]{1,0:T(8,128)} %start_ref.11), channel_id=1, source_target_pairs={{2,1},{4,3},{6,5},{8,7},{10,9},{12,11},{14,13},{18,17},{20,19},{22... | collective-permute-start | bytes 786440 | tf_op jit(solution)/shard_map/ppermute | solution.py:398
  2.9 3.9 %copy-start.2 = (f32[64,1024]{1,0:T(8,128)S(1)}, f32[64,1024]{1,0:T(8,128)}, u32[]{:S(2)}) copy-start(f32[64,1024]{1,0:T(8,128)} %marginal_ref.3) | copy-start | bytes 786436
  2.9 3.9 %copy-start.3 = (f32[64,1]{0,1:T(1,128)S(1)}, f32[64,1]{0,1:T(1,128)}, u32[]{:S(2)}) copy-start(f32[64,1]{0,1:T(1,128)} %param.7) | copy-start | bytes 772
  5.0 2.3 %collective-permute-start = (f32[64,1024]{1,0:T(8,128)S(1)}, f32[64,1024]{1,0:T(8,128)S(1)}, u32[]{:S(2)}, u32[]{:S(2)}) collective-permute-start(f32[64,1024]{1,0:T(8,128)S(1)} %get-tuple-element.42), channel_id=1, source_target_pairs={{0,1},{1,0},{2,3},{3,2},{4,5},{5,4},{6,7},{7,6},{8,9},{9,8},{10,11... | collective-permute-start | bytes 786440 | tf_op jit(solution)/shard_map/ppermute | solution.py:398
  6.2 3.0 %collective-permute-start.2 = (f32[64,1024]{1,0:T(8,128)S(1)}, f32[64,1024]{1,0:T(8,128)S(1)}, u32[]{:S(2)}, u32[]{:S(2)}) collective-permute-start(f32[64,1024]{1,0:T(8,128)S(1)} %get-tuple-element.40.after_ref), channel_id=1, source_target_pairs={{1,2},{3,4},{5,6},{7,8},{9,10},{11,12},{13,14},{17,18},{19,20},{21... | collective-permute-start | bytes 786440 | tf_op jit(solution)/shard_map/ppermute | solution.py:398
  9.8 6.3 %collective-permute-start.3 = (f32[64,1024]{1,0:T(8,128)S(1)}, f32[64,1024]{1,0:T(8,128)S(1)}, u32[]{:S(2)}, u32[]{:S(2)}) collective-permute-start(f32[64,1024]{1,0:T(8,128)S(1)} %get-tuple-element.57), channel_id=1, source_target_pairs={{0,1},{1,0},{2,3},{3,2},{4,5},{5,4},{6,7},{7,6},{8,9},{9,8},{10,11... | collective-permute-start | bytes 786440 | tf_op jit(solution)/shard_map/ppermute | solution.py:398
  13.9 2.7 %collective-permute-start.4 = (f32[64,1024]{1,0:T(8,128)S(1)}, f32[64,1024]{1,0:T(8,128)S(1)}, u32[]{:S(2)}, u32[]{:S(2)}) collective-permute-start(f32[64,1024]{1,0:T(8,128)S(1)} %get-tuple-element.60), channel_id=1, source_target_pairs={{1,2},{3,4},{5,6},{7,8},{9,10},{11,12},{13,14},{17,18},{19,20},{21... | collective-permute-start | bytes 786440 | tf_op jit(solution)/shard_map/ppermute | solution.py:398
  14.6 2.1 %collective-permute-start.5 = (f32[64,1024]{1,0:T(8,128)S(1)}, f32[64,1024]{1,0:T(8,128)S(1)}, u32[]{:S(2)}, u32[]{:S(2)}) collective-permute-start(f32[64,1024]{1,0:T(8,128)S(1)} %get-tuple-element.53.field_ref.before_ref.zero_ref), channel_id=1, source_target_pairs={{2,1},{4,3},{6,5},{8,7},{10,9},{12,11},{14,13},{18,17},{20,19},{22... | collective-permute-start | bytes 786440 | tf_op jit(solution)/shard_map/ppermute | solution.py:398
  16.8 13.8 %collective-permute-start.6 = (f32[64,1024]{1,0:T(8,128)S(1)}, f32[64,1024]{1,0:T(8,128)S(1)}, u32[]{:S(2)}, u32[]{:S(2)}) collective-permute-start(f32[64,1024]{1,0:T(8,128)S(1)} %shard_map.79.field_ref.before_ref.one_ref), channel_id=1, source_target_pairs={{0,1},{1,0},{2,3},{3,2},{4,5},{5,4},{6,7},{7,6},{8,9},{9,8},{10,11... | collective-permute-start | bytes 786440 | tf_op jit(solution)/shard_map/ppermute | solution.py:398
  28.3 2.9 %collective-permute-start.8 = (f32[64,1024]{1,0:T(8,128)S(1)}, f32[64,1024]{1,0:T(8,128)S(1)}, u32[]{:S(2)}, u32[]{:S(2)}) collective-permute-start(f32[64,1024]{1,0:T(8,128)S(1)} %shard_map.83), channel_id=1, source_target_pairs={{0,1},{1,0},{2,3},{3,2},{4,5},{5,4},{6,7},{7,6},{8,9},{9,8},{10,11... | collective-permute-start | bytes 786440 | tf_op jit(solution)/shard_map/ppermute | solution.py:398
  28.3 2.8 %collective-permute-start.9 = (f32[64,1024]{1,0:T(8,128)S(1)}, f32[64,1024]{1,0:T(8,128)S(1)}, u32[]{:S(2)}, u32[]{:S(2)}) collective-permute-start(f32[64,1024]{1,0:T(8,128)S(1)} %shard_map.77.after_ref.even_ref.field_ref), channel_id=1, source_target_pairs={{2,1},{4,3},{6,5},{8,7},{10,9},{12,11},{14,13},{18,17},{20,19},{22... | collective-permute-start | bytes 786440 | tf_op jit(solution)/shard_map/ppermute | solution.py:398
  29.0 2.1 %collective-permute-start.7 = (f32[64,1024]{1,0:T(8,128)S(1)}, f32[64,1024]{1,0:T(8,128)S(1)}, u32[]{:S(2)}, u32[]{:S(2)}) collective-permute-start(f32[64,1024]{1,0:T(8,128)S(1)} %get-tuple-element.65), channel_id=1, source_target_pairs={{1,2},{3,4},{5,6},{7,8},{9,10},{11,12},{13,14},{17,18},{19,20},{21... | collective-permute-start | bytes 786440 | tf_op jit(solution)/shard_map/ppermute | solution.py:398
  31.7 12.2 %collective-permute-start.10 = (f32[64,1024]{1,0:T(8,128)S(1)}, f32[64,1024]{1,0:T(8,128)S(1)}, u32[]{:S(2)}, u32[]{:S(2)}) collective-permute-start(f32[64,1024]{1,0:T(8,128)S(1)} %get-tuple-element.69), channel_id=1, source_target_pairs={{0,1},{1,0},{2,3},{3,2},{4,5},{5,4},{6,7},{7,6},{8,9},{9,8},{10,11... | collective-permute-start | bytes 786440 | tf_op jit(solution)/shard_map/ppermute | solution.py:398
  41.8 2.2 %collective-permute-start.11 = (f32[64,1024]{1,0:T(8,128)S(1)}, f32[64,1024]{1,0:T(8,128)S(1)}, u32[]{:S(2)}, u32[]{:S(2)}) collective-permute-start(f32[64,1024]{1,0:T(8,128)S(1)} %get-tuple-element.70), channel_id=1, source_target_pairs={{1,2},{3,4},{5,6},{7,8},{9,10},{11,12},{13,14},{17,18},{19,20},{21... | collective-permute-start | bytes 786440 | tf_op jit(solution)/shard_map/ppermute | solution.py:398
  42.4 21.7 %collective-permute-start.12 = (f32[64,1024]{1,0:T(8,128)S(1)}, f32[64,1024]{1,0:T(8,128)S(1)}, u32[]{:S(2)}, u32[]{:S(2)}) collective-permute-start(f32[64,1024]{1,0:T(8,128)S(1)} %get-tuple-element.67.field_ref.two_ref), channel_id=1, source_target_pairs={{2,1},{4,3},{6,5},{8,7},{10,9},{12,11},{14,13},{18,17},{20,19},{22... | collective-permute-start | bytes 786440 | tf_op jit(solution)/shard_map/ppermute | solution.py:398

commit v10 on v9

--- a/solution.py
+++ b/solution.py
@@ -430,6 +430,7 @@
         aliases={7: 0, 8: 1, 9: 2, 10: 3}, flops=work,
     )
     join = functools.partial(join_kernel, -1.0)
+    got_early = shift(odd_field, on_chip)
     merged, pair = run(join, [field, field], base, up, odd_field, high_n, low_n, flops=work)
     up = next_up
     fields, tables = [merged], []
@@ -440,19 +441,22 @@
             down = shift(merged, downward)
         before = fields[-2:-1]
         kernel = own_kernel if before else functools.partial(own_kernel, None)
-        if step == 3:
+        if step < 4:
+            split = functools.partial
+            kernels = [split(own_part_kernel, odd_part, *(() if before else (None,))) for odd_part in (False, True)]
             inputs = (*before, merged, high_l, low_l)
-            own, part = run(functools.partial(own_part_kernel, False), [field, table], *inputs, flops=work)
+            own, part = run(kernels[0], [field, table], *inputs, flops=work)
             own, part = run(
-                functools.partial(own_part_kernel, True), [field, table], *inputs, own, part,
-                aliases={4: 0, 5: 1}, flops=work,
+                kernels[1], [field, table], *inputs, own, part,
+                aliases={len(inputs): 0, len(inputs) + 1: 1}, flops=work,
             )
         else:
             own, part = run(kernel, [field, table], *before, merged, high_l, low_l, flops=work)
         tables.append(part)
         if step > ITERS:
             break
-        (base,) = run(pair_kernel, [field], own, got_pair, high_up, low_up, flops=work)
+        there = got_early if step == 2 else got_pair
+        (base,) = run(pair_kernel, [field], own, there, high_up, low_up, flops=work)
         if step % 2 == 0:
             (even_field,) = run(even_kernel, [field], base, up, ridge, flops=work)
             next_down = shift(even_field, downward)

time: 65.8 us -> 62.9 us (0.956)
  starting transfers between devices: 31.8 us -> 28.8 us
    ppermute x13 -> x14, starting transfers between devices: 31.8 us -> 28.8 us  [shift(): return lax.ppermute(value, 'snp', route)]
    pallas_call x22 -> x23, Pallas kernels: 11.1 us -> 11.1 us  [call(): pl.pallas_call(kernel, out_shape=[make(shape, dtype) for shape, dtype in...]
  transfers between devices with their start and end apart: 13 -> 14, of which waited for: 1 -> 1; matrix products, arithmetic and copies ran while one was open for 0% -> 0% of each run, Pallas kernels for 13% -> 15%
where the time goes in v10:
time: 62.9 us; the launch traced here: 62.6 us
  starting transfers between devices  28.8 us (46%)
  blocking collectives  19.8 us (31%)
  Pallas kernels  11.1 us (18%)
  local copies, waits for them, and re-layouts  1.39 us (2%)
  between operations  0.97 us (2%)
    ppermute x14, starting transfers between devices, shift(): return lax.ppermute(value, 'snp', route)  28.8 us
    all_to_all x1, blocking collectives, on_device(): moments = lax.all_to_all(moments, 'snp', 0, 0)  19.8 us
    pallas_call x23, Pallas kernels, call(): pl.pallas_call(kernel, out_shape=[make(shape, dtype) for shape, dtype in...  11.1 us
    unnamed x8, local copies, waits for them, and re-layouts  1.39 us
  transfers between devices with their start and end apart: 14, of which 1 were waited for; matrix products, arithmetic and copies ran while one was open for 0% of the time, Pallas kernels for 15%

profile of v10, /device:TPU:0, one launch (start us, length us, event | category | flops | bytes accessed | tf_op | source)
XLA Modules:
  0.0 62.6 jit_solution(10824113504403713925)
XLA Ops:
  0.6 0.8 %collective-permute-start.1 = (f32[64,1024]{1,0:T(8,128)}, f32[64,1024]{1,0:T(8,128)S(1)}, u32[]{:S(2)}, u32[]{:S(2)}) collective-permute-start(f32[64,1024]{1,0:T(8,128)} %start_ref.11), channel_id=1, source_target_pairs={{2,1},{4,3},{6,5},{8,7},{10,9},{12,11},{14,13},{18,17},{20,19},{22... | collective-permute-start | bytes 786440 | tf_op jit(solution)/shard_map/ppermute | solution.py:398
  1.5 0.1 shard_map.68
  1.5 0.0 copy-done.1
  1.6 1.3 %copy-done = f32[1024,1024]{1,0:T(8,128)S(1)} copy-done((f32[1024,1024]{1,0:T(8,128)S(1)}, f32[1024,1024]{1,0:T(8,128)}, u32[]{:S(2)}) %copy-start) | copy-done | bytes 4194328
  2.9 2.1 %shard_map.70 = (bf16[1024,1024]{1,0:T(8,128)(2,1)S(1)}, bf16[1024,1024]{1,0:T(8,128)(2,1)S(1)}, f32[64,1024]{1,0:T(8,128)S(1)}) custom-call(f32[1024,1024]{1,0:T(8,128)} %next_ref.3, f32[64,1024]{1,0:T(8,128)S(1)} %copy-done.1, bf16[1024,1024]{1,0:T(8,128)(2,1)S(1)} %get-tuple-element.40.high_n_in, ...), custom_call_target="tpu_custom_call", output_to_operand_aliasing={{0}: (2, {}), {1}: (3, {}), {2}: (4, {})} | custom-call | flops 402653184 | tf_op jit(solution)/shard_map/pallas_call | solution.py:369
  5.0 1.1 %collective-permute-start = (f32[64,1024]{1,0:T(8,128)S(1)}, f32[64,1024]{1,0:T(8,128)S(1)}, u32[]{:S(2)}, u32[]{:S(2)}) collective-permute-start(f32[64,1024]{1,0:T(8,128)S(1)} %get-tuple-element.44), channel_id=1, source_target_pairs={{0,1},{1,0},{2,3},{3,2},{4,5},{5,4},{6,7},{7,6},{8,9},{9,8},{10,11... | collective-permute-start | bytes 786440 | tf_op jit(solution)/shard_map/ppermute | solution.py:398
  6.2 0.7 %collective-permute-start.2 = (f32[64,1024]{1,0:T(8,128)S(1)}, f32[64,1024]{1,0:T(8,128)S(1)}, u32[]{:S(2)}, u32[]{:S(2)}) collective-permute-start(f32[64,1024]{1,0:T(8,128)S(1)} %get-tuple-element.42.after_ref), channel_id=1, source_target_pairs={{1,2},{3,4},{5,6},{7,8},{9,10},{11,12},{13,14},{17,18},{19,20},{21... | collective-permute-start | bytes 786440 | tf_op jit(solution)/shard_map/ppermute | solution.py:398
  6.9 0.4 collective-permute-done.got_pair_ref
  7.3 0.7 %collective-permute-start.4 = (f32[64,1024]{1,0:T(8,128)S(1)}, f32[64,1024]{1,0:T(8,128)S(1)}, u32[]{:S(2)}, u32[]{:S(2)}) collective-permute-start(f32[64,1024]{1,0:T(8,128)S(1)} %get-tuple-element.63), channel_id=1, source_target_pairs={{1,2},{3,4},{5,6},{7,8},{9,10},{11,12},{13,14},{17,18},{19,20},{21... | collective-permute-start | bytes 786440 | tf_op jit(solution)/shard_map/ppermute | solution.py:398
  8.0 5.8 %collective-permute-start.3 = (f32[64,1024]{1,0:T(8,128)S(1)}, f32[64,1024]{1,0:T(8,128)S(1)}, u32[]{:S(2)}, u32[]{:S(2)}) collective-permute-start(f32[64,1024]{1,0:T(8,128)S(1)} %get-tuple-element.53.after_ref.odd_ref), channel_id=1, source_target_pairs={{0,1},{1,0},{2,3},{3,2},{4,5},{5,4},{6,7},{7,6},{8,9},{9,8},{10,11... | collective-permute-start | bytes 786440 | tf_op jit(solution)/shard_map/ppermute | solution.py:398
  13.8 1.9 %shard_map.73 = (bf16[1024,1024]{1,0:T(8,128)(2,1)S(1)}, bf16[1024,1024]{1,0:T(8,128)(2,1)S(1)}, bf16[1024,1024]{1,0:T(8,128)(2,1)S(1)}, bf16[1024,1024]{1,0:T(8,128)(2,1)S(1)}, f32[64,1024]{1,0:T(8,128)S(1)}) custom-call(f32[1024,1024]{1,0:T(8,128)S(1)} %copy-done, ...), custom_call_target="tpu_custom_call", output_to_operand_aliasing={{0}: (7, {}), {1}: (8, {}), {2}: (9, {}), {3}: (10, {})} | custom-call | flops 402653184 | tf_op jit(solution)/shard_map/pallas_call | solution.py:369
  15.7 0.6 shard_map.74
  16.3 0.1 collective-permute-start.5
  16.3 0.7 %collective-permute-start.6 = (f32[64,1024]{1,0:T(8,128)S(1)}, f32[64,1024]{1,0:T(8,128)S(1)}, u32[]{:S(2)}, u32[]{:S(2)}) collective-permute-start(f32[64,1024]{1,0:T(8,128)S(1)} %get-tuple-element.55.field_ref.before_ref.zero_ref), channel_id=1, source_target_pairs={{2,1},{4,3},{6,5},{8,7},{10,9},{12,11},{14,13},{18,17},{20,19},{22... | collective-permute-start | bytes 786440 | tf_op jit(solution)/shard_map/ppermute | solution.py:398
  17.0 0.8 %shard_map.75 = (f32[64,1024]{1,0:T(8,128)S(1)}, f32[64,128]{1,0:T(8,128)S(1)}) custom-call(f32[64,1024]{1,0:T(8,128)S(1)} %get-tuple-element.55.field_ref.before_ref.zero_ref, bf16[1024,1024]{1,0:T(8,128)(2,1)S(1)} %get-tuple-element.56.high_ref, bf16[1024,1024]{1,0:T(8,128)(2,1)S(1)} %get-tuple-element.57.low_ref), custom_call_target="tpu_custom_call" | custom-call | flops 402653184 | tf_op jit(solution)/shard_map/pallas_call | solution.py:369
  17.9 0.6 shard_map.77.base_ref
  18.6 7.1 %collective-permute-start.7 = (f32[64,1024]{1,0:T(8,128)S(1)}, f32[64,1024]{1,0:T(8,128)S(1)}, u32[]{:S(2)}, u32[]{:S(2)}) collective-permute-start(f32[64,1024]{1,0:T(8,128)S(1)} %shard_map.80.field_ref.before_ref.one_ref), channel_id=1, source_target_pairs={{0,1},{1,0},{2,3},{3,2},{4,5},{5,4},{6,7},{7,6},{8,9},{9,8},{10,11... | collective-permute-start | bytes 786440 | tf_op jit(solution)/shard_map/ppermute | solution.py:398
  25.7 0.5 shard_map.84
  26.2 0.1 collective-permute-start.9
  26.3 0.7 %collective-permute-start.10 = (f32[64,1024]{1,0:T(8,128)S(1)}, f32[64,1024]{1,0:T(8,128)S(1)}, u32[]{:S(2)}, u32[]{:S(2)}) collective-permute-start(f32[64,1024]{1,0:T(8,128)S(1)} %shard_map.78.after_ref.even_ref.field_ref), channel_id=1, source_target_pairs={{2,1},{4,3},{6,5},{8,7},{10,9},{12,11},{14,13},{18,17},{20,19},{22... | collective-permute-start | bytes 786440 | tf_op jit(solution)/shard_map/ppermute | solution.py:398
  27.0 0.7 %collective-permute-start.8 = (f32[64,1024]{1,0:T(8,128)S(1)}, f32[64,1024]{1,0:T(8,128)S(1)}, u32[]{:S(2)}, u32[]{:S(2)}) collective-permute-start(f32[64,1024]{1,0:T(8,128)S(1)} %get-tuple-element.69), channel_id=1, source_target_pairs={{1,2},{3,4},{5,6},{7,8},{9,10},{11,12},{13,14},{17,18},{19,20},{21... | collective-permute-start | bytes 786440 | tf_op jit(solution)/shard_map/ppermute | solution.py:398
  27.7 0.8 %shard_map.81 = (f32[64,1024]{1,0:T(8,128)S(1)}, f32[64,128]{1,0:T(8,128)S(1)}) custom-call(f32[64,1024]{1,0:T(8,128)S(1)} %get-tuple-element.55.field_ref.before_ref.zero_ref, f32[64,1024]{1,0:T(8,128)S(1)} %shard_map.80.field_ref.before_ref.one_ref, bf16[1024,1024]{1,0:T(8,128)(2,1)S(1)} %get-tuple-element.56.high_ref, ...), custom_call_target="tpu_custom_call" | custom-call | flops 402653184 | tf_op jit(solution)/shard_map/pallas_call | solution.py:369
  28.5 0.6 shard_map.83.base_ref
  29.1 0.6 shard_map.86
  29.7 9.1 %collective-permute-start.11 = (f32[64,1024]{1,0:T(8,128)S(1)}, f32[64,1024]{1,0:T(8,128)S(1)}, u32[]{:S(2)}, u32[]{:S(2)}) collective-permute-start(f32[64,1024]{1,0:T(8,128)S(1)} %get-tuple-element.73), channel_id=1, source_target_pairs={{0,1},{1,0},{2,3},{3,2},{4,5},{5,4},{6,7},{7,6},{8,9},{9,8},{10,11... | collective-permute-start | bytes 786440 | tf_op jit(solution)/shard_map/ppermute | solution.py:398
  38.8 0.7 %collective-permute-start.12 = (f32[64,1024]{1,0:T(8,128)S(1)}, f32[64,1024]{1,0:T(8,128)S(1)}, u32[]{:S(2)}, u32[]{:S(2)}) collective-permute-start(f32[64,1024]{1,0:T(8,128)S(1)} %get-tuple-element.74), channel_id=1, source_target_pairs={{1,2},{3,4},{5,6},{7,8},{9,10},{11,12},{13,14},{17,18},{19,20},{21... | collective-permute-start | bytes 786440 | tf_op jit(solution)/shard_map/ppermute | solution.py:398
  39.5 0.7 %collective-permute-start.13 = (f32[64,1024]{1,0:T(8,128)S(1)}, f32[64,1024]{1,0:T(8,128)S(1)}, u32[]{:S(2)}, u32[]{:S(2)}) collective-permute-start(f32[64,1024]{1,0:T(8,128)S(1)} %get-tuple-element.71.field_ref.two_ref), channel_id=1, source_target_pairs={{2,1},{4,3},{6,5},{8,7},{10,9},{12,11},{14,13},{18,17},{20,19},{22... | collective-permute-start | bytes 786440 | tf_op jit(solution)/shard_map/ppermute | solution.py:398
  40.2 0.8 %shard_map.87 = (f32[64,1024]{1,0:T(8,128)S(1)}, f32[64,128]{1,0:T(8,128)S(1)}) custom-call(f32[64,1024]{1,0:T(8,128)S(1)} %shard_map.80.field_ref.before_ref.one_ref, f32[64,1024]{1,0:T(8,128)S(1)} %get-tuple-element.71.field_ref.two_ref, bf16[1024,1024]{1,0:T(8,128)(2,1)S(1)} %get-tuple-element.56.high_ref, bf16[1024,1024]{1,0:T(8,128)(2,1)S(1)} %get-tuple-element.57.low_ref), custom_call_target="tpu_custom_call" | custom-call | flops 402653184 | tf_op jit(solution)/shard_map/pallas_call | solution.py:369
  41.0 0.3 shard_map.88
  41.3 19.8 %all_to_all.5.table_ref = f32[16,8,128]{2,1,0:T(8,128)S(1)} all-to-all(f32[16,8,128]{2,1,0:T(8,128)S(1)} %shard_map.88), channel_id=1, replica_groups=mesh['parts'=2,'snp'=16] {'snp'}, dimensions={0} | all-to-all | bytes 131072 | tf_op jit(solution)/shard_map/all_to_all | solution.py:484
  61.0 0.2 shard_map.89.weights_ref
  61.2 1.4 %shard_map.90 = (f32[64,1024]{1,0:T(8,128)}, f32[64,1024]{1,0:T(8,128)}) custom-call(f32[64,128]{1,0:T(8,128)S(1)} %shard_map.89.weights_ref, f32[64,1024]{1,0:T(8,128)S(1)} %copy-done.1, f32[64,1024]{1,0:T(8,128)S(1)} %get-tuple-element.55.field_ref.before_ref.zero_ref, f32[64,1024]{1,0:T(8,128)S(1)} %shard_map.80.field_ref.before_ref.one_ref, ...), custom_call_target="tpu_custom_call" | custom-call | tf_op jit(solution)/shard_map/pallas_call | solution.py:369
  (28 shorter events, 0.2 us)
Async XLA Ops:
  0.6 1.0 %copy-start.1 = (f32[64,1024]{1,0:T(8,128)S(1)}, f32[64,1024]{1,0:T(8,128)}, u32[]{:S(2)}) copy-start(f32[64,1024]{1,0:T(8,128)} %start_ref.11) | copy-start | bytes 786436
  0.6 2.3 %copy-start = (f32[1024,1024]{1,0:T(8,128)S(1)}, f32[1024,1024]{1,0:T(8,128)}, u32[]{:S(2)}) copy-start(f32[1024,1024]{1,0:T(8,128)} %local_ref.3) | copy-start | bytes 12582916
  0.6 6.2 %collective-permute-start.1 = (f32[64,1024]{1,0:T(8,128)}, f32[64,1024]{1,0:T(8,128)S(1)}, u32[]{:S(2)}, u32[]{:S(2)}) collective-permute-start(f32[64,1024]{1,0:T(8,128)} %start_ref.11), channel_id=1, source_target_pairs={{2,1},{4,3},{6,5},{8,7},{10,9},{12,11},{14,13},{18,17},{20,19},{22... | collective-permute-start | bytes 786440 | tf_op jit(solution)/shard_map/ppermute | solution.py:398
  2.9 3.9 %copy-start.2 = (f32[64,1024]{1,0:T(8,128)S(1)}, f32[64,1024]{1,0:T(8,128)}, u32[]{:S(2)}) copy-start(f32[64,1024]{1,0:T(8,128)} %marginal_ref.3) | copy-start | bytes 786436
  2.9 3.9 %copy-start.3 = (f32[64,1]{0,1:T(1,128)S(1)}, f32[64,1]{0,1:T(1,128)}, u32[]{:S(2)}) copy-start(f32[64,1]{0,1:T(1,128)} %param.7) | copy-start | bytes 772
  5.0 2.3 %collective-permute-start = (f32[64,1024]{1,0:T(8,128)S(1)}, f32[64,1024]{1,0:T(8,128)S(1)}, u32[]{:S(2)}, u32[]{:S(2)}) collective-permute-start(f32[64,1024]{1,0:T(8,128)S(1)} %get-tuple-element.44), channel_id=1, source_target_pairs={{0,1},{1,0},{2,3},{3,2},{4,5},{5,4},{6,7},{7,6},{8,9},{9,8},{10,11... | collective-permute-start | bytes 786440 | tf_op jit(solution)/shard_map/ppermute | solution.py:398
  6.2 9.5 %collective-permute-start.2 = (f32[64,1024]{1,0:T(8,128)S(1)}, f32[64,1024]{1,0:T(8,128)S(1)}, u32[]{:S(2)}, u32[]{:S(2)}) collective-permute-start(f32[64,1024]{1,0:T(8,128)S(1)} %get-tuple-element.42.after_ref), channel_id=1, source_target_pairs={{1,2},{3,4},{5,6},{7,8},{9,10},{11,12},{13,14},{17,18},{19,20},{21... | collective-permute-start | bytes 786440 | tf_op jit(solution)/shard_map/ppermute | solution.py:398
  7.3 11.1 %collective-permute-start.4 = (f32[64,1024]{1,0:T(8,128)S(1)}, f32[64,1024]{1,0:T(8,128)S(1)}, u32[]{:S(2)}, u32[]{:S(2)}) collective-permute-start(f32[64,1024]{1,0:T(8,128)S(1)} %get-tuple-element.63), channel_id=1, source_target_pairs={{1,2},{3,4},{5,6},{7,8},{9,10},{11,12},{13,14},{17,18},{19,20},{21... | collective-permute-start | bytes 786440 | tf_op jit(solution)/shard_map/ppermute | solution.py:398
  8.0 9.9 %collective-permute-start.3 = (f32[64,1024]{1,0:T(8,128)S(1)}, f32[64,1024]{1,0:T(8,128)S(1)}, u32[]{:S(2)}, u32[]{:S(2)}) collective-permute-start(f32[64,1024]{1,0:T(8,128)S(1)} %get-tuple-element.53.after_ref.odd_ref), channel_id=1, source_target_pairs={{0,1},{1,0},{2,3},{3,2},{4,5},{5,4},{6,7},{7,6},{8,9},{9,8},{10,11... | collective-permute-start | bytes 786440 | tf_op jit(solution)/shard_map/ppermute | solution.py:398
  16.3 2.2 %collective-permute-start.5 = (f32[64,1024]{1,0:T(8,128)S(1)}, f32[64,1024]{1,0:T(8,128)S(1)}, u32[]{:S(2)}, u32[]{:S(2)}) collective-permute-start(f32[64,1024]{1,0:T(8,128)S(1)} %get-tuple-element.64), channel_id=1, source_target_pairs={{0,1},{1,0},{2,3},{3,2},{4,5},{5,4},{6,7},{7,6},{8,9},{9,8},{10,11... | collective-permute-start | bytes 786440 | tf_op jit(solution)/shard_map/ppermute | solution.py:398
  16.3 2.1 %collective-permute-start.6 = (f32[64,1024]{1,0:T(8,128)S(1)}, f32[64,1024]{1,0:T(8,128)S(1)}, u32[]{:S(2)}, u32[]{:S(2)}) collective-permute-start(f32[64,1024]{1,0:T(8,128)S(1)} %get-tuple-element.55.field_ref.before_ref.zero_ref), channel_id=1, source_target_pairs={{2,1},{4,3},{6,5},{8,7},{10,9},{12,11},{14,13},{18,17},{20,19},{22... | collective-permute-start | bytes 786440 | tf_op jit(solution)/shard_map/ppermute | solution.py:398
  18.6 10.0 %collective-permute-start.7 = (f32[64,1024]{1,0:T(8,128)S(1)}, f32[64,1024]{1,0:T(8,128)S(1)}, u32[]{:S(2)}, u32[]{:S(2)}) collective-permute-start(f32[64,1024]{1,0:T(8,128)S(1)} %shard_map.80.field_ref.before_ref.one_ref), channel_id=1, source_target_pairs={{0,1},{1,0},{2,3},{3,2},{4,5},{5,4},{6,7},{7,6},{8,9},{9,8},{10,11... | collective-permute-start | bytes 786440 | tf_op jit(solution)/shard_map/ppermute | solution.py:398
  26.2 2.9 %collective-permute-start.9 = (f32[64,1024]{1,0:T(8,128)S(1)}, f32[64,1024]{1,0:T(8,128)S(1)}, u32[]{:S(2)}, u32[]{:S(2)}) collective-permute-start(f32[64,1024]{1,0:T(8,128)S(1)} %shard_map.84), channel_id=1, source_target_pairs={{0,1},{1,0},{2,3},{3,2},{4,5},{5,4},{6,7},{7,6},{8,9},{9,8},{10,11... | collective-permute-start | bytes 786440 | tf_op jit(solution)/shard_map/ppermute | solution.py:398
  26.3 2.8 %collective-permute-start.10 = (f32[64,1024]{1,0:T(8,128)S(1)}, f32[64,1024]{1,0:T(8,128)S(1)}, u32[]{:S(2)}, u32[]{:S(2)}) collective-permute-start(f32[64,1024]{1,0:T(8,128)S(1)} %shard_map.78.after_ref.even_ref.field_ref), channel_id=1, source_target_pairs={{2,1},{4,3},{6,5},{8,7},{10,9},{12,11},{14,13},{18,17},{20,19},{22... | collective-permute-start | bytes 786440 | tf_op jit(solution)/shard_map/ppermute | solution.py:398
  27.0 2.1 %collective-permute-start.8 = (f32[64,1024]{1,0:T(8,128)S(1)}, f32[64,1024]{1,0:T(8,128)S(1)}, u32[]{:S(2)}, u32[]{:S(2)}) collective-permute-start(f32[64,1024]{1,0:T(8,128)S(1)} %get-tuple-element.69), channel_id=1, source_target_pairs={{1,2},{3,4},{5,6},{7,8},{9,10},{11,12},{13,14},{17,18},{19,20},{21... | collective-permute-start | bytes 786440 | tf_op jit(solution)/shard_map/ppermute | solution.py:398
  29.7 11.3 %collective-permute-start.11 = (f32[64,1024]{1,0:T(8,128)S(1)}, f32[64,1024]{1,0:T(8,128)S(1)}, u32[]{:S(2)}, u32[]{:S(2)}) collective-permute-start(f32[64,1024]{1,0:T(8,128)S(1)} %get-tuple-element.73), channel_id=1, source_target_pairs={{0,1},{1,0},{2,3},{3,2},{4,5},{5,4},{6,7},{7,6},{8,9},{9,8},{10,11... | collective-permute-start | bytes 786440 | tf_op jit(solution)/shard_map/ppermute | solution.py:398
  38.8 2.2 %collective-permute-start.12 = (f32[64,1024]{1,0:T(8,128)S(1)}, f32[64,1024]{1,0:T(8,128)S(1)}, u32[]{:S(2)}, u32[]{:S(2)}) collective-permute-start(f32[64,1024]{1,0:T(8,128)S(1)} %get-tuple-element.74), channel_id=1, source_target_pairs={{1,2},{3,4},{5,6},{7,8},{9,10},{11,12},{13,14},{17,18},{19,20},{21... | collective-permute-start | bytes 786440 | tf_op jit(solution)/shard_map/ppermute | solution.py:398
  39.5 21.7 %collective-permute-start.13 = (f32[64,1024]{1,0:T(8,128)S(1)}, f32[64,1024]{1,0:T(8,128)S(1)}, u32[]{:S(2)}, u32[]{:S(2)}) collective-permute-start(f32[64,1024]{1,0:T(8,128)S(1)} %get-tuple-element.71.field_ref.two_ref), channel_id=1, source_target_pairs={{2,1},{4,3},{6,5},{8,7},{10,9},{12,11},{14,13},{18,17},{20,19},{22... | collective-permute-start | bytes 786440 | tf_op jit(solution)/shard_map/ppermute | solution.py:398

commit v11 on v9

--- a/solution.py
+++ b/solution.py
@@ -340,22 +340,28 @@
 
 def final_kernel(
     weights_ref, start_ref, zero_ref, one_ref, two_ref, own_ref, got_pair_ref, got_down_ref, got_up_ref,
-    high_up, low_up, solution_ref, residual_ref,
+    high_up, low_up, solution_ref, residual_ref, solution, residual, sems,
 ):
     tile = tile_of(own_ref.shape[1])
     weights = [weights_ref[:, i : i + 1] for i in range(2 * ITERS + 1)]
-    gain, residual = weights[:ITERS], weights[ITERS:]
+    gain, rest = weights[:ITERS], weights[ITERS:]
     odd = is_odd()
+    zero, one, two = zero_ref[...], one_ref[...], two_ref[...]
+    solution[...] = start_ref[...] + gain[0] * zero + gain[1] * one + gain[2] * two
+    first = pltpu.make_async_copy(solution, solution_ref, sems.at[0])
+    first.start()
     upper = jnp.where(odd, got_down_ref[...], got_pair_ref[...])
     lower = jnp.where(odd, got_pair_ref[...], got_up_ref[...])
-    zero, one, two = zero_ref[...], one_ref[...], two_ref[...]
-    solution_ref[...] = start_ref[...] + gain[0] * zero + gain[1] * one + gain[2] * two
-    base = residual[0] * zero + residual[1] * one + residual[2] * two + residual[3] * (own_ref[...] + lower)
+    base = rest[0] * zero + rest[1] * one + rest[2] * two + rest[3] * (own_ref[...] + lower)
 
     def store(start, part):
-        residual_ref[:, pl.ds(start, tile)] = base[:, start : start + tile] + residual[3] * part
+        residual[:, pl.ds(start, tile)] = base[:, start : start + tile] + rest[3] * part
 
     forward(stacked(upper), high_up, low_up, store)
+    second = pltpu.make_async_copy(residual, residual_ref, sems.at[1])
+    second.start()
+    first.wait()
+    second.wait()
 
 
 def call(kernel, out, *args, spaces=None, scratch=(), limit=12, aliases=None, keep=True, flops=0):
@@ -370,7 +376,7 @@
         kernel,
         out_shape=[make(shape, dtype) for shape, dtype in out],
         in_specs=[pl.BlockSpec(memory_space=place) for place in places],
-        out_specs=[pl.BlockSpec(memory_space=VMEM) for _ in out],
+        out_specs=[pl.BlockSpec(memory_space=VMEM if keep else pltpu.HBM) for _ in out],
         scratch_shapes=scratch,
         input_output_aliases=aliases or {},
         cost_estimate=pl.CostEstimate(flops=flops, bytes_accessed=0, transcendentals=0) if flops else None,
@@ -484,6 +490,7 @@
             final_kernel, [field, field],
             weights, warm_start, *fields, own, got_pair, down, up, high_up, low_up,
             keep=False,
+            scratch=(pltpu.VMEM((traits, size), F32), pltpu.VMEM((traits, size), F32), pltpu.SemaphoreType.DMA((2,))),
         )
     )
 

time: 65.8 us -> 65.8 us (level)
  no operation moved by 1% of the time
where the time goes in v11:
time: 65.8 us; the launch traced here: 65.5 us
  starting transfers between devices  31.8 us (48%)
  blocking collectives  19.8 us (30%)
  Pallas kernels  11.1 us (17%)
  local copies, waits for them, and re-layouts  1.39 us (2%)
  between operations  0.94 us (1%)
    ppermute x13, starting transfers between devices, shift(): return lax.ppermute(value, 'snp', route)  31.8 us
    all_to_all x1, blocking collectives, on_device(): moments = lax.all_to_all(moments, 'snp', 0, 0)  19.8 us
    pallas_call x22, Pallas kernels, call(): pl.pallas_call(kernel, out_shape=[make(shape, dtype) for shape, dtype in...  11.1 us
    unnamed x8, local copies, waits for them, and re-layouts  1.39 us
  transfers between devices with their start and end apart: 13, of which 1 were waited for; matrix products, arithmetic and copies ran while one was open for 0% of the time, Pallas kernels for 13%

profile of v11, /device:TPU:0, one launch (start us, length us, event | category | flops | bytes accessed | tf_op | source)
XLA Modules:
  0.0 65.5 jit_solution(11219961711394677913)
XLA Ops:
  0.6 0.8 %collective-permute-start.1 = (f32[64,1024]{1,0:T(8,128)}, f32[64,1024]{1,0:T(8,128)S(1)}, u32[]{:S(2)}, u32[]{:S(2)}) collective-permute-start(f32[64,1024]{1,0:T(8,128)} %start_ref.11), channel_id=1, source_target_pairs={{2,1},{4,3},{6,5},{8,7},{10,9},{12,11},{14,13},{18,17},{20,19},{22... | collective-permute-start | bytes 786440 | tf_op jit(solution)/shard_map/ppermute | solution.py:404
  1.5 0.1 shard_map.68
  1.5 0.0 copy-done.1
  1.6 1.3 %copy-done = f32[1024,1024]{1,0:T(8,128)S(1)} copy-done((f32[1024,1024]{1,0:T(8,128)S(1)}, f32[1024,1024]{1,0:T(8,128)}, u32[]{:S(2)}) %copy-start) | copy-done | bytes 4194328
  2.9 2.1 %shard_map.70 = (bf16[1024,1024]{1,0:T(8,128)(2,1)S(1)}, bf16[1024,1024]{1,0:T(8,128)(2,1)S(1)}, f32[64,1024]{1,0:T(8,128)S(1)}) custom-call(f32[1024,1024]{1,0:T(8,128)} %next_ref.3, f32[64,1024]{1,0:T(8,128)S(1)} %copy-done.1, bf16[1024,1024]{1,0:T(8,128)(2,1)S(1)} %get-tuple-element.38.high_n_in, ...), custom_call_target="tpu_custom_call", output_to_operand_aliasing={{0}: (2, {}), {1}: (3, {}), {2}: (4, {})} | custom-call | flops 402653184 | tf_op jit(solution)/shard_map/pallas_call | solution.py:375
  5.0 1.1 %collective-permute-start = (f32[64,1024]{1,0:T(8,128)S(1)}, f32[64,1024]{1,0:T(8,128)S(1)}, u32[]{:S(2)}, u32[]{:S(2)}) collective-permute-start(f32[64,1024]{1,0:T(8,128)S(1)} %get-tuple-element.42), channel_id=1, source_target_pairs={{0,1},{1,0},{2,3},{3,2},{4,5},{5,4},{6,7},{7,6},{8,9},{9,8},{10,11... | collective-permute-start | bytes 786440 | tf_op jit(solution)/shard_map/ppermute | solution.py:404
  6.2 0.7 %collective-permute-start.2 = (f32[64,1024]{1,0:T(8,128)S(1)}, f32[64,1024]{1,0:T(8,128)S(1)}, u32[]{:S(2)}, u32[]{:S(2)}) collective-permute-start(f32[64,1024]{1,0:T(8,128)S(1)} %get-tuple-element.40.after_ref), channel_id=1, source_target_pairs={{1,2},{3,4},{5,6},{7,8},{9,10},{11,12},{13,14},{17,18},{19,20},{21... | collective-permute-start | bytes 786440 | tf_op jit(solution)/shard_map/ppermute | solution.py:404
  6.9 0.0 collective-permute-done.1.got_ref
  6.9 0.4 collective-permute-done.got_pair_ref
  7.3 1.9 %shard_map.73 = (bf16[1024,1024]{1,0:T(8,128)(2,1)S(1)}, bf16[1024,1024]{1,0:T(8,128)(2,1)S(1)}, bf16[1024,1024]{1,0:T(8,128)(2,1)S(1)}, bf16[1024,1024]{1,0:T(8,128)(2,1)S(1)}, f32[64,1024]{1,0:T(8,128)S(1)}) custom-call(f32[1024,1024]{1,0:T(8,128)S(1)} %copy-done, ...), custom_call_target="tpu_custom_call", output_to_operand_aliasing={{0}: (7, {}), {1}: (8, {}), {2}: (9, {}), {3}: (10, {})} | custom-call | flops 402653184 | tf_op jit(solution)/shard_map/pallas_call | solution.py:375
  9.2 0.6 shard_map.74
  9.8 4.1 %collective-permute-start.3 = (f32[64,1024]{1,0:T(8,128)S(1)}, f32[64,1024]{1,0:T(8,128)S(1)}, u32[]{:S(2)}, u32[]{:S(2)}) collective-permute-start(f32[64,1024]{1,0:T(8,128)S(1)} %get-tuple-element.57), channel_id=1, source_target_pairs={{0,1},{1,0},{2,3},{3,2},{4,5},{5,4},{6,7},{7,6},{8,9},{9,8},{10,11... | collective-permute-start | bytes 786440 | tf_op jit(solution)/shard_map/ppermute | solution.py:404
  13.9 0.7 %collective-permute-start.4 = (f32[64,1024]{1,0:T(8,128)S(1)}, f32[64,1024]{1,0:T(8,128)S(1)}, u32[]{:S(2)}, u32[]{:S(2)}) collective-permute-start(f32[64,1024]{1,0:T(8,128)S(1)} %get-tuple-element.60), channel_id=1, source_target_pairs={{1,2},{3,4},{5,6},{7,8},{9,10},{11,12},{13,14},{17,18},{19,20},{21... | collective-permute-start | bytes 786440 | tf_op jit(solution)/shard_map/ppermute | solution.py:404
  14.6 0.7 %collective-permute-start.5 = (f32[64,1024]{1,0:T(8,128)S(1)}, f32[64,1024]{1,0:T(8,128)S(1)}, u32[]{:S(2)}, u32[]{:S(2)}) collective-permute-start(f32[64,1024]{1,0:T(8,128)S(1)} %get-tuple-element.53.field_ref.before_ref.zero_ref), channel_id=1, source_target_pairs={{2,1},{4,3},{6,5},{8,7},{10,9},{12,11},{14,13},{18,17},{20,19},{22... | collective-permute-start | bytes 786440 | tf_op jit(solution)/shard_map/ppermute | solution.py:404
  15.3 0.8 %shard_map.75 = (f32[64,1024]{1,0:T(8,128)S(1)}, f32[64,128]{1,0:T(8,128)S(1)}) custom-call(f32[64,1024]{1,0:T(8,128)S(1)} %get-tuple-element.53.field_ref.before_ref.zero_ref, bf16[1024,1024]{1,0:T(8,128)(2,1)S(1)} %get-tuple-element.54.high_ref, bf16[1024,1024]{1,0:T(8,128)(2,1)S(1)} %get-tuple-element.55.low_ref), custom_call_target="tpu_custom_call" | custom-call | flops 402653184 | tf_op jit(solution)/shard_map/pallas_call | solution.py:375
  16.1 0.6 shard_map.76.base_ref
  16.8 10.9 %collective-permute-start.6 = (f32[64,1024]{1,0:T(8,128)S(1)}, f32[64,1024]{1,0:T(8,128)S(1)}, u32[]{:S(2)}, u32[]{:S(2)}) collective-permute-start(f32[64,1024]{1,0:T(8,128)S(1)} %shard_map.79.field_ref.before_ref.one_ref), channel_id=1, source_target_pairs={{0,1},{1,0},{2,3},{3,2},{4,5},{5,4},{6,7},{7,6},{8,9},{9,8},{10,11... | collective-permute-start | bytes 786440 | tf_op jit(solution)/shard_map/ppermute | solution.py:404
  27.7 0.5 shard_map.83
  28.3 0.1 collective-permute-start.8
  28.3 0.7 %collective-permute-start.9 = (f32[64,1024]{1,0:T(8,128)S(1)}, f32[64,1024]{1,0:T(8,128)S(1)}, u32[]{:S(2)}, u32[]{:S(2)}) collective-permute-start(f32[64,1024]{1,0:T(8,128)S(1)} %shard_map.77.after_ref.even_ref.field_ref), channel_id=1, source_target_pairs={{2,1},{4,3},{6,5},{8,7},{10,9},{12,11},{14,13},{18,17},{20,19},{22... | collective-permute-start | bytes 786440 | tf_op jit(solution)/shard_map/ppermute | solution.py:404
  29.0 0.7 %collective-permute-start.7 = (f32[64,1024]{1,0:T(8,128)S(1)}, f32[64,1024]{1,0:T(8,128)S(1)}, u32[]{:S(2)}, u32[]{:S(2)}) collective-permute-start(f32[64,1024]{1,0:T(8,128)S(1)} %get-tuple-element.65), channel_id=1, source_target_pairs={{1,2},{3,4},{5,6},{7,8},{9,10},{11,12},{13,14},{17,18},{19,20},{21... | collective-permute-start | bytes 786440 | tf_op jit(solution)/shard_map/ppermute | solution.py:404
  29.7 0.8 %shard_map.80 = (f32[64,1024]{1,0:T(8,128)S(1)}, f32[64,128]{1,0:T(8,128)S(1)}) custom-call(f32[64,1024]{1,0:T(8,128)S(1)} %get-tuple-element.53.field_ref.before_ref.zero_ref, f32[64,1024]{1,0:T(8,128)S(1)} %shard_map.79.field_ref.before_ref.one_ref, bf16[1024,1024]{1,0:T(8,128)(2,1)S(1)} %get-tuple-element.54.high_ref, ...), custom_call_target="tpu_custom_call" | custom-call | flops 402653184 | tf_op jit(solution)/shard_map/pallas_call | solution.py:375
  30.6 0.6 shard_map.82.base_ref
  31.2 0.6 shard_map.85
  31.7 10.0 %collective-permute-start.10 = (f32[64,1024]{1,0:T(8,128)S(1)}, f32[64,1024]{1,0:T(8,128)S(1)}, u32[]{:S(2)}, u32[]{:S(2)}) collective-permute-start(f32[64,1024]{1,0:T(8,128)S(1)} %get-tuple-element.69), channel_id=1, source_target_pairs={{0,1},{1,0},{2,3},{3,2},{4,5},{5,4},{6,7},{7,6},{8,9},{9,8},{10,11... | collective-permute-start | bytes 786440 | tf_op jit(solution)/shard_map/ppermute | solution.py:404
  41.8 0.7 %collective-permute-start.11 = (f32[64,1024]{1,0:T(8,128)S(1)}, f32[64,1024]{1,0:T(8,128)S(1)}, u32[]{:S(2)}, u32[]{:S(2)}) collective-permute-start(f32[64,1024]{1,0:T(8,128)S(1)} %get-tuple-element.70), channel_id=1, source_target_pairs={{1,2},{3,4},{5,6},{7,8},{9,10},{11,12},{13,14},{17,18},{19,20},{21... | collective-permute-start | bytes 786440 | tf_op jit(solution)/shard_map/ppermute | solution.py:404
  42.4 0.7 %collective-permute-start.12 = (f32[64,1024]{1,0:T(8,128)S(1)}, f32[64,1024]{1,0:T(8,128)S(1)}, u32[]{:S(2)}, u32[]{:S(2)}) collective-permute-start(f32[64,1024]{1,0:T(8,128)S(1)} %get-tuple-element.67.field_ref.two_ref), channel_id=1, source_target_pairs={{2,1},{4,3},{6,5},{8,7},{10,9},{12,11},{14,13},{18,17},{20,19},{22... | collective-permute-start | bytes 786440 | tf_op jit(solution)/shard_map/ppermute | solution.py:404
  43.1 0.8 %shard_map.86 = (f32[64,1024]{1,0:T(8,128)S(1)}, f32[64,128]{1,0:T(8,128)S(1)}) custom-call(f32[64,1024]{1,0:T(8,128)S(1)} %shard_map.79.field_ref.before_ref.one_ref, f32[64,1024]{1,0:T(8,128)S(1)} %get-tuple-element.67.field_ref.two_ref, bf16[1024,1024]{1,0:T(8,128)(2,1)S(1)} %get-tuple-element.54.high_ref, bf16[1024,1024]{1,0:T(8,128)(2,1)S(1)} %get-tuple-element.55.low_ref), custom_call_target="tpu_custom_call" | custom-call | flops 402653184 | tf_op jit(solution)/shard_map/pallas_call | solution.py:375
  44.0 0.3 shard_map.87
  44.2 19.8 %all_to_all.5.table_ref = f32[16,8,128]{2,1,0:T(8,128)S(1)} all-to-all(f32[16,8,128]{2,1,0:T(8,128)S(1)} %shard_map.87), channel_id=1, replica_groups=mesh['parts'=2,'snp'=16] {'snp'}, dimensions={0} | all-to-all | bytes 131072 | tf_op jit(solution)/shard_map/all_to_all | solution.py:486
  64.0 0.2 shard_map.88.weights_ref
  64.2 1.4 %shard_map.89 = (f32[64,1024]{1,0:T(8,128)}, f32[64,1024]{1,0:T(8,128)}) custom-call(f32[64,128]{1,0:T(8,128)S(1)} %shard_map.88.weights_ref, f32[64,1024]{1,0:T(8,128)S(1)} %copy-done.1, f32[64,1024]{1,0:T(8,128)S(1)} %get-tuple-element.53.field_ref.before_ref.zero_ref, f32[64,1024]{1,0:T(8,128)S(1)} %shard_map.79.field_ref.before_ref.one_ref, ...), custom_call_target="tpu_custom_call" | custom-call | tf_op jit(solution)/shard_map/pallas_call | solution.py:375
  (25 shorter events, 0.2 us)
Async XLA Ops:
  0.6 1.0 %copy-start.1 = (f32[64,1024]{1,0:T(8,128)S(1)}, f32[64,1024]{1,0:T(8,128)}, u32[]{:S(2)}) copy-start(f32[64,1024]{1,0:T(8,128)} %start_ref.11) | copy-start | bytes 786436
  0.6 2.3 %copy-start = (f32[1024,1024]{1,0:T(8,128)S(1)}, f32[1024,1024]{1,0:T(8,128)}, u32[]{:S(2)}) copy-start(f32[1024,1024]{1,0:T(8,128)} %local_ref.3) | copy-start | bytes 12582916
  0.6 6.2 %collective-permute-start.1 = (f32[64,1024]{1,0:T(8,128)}, f32[64,1024]{1,0:T(8,128)S(1)}, u32[]{:S(2)}, u32[]{:S(2)}) collective-permute-start(f32[64,1024]{1,0:T(8,128)} %start_ref.11), channel_id=1, source_target_pairs={{2,1},{4,3},{6,5},{8,7},{10,9},{12,11},{14,13},{18,17},{20,19},{22... | collective-permute-start | bytes 786440 | tf_op jit(solution)/shard_map/ppermute | solution.py:404
  2.9 3.9 %copy-start.2 = (f32[64,1024]{1,0:T(8,128)S(1)}, f32[64,1024]{1,0:T(8,128)}, u32[]{:S(2)}) copy-start(f32[64,1024]{1,0:T(8,128)} %marginal_ref.3) | copy-start | bytes 786436
  2.9 3.9 %copy-start.3 = (f32[64,1]{0,1:T(1,128)S(1)}, f32[64,1]{0,1:T(1,128)}, u32[]{:S(2)}) copy-start(f32[64,1]{0,1:T(1,128)} %param.7) | copy-start | bytes 772
  5.0 2.3 %collective-permute-start = (f32[64,1024]{1,0:T(8,128)S(1)}, f32[64,1024]{1,0:T(8,128)S(1)}, u32[]{:S(2)}, u32[]{:S(2)}) collective-permute-start(f32[64,1024]{1,0:T(8,128)S(1)} %get-tuple-element.42), channel_id=1, source_target_pairs={{0,1},{1,0},{2,3},{3,2},{4,5},{5,4},{6,7},{7,6},{8,9},{9,8},{10,11... | collective-permute-start | bytes 786440 | tf_op jit(solution)/shard_map/ppermute | solution.py:404
  6.2 3.0 %collective-permute-start.2 = (f32[64,1024]{1,0:T(8,128)S(1)}, f32[64,1024]{1,0:T(8,128)S(1)}, u32[]{:S(2)}, u32[]{:S(2)}) collective-permute-start(f32[64,1024]{1,0:T(8,128)S(1)} %get-tuple-element.40.after_ref), channel_id=1, source_target_pairs={{1,2},{3,4},{5,6},{7,8},{9,10},{11,12},{13,14},{17,18},{19,20},{21... | collective-permute-start | bytes 786440 | tf_op jit(solution)/shard_map/ppermute | solution.py:404
  9.8 6.3 %collective-permute-start.3 = (f32[64,1024]{1,0:T(8,128)S(1)}, f32[64,1024]{1,0:T(8,128)S(1)}, u32[]{:S(2)}, u32[]{:S(2)}) collective-permute-start(f32[64,1024]{1,0:T(8,128)S(1)} %get-tuple-element.57), channel_id=1, source_target_pairs={{0,1},{1,0},{2,3},{3,2},{4,5},{5,4},{6,7},{7,6},{8,9},{9,8},{10,11... | collective-permute-start | bytes 786440 | tf_op jit(solution)/shard_map/ppermute | solution.py:404
  13.9 2.7 %collective-permute-start.4 = (f32[64,1024]{1,0:T(8,128)S(1)}, f32[64,1024]{1,0:T(8,128)S(1)}, u32[]{:S(2)}, u32[]{:S(2)}) collective-permute-start(f32[64,1024]{1,0:T(8,128)S(1)} %get-tuple-element.60), channel_id=1, source_target_pairs={{1,2},{3,4},{5,6},{7,8},{9,10},{11,12},{13,14},{17,18},{19,20},{21... | collective-permute-start | bytes 786440 | tf_op jit(solution)/shard_map/ppermute | solution.py:404
  14.6 2.1 %collective-permute-start.5 = (f32[64,1024]{1,0:T(8,128)S(1)}, f32[64,1024]{1,0:T(8,128)S(1)}, u32[]{:S(2)}, u32[]{:S(2)}) collective-permute-start(f32[64,1024]{1,0:T(8,128)S(1)} %get-tuple-element.53.field_ref.before_ref.zero_ref), channel_id=1, source_target_pairs={{2,1},{4,3},{6,5},{8,7},{10,9},{12,11},{14,13},{18,17},{20,19},{22... | collective-permute-start | bytes 786440 | tf_op jit(solution)/shard_map/ppermute | solution.py:404
  16.8 13.8 %collective-permute-start.6 = (f32[64,1024]{1,0:T(8,128)S(1)}, f32[64,1024]{1,0:T(8,128)S(1)}, u32[]{:S(2)}, u32[]{:S(2)}) collective-permute-start(f32[64,1024]{1,0:T(8,128)S(1)} %shard_map.79.field_ref.before_ref.one_ref), channel_id=1, source_target_pairs={{0,1},{1,0},{2,3},{3,2},{4,5},{5,4},{6,7},{7,6},{8,9},{9,8},{10,11... | collective-permute-start | bytes 786440 | tf_op jit(solution)/shard_map/ppermute | solution.py:404
  28.3 2.9 %collective-permute-start.8 = (f32[64,1024]{1,0:T(8,128)S(1)}, f32[64,1024]{1,0:T(8,128)S(1)}, u32[]{:S(2)}, u32[]{:S(2)}) collective-permute-start(f32[64,1024]{1,0:T(8,128)S(1)} %shard_map.83), channel_id=1, source_target_pairs={{0,1},{1,0},{2,3},{3,2},{4,5},{5,4},{6,7},{7,6},{8,9},{9,8},{10,11... | collective-permute-start | bytes 786440 | tf_op jit(solution)/shard_map/ppermute | solution.py:404
  28.3 2.8 %collective-permute-start.9 = (f32[64,1024]{1,0:T(8,128)S(1)}, f32[64,1024]{1,0:T(8,128)S(1)}, u32[]{:S(2)}, u32[]{:S(2)}) collective-permute-start(f32[64,1024]{1,0:T(8,128)S(1)} %shard_map.77.after_ref.even_ref.field_ref), channel_id=1, source_target_pairs={{2,1},{4,3},{6,5},{8,7},{10,9},{12,11},{14,13},{18,17},{20,19},{22... | collective-permute-start | bytes 786440 | tf_op jit(solution)/shard_map/ppermute | solution.py:404
  29.0 2.1 %collective-permute-start.7 = (f32[64,1024]{1,0:T(8,128)S(1)}, f32[64,1024]{1,0:T(8,128)S(1)}, u32[]{:S(2)}, u32[]{:S(2)}) collective-permute-start(f32[64,1024]{1,0:T(8,128)S(1)} %get-tuple-element.65), channel_id=1, source_target_pairs={{1,2},{3,4},{5,6},{7,8},{9,10},{11,12},{13,14},{17,18},{19,20},{21... | collective-permute-start | bytes 786440 | tf_op jit(solution)/shard_map/ppermute | solution.py:404
  31.7 12.2 %collective-permute-start.10 = (f32[64,1024]{1,0:T(8,128)S(1)}, f32[64,1024]{1,0:T(8,128)S(1)}, u32[]{:S(2)}, u32[]{:S(2)}) collective-permute-start(f32[64,1024]{1,0:T(8,128)S(1)} %get-tuple-element.69), channel_id=1, source_target_pairs={{0,1},{1,0},{2,3},{3,2},{4,5},{5,4},{6,7},{7,6},{8,9},{9,8},{10,11... | collective-permute-start | bytes 786440 | tf_op jit(solution)/shard_map/ppermute | solution.py:404
  41.8 2.2 %collective-permute-start.11 = (f32[64,1024]{1,0:T(8,128)S(1)}, f32[64,1024]{1,0:T(8,128)S(1)}, u32[]{:S(2)}, u32[]{:S(2)}) collective-permute-start(f32[64,1024]{1,0:T(8,128)S(1)} %get-tuple-element.70), channel_id=1, source_target_pairs={{1,2},{3,4},{5,6},{7,8},{9,10},{11,12},{13,14},{17,18},{19,20},{21... | collective-permute-start | bytes 786440 | tf_op jit(solution)/shard_map/ppermute | solution.py:404
  42.4 21.7 %collective-permute-start.12 = (f32[64,1024]{1,0:T(8,128)S(1)}, f32[64,1024]{1,0:T(8,128)S(1)}, u32[]{:S(2)}, u32[]{:S(2)}) collective-permute-start(f32[64,1024]{1,0:T(8,128)S(1)} %get-tuple-element.67.field_ref.two_ref), channel_id=1, source_target_pairs={{2,1},{4,3},{6,5},{8,7},{10,9},{12,11},{14,13},{18,17},{20,19},{22... | collective-permute-start | bytes 786440 | tf_op jit(solution)/shard_map/ppermute | solution.py:404
